TPU v7x, 256 devices: a whole 4x4x8 slice. The times are simulated.
256 devices in a mesh: section: 8 (over y_hi, x), sta: 32 (over z, y_lo, core).
Axes of the slice: x: 4, y: 4 (y_hi: 2, y_lo: 2; y = y_hi * 2 + y_lo), z: 8, core: 2. Of those that a mesh axis runs over, the one named last changes fastest.
Arguments:
- waveforms: bfloat16 [8, 256, 8, 4096], P('section', 'sta'), may hold values from -6 to 6
- segment_mask: int32 [8, 256, 8], P('section', 'sta'), may hold values 0 or 1
- pair_blocks: int32 [32, 4], P('sta'), may hold values from 0 to 31, as said below
- window_decay: float32 [8], P('section'), may hold values from 0.5 to 1
Outputs:
- stacked: bfloat16 [8, 256, 32, 384], P('section', 'sta')
Inputs may be any that keep to these rules, and one draw needn't show every extreme that they name: `pair_blocks`: entry k of row b names a block of 8 stations other than b; entries of a row may repeat.
All inputs are finite; a program needn't handle non-finite values. No bound on the sum of `segment_mask` on one device may be relied on, other than what follows from the above.
Results may differ from a plain program's by a relative error of at most 0.008.
Values may be sent and summed in bfloat16 or wider, within the bound.
No kernel may reach another device: no remote copies, remote signals or barrier semaphores. Data moves between devices by JAX's collectives and lax.ppermute only.
A program may use at most 64 MiB of HBM per device.

v0:
```python
import functools
import math

import jax
import jax.numpy as jnp
import numpy as np
from jax import lax
from jax.experimental import pallas as pl
from jax.experimental.pallas import tpu as pltpu
from jax.sharding import PartitionSpec as P


NF = 1024
LAGS = 384
NSAMP = 4096
LS = 8
SEGS = 8
PB = 4
EPSILON = 1e-05
CHUNKS = (5, 3)


def twiddles():
    k = np.arange(32)[:, None]
    b = np.arange(128)[None, :]
    angle = 2.0 * np.pi * (k * b) / NSAMP
    return np.stack([np.cos(angle), np.sin(angle)]).astype(np.float32)


def second_dft():
    b = np.arange(128)[:, None]
    m = np.arange(4, 36)[None, :]
    angle = 2.0 * np.pi * ((b * m) % 128) / 128
    cos, sin = np.cos(angle) / 64, np.sin(angle) / 64
    full = np.zeros((256, 256))
    full[:128, :32] = cos
    full[128:, :32] = sin
    full[:128, 128:160] = -sin
    full[128:, 128:160] = cos
    high = full.astype(jnp.bfloat16)
    low = (full - high.astype(np.float64)).astype(jnp.bfloat16)
    return np.stack([high, low])


def lag_table():
    freq = 128 + np.arange(NF)
    shift = np.arange(LAGS) + NSAMP - LAGS // 2
    phase = (freq[:, None] * shift[None, :] % NSAMP).astype(np.float32)
    phase = phase * np.float32(2.0 * np.pi / NSAMP)
    cos = np.cos(phase) / np.float32(math.sqrt(NF))
    sin = -np.sin(phase) / np.float32(math.sqrt(NF))
    lane = np.arange(128)
    rows = []
    for c in range(8):
        f = 8 * (lane // 32) + c + 32 * (lane % 32)
        rows += [cos[f], sin[f]]
    return np.concatenate(rows).reshape(8, 256, LAGS).astype(jnp.bfloat16)


def add(a, b):
    return b if a is None else a if b is None else a + b


def sub(a, b):
    if b is None:
        return a
    return -b if a is None else a - b


def real_fft(xs):
    n = len(xs)
    if n == 1:
        return [(xs[0], None)]
    if n == 2:
        return [(xs[0] + xs[1], None), (xs[0] - xs[1], None)]
    even, odd = real_fft(xs[0::2]), real_fft(xs[1::2])
    out = [None] * (n // 2 + 1)
    for k in range(n // 4 + 1):
        (er, ei), (orr, oi) = even[k], odd[k]
        if k == 0:
            tr, ti = orr, oi
        elif 4 * k == n:
            tr, ti = oi, None if orr is None else -orr
        else:
            c, s = math.cos(2 * math.pi * k / n), math.sin(2 * math.pi * k / n)
            if oi is None:
                tr, ti = orr * c, orr * (-s)
            else:
                tr, ti = orr * c + oi * s, oi * c - orr * s
        out[k] = (add(er, tr), add(ei, ti))
        out[n // 2 - k] = (sub(er, tr), sub(ti, ei))
    return out


def spots():
    here = lax.axis_index("sta")
    return here % 4, here // 4, lax.axis_index("section")


def spectrum_kernel(mask_ref, wave_ref, turn_ref, dft_ref, *refs):
    outs, (mid, bins, white, marks) = refs[:-4], refs[-4:]

    def station(i, carry):
        xs = [wave_ref[i, :, 128 * a : 128 * (a + 1)].astype(jnp.float32) for a in range(32)]
        half = real_fft(xs)
        for k in range(32):
            re, im = half[k] if k <= 16 else half[32 - k]
            if k > 16 and im is not None:
                im = -im
            if k:
                cos, sin = turn_ref[0, k : k + 1, :], turn_ref[1, k : k + 1, :]
                if im is None:
                    re, im = re * cos, -(re * sin)
                else:
                    re, im = re * cos + im * sin, im * cos - re * sin
            klo, c = divmod(k, 8)
            rows = pl.ds(pl.multiple_of(c * 64 + i * 8, 8), 8)
            mid[klo, rows, :128] = re
            mid[klo, rows, 128:] = jnp.zeros_like(re) if im is None else im
        seg = lax.broadcasted_iota(jnp.int32, (SEGS, 128), 0)
        mark = jnp.zeros((SEGS, 128), jnp.float32)
        for e in range(SEGS):
            mark = jnp.where(seg == e, mask_ref[0, i, e].astype(jnp.float32), mark)
        marks[pl.ds(pl.multiple_of(i * 8, 8), 8), :] = mark
        return carry

    lax.fori_loop(0, LS, station, 0)
    dot = functools.partial(jnp.dot, preferred_element_type=jnp.float32)
    bins[...] = jnp.zeros_like(bins)

    def second(klo, carry):
        weights = []
        for part in range(2):
            base = dft_ref[part].astype(jnp.float32)
            sides = [pltpu.roll(base[:, at : at + 128], 32 * klo, 1) for at in (0, 128)]
            weights.append(jnp.concatenate(sides, axis=1).astype(jnp.bfloat16))
        wh, wl = weights
        value = mid[klo]
        high = value.astype(jnp.bfloat16)
        low = (value - high.astype(jnp.float32)).astype(jnp.bfloat16)
        bins[...] += dot(high, wh) + (dot(low, wh) + dot(high, wl))
        return carry

    lax.fori_loop(0, 4, second, 0)
    re, im = bins[:, :128], bins[:, 128:]
    amp = jnp.sqrt(re * re + im * im)
    amps = [amp[64 * c : 64 * (c + 1)] for c in range(8)]
    before, after = [amps[0]], [amps[7]]
    for c in range(1, 8):
        before.append(before[-1] + amps[c])
        after.append(after[-1] + amps[7 - c])
    after = after[::-1]
    total = before[7]
    lane = lax.broadcasted_iota(jnp.int32, (64, 128), 1)
    klo = lane // 32
    m = lane % 32
    turned = [pltpu.roll(total, 32 * d, 1) for d in (1, 2, 3)]
    zero = jnp.zeros_like(total)
    all_klo = total + turned[0] + turned[1] + turned[2]
    lower = upper = zero
    for d in (1, 2, 3):
        lower = lower + jnp.where(klo >= d, turned[d - 1], zero)
        upper = upper + jnp.where(klo + d <= 3, turned[3 - d], zero)
    for c in range(8):
        left = pltpu.roll(after[c] + upper, 1, 1)
        right = pltpu.roll(before[c] + lower, 127, 1)
        smooth = all_klo + jnp.where(m >= 1, left, zero) + jnp.where(m <= 30, right, zero)
        scale = marks[...] / (smooth * (1.0 / 65) + EPSILON)
        rows = slice(64 * c, 64 * (c + 1))
        white[0, rows, :] = re[rows] * scale
        white[1, rows, :] = im[rows] * scale
    place = spots()[0]
    count = len(CHUNKS)
    for r in range(4):
        for e in range(2):
            seg = 2 * (place ^ r) + e
            c = 0
            for h in range(count):
                out = outs[r * count + h]
                for local in range(CHUNKS[h]):
                    at = pl.ds(64 * c + seg, 8, stride=8)
                    tile = jnp.concatenate([white[0, at, :], white[1, at, :]], axis=0)
                    out[2 * local + e] = tile.astype(jnp.bfloat16)
                    c += 1
        seg = 2 * (place ^ r)
        tile = [marks[pl.ds(seg + e, 8, stride=8), :] for e in range(2)]
        outs[r * count][2 * CHUNKS[0]] = jnp.concatenate(tile, axis=0).astype(jnp.bfloat16)


def tiles_of(h):
    return 2 * CHUNKS[h] + (h == 0)


def spectrum(waves, mask):
    shapes = [
        jax.ShapeDtypeStruct((tiles_of(h), 16, 128), jnp.bfloat16)
        for _ in range(4)
        for h in range(len(CHUNKS))
    ]
    vmem = pl.BlockSpec(memory_space=pltpu.VMEM)
    return pl.pallas_call(
        spectrum_kernel,
        out_shape=shapes,
        in_specs=[pl.BlockSpec(memory_space=pltpu.SMEM)] + [vmem] * 3,
        out_specs=[vmem] * len(shapes),
        scratch_shapes=[
            pltpu.VMEM((4, 512, 256), jnp.float32),
            pltpu.VMEM((512, 256), jnp.float32),
            pltpu.VMEM((2, 512, 128), jnp.float32),
            pltpu.VMEM((64, 128), jnp.float32),
        ],
        name="spectrum",
    )(mask, waves, jnp.asarray(twiddles()), jnp.asarray(second_dft()))


def select_kernel(*refs):
    pairs, planes, outs, held = refs[:4], refs[4:12], refs[12:16], refs[16]
    for dz in range(8):
        held[dz] = planes[dz][...]
    mate, z, _ = spots()
    for r in range(4):
        for k in range(PB):
            p = pairs[r][0, k]
            dz = ((p // 4) - z + 8) % 8
            outs[r][k] = held[dz, (p % 4) ^ mate]


def select(pairs, planes):
    tiles = planes[0].shape[1]
    smem, vmem = pl.BlockSpec(memory_space=pltpu.SMEM), pl.BlockSpec(memory_space=pltpu.VMEM)
    return pl.pallas_call(
        select_kernel,
        out_shape=[jax.ShapeDtypeStruct((PB, tiles, 16, 128), jnp.bfloat16)] * 4,
        in_specs=[smem] * 4 + [vmem] * 8,
        out_specs=[vmem] * 4,
        scratch_shapes=[pltpu.VMEM((8, 4, tiles, 16, 128), jnp.bfloat16)],
        name="select",
    )(*pairs, *planes)


def cross_of(own, theirs, i):
    real, imag = None, None
    for (orr, oi), (pr, pi) in zip(own(i), theirs):
        real = add(real, orr * pr)
        real = add(real, oi * pi)
        imag = add(imag, orr * pi)
        imag = sub(imag, oi * pr)
    return real, imag


def correlate_kernel(h, decay_ref, *refs):
    chunk, last = CHUNKS[h], h == len(CHUNKS) - 1
    refs = list(refs)
    take = lambda n: [refs.pop(0) for _ in range(n)]
    mine, theirs = take(4), take(4)
    (table_ref,) = take(1)
    (carry_ref, inverse_in) = take(2) if h else (None, None)
    outs = take(4) if last else take(2)
    own, cross, inverse, total = take(4)
    for r in range(4):
        own[r] = mine[r][...].astype(jnp.float32)

    def rows_of(tile, e_rows):
        def at(i):
            found = []
            for r in range(4):
                for e in e_rows:
                    re = own[r, tile + e, pl.ds(i, 1), :]
                    im = own[r, tile + e, pl.ds(8 + i, 1), :]
                    found.append((jnp.broadcast_to(re, (8, 128)), jnp.broadcast_to(im, (8, 128))))
            return found

        return at

    def partners(tile, k, e_rows):
        found = []
        for r in range(4):
            for e in e_rows:
                both = theirs[r][k, tile + e].astype(jnp.float32)
                found.append((both[:8], both[8:]))
        return found

    if h:
        inverse[...] = inverse_in[...]
    else:
        for k in range(PB):
            there = partners(2 * chunk, k, (0,))
            for i in range(LS):
                count = sum(
                    a * c + b * d for (a, b), (c, d) in zip(rows_of(2 * chunk, (0,))(i), there)
                )
                at = i * 32 + k * 8
                inverse[at : at + 8, :] = 1.0 / jnp.maximum(count, 1.0)

    def per_slot(step, carry):
        c, k = step // PB, step % PB
        there = partners(2 * c, k, (0, 1))
        for i in range(LS):
            real, imag = cross_of(rows_of(2 * c, (0, 1)), there, i)
            at = pl.ds(pl.multiple_of(i * 32 + k * 8, 8), 8)
            part = inverse[at, :]
            cross[c, at, :128] = real * part
            cross[c, at, 128:] = imag * part
        return carry

    lax.fori_loop(0, chunk * PB, per_slot, 0)
    total[...] = carry_ref[...] if h else jnp.zeros_like(total)

    def per_row(c, carry):
        spectra = cross[c].astype(jnp.bfloat16)
        total[...] += jnp.dot(spectra, table_ref[c], preferred_element_type=jnp.float32)
        return carry

    lax.fori_loop(0, chunk, per_row, 0)
    if not last:
        outs[0][...] = total[...]
        outs[1][...] = inverse[...]
        return
    x = spots()[2] % 4
    decay = jnp.full((8, 128), decay_ref[0], jnp.float32)
    high = decay.astype(jnp.bfloat16)
    low = (decay - high.astype(jnp.float32)).astype(jnp.bfloat16)
    for r in range(4):
        at = pl.ds(pl.multiple_of((x ^ r) * 64, 64), 64)
        outs[r][:64, :] = total[at, :].astype(jnp.bfloat16)
        outs[r][64:72, :] = jnp.concatenate([high, low, jnp.zeros_like(low)], axis=1)


def correlate(h, decay, mine, theirs, table, carried):
    last = h == len(CHUNKS) - 1
    smem, vmem = pl.BlockSpec(memory_space=pltpu.SMEM), pl.BlockSpec(memory_space=pltpu.VMEM)
    if last:
        shapes = [jax.ShapeDtypeStruct((72, LAGS), jnp.bfloat16)] * 4
    else:
        shapes = [
            jax.ShapeDtypeStruct((256, LAGS), jnp.float32),
            jax.ShapeDtypeStruct((256, 128), jnp.float32),
        ]
    args = [*mine, *theirs, table, *carried]
    return pl.pallas_call(
        functools.partial(correlate_kernel, h),
        out_shape=shapes,
        in_specs=[smem] + [vmem] * len(args),
        out_specs=[vmem] * len(shapes),
        scratch_shapes=[
            pltpu.VMEM((4, tiles_of(h), 16, 128), jnp.float32),
            pltpu.VMEM((CHUNKS[h], 256, 256), jnp.float32),
            pltpu.VMEM((256, 128), jnp.float32),
            pltpu.VMEM((256, LAGS), jnp.float32),
        ],
    )(decay, *args)


def scan_kernel(rescan, *refs):
    ins, outs, (held, done) = refs[:4], refs[4:-2], refs[-2:]
    for r in range(4):
        held[r] = ins[r][...].astype(jnp.float32)
    x = spots()[2] % 4
    if rescan:
        state, outs = outs[0][...].astype(jnp.float32), outs[1:]
    else:
        state = jnp.zeros((64, LAGS), jnp.float32)
    for w in range(4):
        slot = x ^ w
        decay = held[slot, 64:65, :128] + held[slot, 64:65, 128:256]
        decay = jnp.concatenate([decay] * 3, axis=1)
        state = decay * state + held[slot, :64, :]
        if rescan:
            done[slot] = state
    if not rescan:
        outs[0][...] = state.astype(jnp.bfloat16)
        return
    for r in range(4):
        outs[r][...] = done[r].astype(jnp.bfloat16)


def scan_windows(ins, entering):
    vmem = pl.BlockSpec(memory_space=pltpu.VMEM)
    count = 4 if entering else 1
    return pl.pallas_call(
        functools.partial(scan_kernel, bool(entering)),
        out_shape=[jax.ShapeDtypeStruct((64, LAGS), jnp.bfloat16)] * count,
        in_specs=[vmem] * (4 + len(entering)),
        out_specs=[vmem] * count,
        scratch_shapes=[
            pltpu.VMEM((4, 72, LAGS), jnp.float32),
            pltpu.VMEM((4, 64, LAGS), jnp.float32),
        ],
        name="rescan" if entering else "scan",
    )(*ins, *entering)


def gather_kernel(*refs):
    ins, out = refs[:4], refs[4]
    x = spots()[2] % 4
    for r in range(4):
        out[x ^ r] = ins[r][...]


def gather_stations(ins):
    vmem = pl.BlockSpec(memory_space=pltpu.VMEM)
    return pl.pallas_call(
        gather_kernel,
        out_shape=jax.ShapeDtypeStruct((4, 64, LAGS), jnp.bfloat16),
        in_specs=[vmem] * 4,
        out_specs=vmem,
        name="gather",
    )(*ins)


def across(value, axis, size, r):
    return lax.ppermute(value, axis, [(d, d ^ r) for d in range(size)])


def along(value, step):
    return lax.ppermute(value, "sta", [(d, (d + 4 * step) % 32) for d in range(32)])


def body(waveforms, segment_mask, pair_blocks, window_decay):
    pairs = [pair_blocks] + [across(pair_blocks, "sta", 32, r) for r in (1, 2, 3)]
    count = len(CHUNKS)
    flat = spectrum(waveforms[0], segment_mask)
    table = lag_table()
    carried, start = [], 0
    for h in range(count):
        mine = [flat[r * count + h] for r in range(4)]
        plane = [mine[0]] + [across(mine[r], "sta", 32, r) for r in (1, 2, 3)]
        plane = jnp.stack(plane)
        planes = [plane] + [None] * 7
        ahead = back = plane
        for step in range(1, 5):
            if step < 4 or h % 2 == 0:
                ahead = along(ahead, 1)
                planes[8 - step] = ahead
            if step < 4 or h % 2 == 1:
                back = along(back, -1)
                planes[step] = back
        chosen = select(pairs, planes)
        theirs = [across(chosen[r], "sta", 32, r) for r in (1, 2, 3)]
        part = jnp.asarray(table[start : start + CHUNKS[h]])
        carried = correlate(h, window_decay, mine, [chosen[0], *theirs], part, carried)
        start += CHUNKS[h]
    ins = [carried[0]] + [across(carried[r], "section", 8, r) for r in (1, 2, 3)]
    (total,) = scan_windows(ins, [])
    entering = lax.ppermute(total, "section", [(d, d + 4) for d in range(4)])
    outs = scan_windows(ins, [entering])
    outs = [outs[0]] + [across(outs[r], "section", 8, r) for r in (1, 2, 3)]
    return gather_stations(outs).reshape(1, LS, 32, LAGS)


def solution(mesh):
    placed = (
        P("section", "sta", None, None),
        P("section", "sta", None),
        P("sta", None),
        P("section"),
    )

    return jax.shard_map(
        body, mesh=mesh, in_specs=placed, out_specs=P("section", "sta", None, None), check_vma=False
    )
```

profile of v0, /device:TPU:6, one launch (start us, length us, event | category | flops | bytes accessed | tf_op | source)
XLA Modules:
  0.0 116.3 jit_solution(6402954927655836850)
XLA Ops:
  0.0 4.8 %spectrum.1 = (bf16[11,16,128]{2,1,0:T(8,128)(2,1)}, bf16[6,16,128]{2,1,0:T(8,128)(2,1)}, bf16[11,16,128]{2,1,0:T(8,128)(2,1)}, bf16[6,16,128]{2,1,0:T(8,128)(2,...) custom-call(s32[1,8,8]{2,1,0:T(8,128)} %mask_ref.1, ...), custom_call_target="tpu_custom_call" | custom-call | tf_op jit(solution)/shard_map/spectrum/pallas_call | solution.py:201
  4.9 1.7 %collective-permute-start.17 = (bf16[11,16,128]{2,1,0:T(8,128)(2,1)}, bf16[11,16,128]{2,1,0:T(8,128)(2,1)S(1)}, u32[]{:S(2)}, u32[]{:S(2)}) collective-permute-start(bf16[11,16,128]{2,1,0:T(8,128)(2,1)} %get-tuple-element.41.refs_2_), channel_id=1, source_target_pairs={{0,2},{1,3},{2,0},{3,1},{4,6},{5,7},{6,4},{7,5},{8,10},{9,11},{10,... | collective-permute-start | bytes 135176 | tf_op jit(solution)/shard_map/ppermute | solution.py:412
  6.5 0.2 collective-permute-start.18
  6.7 2.5 %collective-permute-done.17 = bf16[11,16,128]{2,1,0:T(8,128)(2,1)S(1)} collective-permute-done((bf16[11,16,128]{2,1,0:T(8,128)(2,1)}, bf16[11,16,128]{2,1,0:T(8,128)(2,1)S(1)}, u32[]{:S(2)}, u32[]{:S(2)}) %collective-permute-start.17) | collective-permute-done | bytes 45088 | tf_op jit(solution)/shard_map/ppermute | solution.py:412
  9.2 1.2 %collective-permute-done.18 = bf16[11,16,128]{2,1,0:T(8,128)(2,1)S(1)} collective-permute-done((bf16[11,16,128]{2,1,0:T(8,128)(2,1)}, bf16[11,16,128]{2,1,0:T(8,128)(2,1)S(1)}, u32[]{:S(2)}, u32[]{:S(2)}) %collective-permute-start.18) | collective-permute-done | bytes 45088 | tf_op jit(solution)/shard_map/ppermute | solution.py:412
  10.4 0.8 pad_maximum_fusion.refs_4_
  11.3 2.0 %collective-permute-start.22 = (bf16[4,11,16,128]{3,2,1,0:T(8,128)(2,1)S(1)}, bf16[4,11,16,128]{3,2,1,0:T(8,128)(2,1)S(1)}, u32[]{:S(2)}, u32[]{:S(2)}) collective-permute-start(bf16[4,11,16,128]{3,2,1,0:T(8,128)(2,1)S(1)} %pad_maximum_fusion.refs_4_), channel_id=1, source_target_pairs={{0,4},{1,5},{2,6},{3,7},{4,8},{5,9},{6,10},{7,11},{8,12},{9,13},{1... | collective-permute-start | bytes 540680 | tf_op jit(solution)/shard_map/ppermute | solution.py:416
  13.3 4.0 %collective-permute-start.19 = (bf16[4,11,16,128]{3,2,1,0:T(8,128)(2,1)S(1)}, bf16[4,11,16,128]{3,2,1,0:T(8,128)(2,1)S(1)}, u32[]{:S(2)}, u32[]{:S(2)}) collective-permute-start(bf16[4,11,16,128]{3,2,1,0:T(8,128)(2,1)S(1)} %pad_maximum_fusion.refs_4_), channel_id=1, source_target_pairs={{0,28},{1,29},{2,30},{3,31},{4,0},{5,1},{6,2},{7,3},{8,4},{9,5},{1... | collective-permute-start | bytes 540680 | tf_op jit(solution)/shard_map/ppermute | solution.py:416
  17.3 4.8 %collective-permute-done.22.refs_11_ = bf16[4,11,16,128]{3,2,1,0:T(8,128)(2,1)S(1)} collective-permute-done((bf16[4,11,16,128]{3,2,1,0:T(8,128)(2,1)S(1)}, bf16[4,11,16,128]{3,2,1,0:T(8,128)(2,1)S(1)}, u32[]{:S(2)}, u32[]{:S(2)}) %collective-permute-start.22) | collective-permute-done | bytes 180256 | tf_op jit(solution)/shard_map/ppermute | solution.py:416
  22.1 3.2 %collective-permute-start.20 = (bf16[4,11,16,128]{3,2,1,0:T(8,128)(2,1)S(1)}, bf16[4,11,16,128]{3,2,1,0:T(8,128)(2,1)S(1)}, u32[]{:S(2)}, u32[]{:S(2)}) collective-permute-start(bf16[4,11,16,128]{3,2,1,0:T(8,128)(2,1)S(1)} %collective-permute-done.19.refs_5_), channel_id=1, source_target_pairs={{0,28},{1,29},{2,30},{3,31},{4,0},{5,1},{6,2},{7,3},{8,4},{9,5},{1... | collective-permute-start | bytes 540680 | tf_op jit(solution)/shard_map/ppermute | solution.py:416
  25.3 4.0 %collective-permute-done.23.refs_10_ = bf16[4,11,16,128]{3,2,1,0:T(8,128)(2,1)S(1)} collective-permute-done((bf16[4,11,16,128]{3,2,1,0:T(8,128)(2,1)S(1)}, bf16[4,11,16,128]{3,2,1,0:T(8,128)(2,1)S(1)}, u32[]{:S(2)}, u32[]{:S(2)}) %collective-permute-start.23) | collective-permute-done | bytes 180256 | tf_op jit(solution)/shard_map/ppermute | solution.py:416
  29.4 1.2 %collective-permute-start.4 = (bf16[6,16,128]{2,1,0:T(8,128)(2,1)S(1)}, bf16[6,16,128]{2,1,0:T(8,128)(2,1)S(1)}, u32[]{:S(2)}, u32[]{:S(2)}) collective-permute-start(bf16[6,16,128]{2,1,0:T(8,128)(2,1)S(1)} %copy-done.31), channel_id=1, source_target_pairs={{0,2},{1,3},{2,0},{3,1},{4,6},{5,7},{6,4},{7,5},{8,10},{9,11},{10,... | collective-permute-start | bytes 73736 | tf_op jit(solution)/shard_map/ppermute | solution.py:412
  30.6 0.6 collective-permute-start.5
  31.2 2.1 %collective-permute-done.4 = bf16[6,16,128]{2,1,0:T(8,128)(2,1)S(1)} collective-permute-done((bf16[6,16,128]{2,1,0:T(8,128)(2,1)S(1)}, bf16[6,16,128]{2,1,0:T(8,128)(2,1)S(1)}, u32[]{:S(2)}, u32[]{:S(2)}) %collective-permute-start.4) | collective-permute-done | bytes 24608 | tf_op jit(solution)/shard_map/ppermute | solution.py:412
  33.3 0.6 collective-permute-done.5
  33.9 3.2 %collective-permute-start.6 = (bf16[4,6,16,128]{3,2,1,0:T(8,128)(2,1)S(1)}, bf16[4,6,16,128]{3,2,1,0:T(8,128)(2,1)S(1)}, u32[]{:S(2)}, u32[]{:S(2)}) collective-permute-start(bf16[4,6,16,128]{3,2,1,0:T(8,128)(2,1)S(1)} %pad_maximum_fusion.1.refs_4_), channel_id=1, source_target_pairs={{0,28},{1,29},{2,30},{3,31},{4,0},{5,1},{6,2},{7,3},{8,4},{9,5},{1... | collective-permute-start | bytes 294920 | tf_op jit(solution)/shard_map/ppermute | solution.py:416
  37.1 0.1 collective-permute-start.21
  37.2 1.9 %collective-permute-start.25 = (bf16[4,11,16,128]{3,2,1,0:T(8,128)(2,1)S(1)}, bf16[4,11,16,128]{3,2,1,0:T(8,128)(2,1)S(1)}, u32[]{:S(2)}, u32[]{:S(2)}) collective-permute-start(bf16[4,11,16,128]{3,2,1,0:T(8,128)(2,1)S(1)} %collective-permute-done.24.refs_9_), channel_id=1, source_target_pairs={{0,4},{1,5},{2,6},{3,7},{4,8},{5,9},{6,10},{7,11},{8,12},{9,13},{1... | collective-permute-start | bytes 540680 | tf_op jit(solution)/shard_map/ppermute | solution.py:416
  39.2 1.1 collective-permute-done.6.refs_5_
  40.3 3.7 %collective-permute-start.7 = (bf16[4,6,16,128]{3,2,1,0:T(8,128)(2,1)S(1)}, bf16[4,6,16,128]{3,2,1,0:T(8,128)(2,1)S(1)}, u32[]{:S(2)}, u32[]{:S(2)}) collective-permute-start(bf16[4,6,16,128]{3,2,1,0:T(8,128)(2,1)S(1)} %collective-permute-done.6.refs_5_), channel_id=1, source_target_pairs={{0,28},{1,29},{2,30},{3,31},{4,0},{5,1},{6,2},{7,3},{8,4},{9,5},{1... | collective-permute-start | bytes 294920 | tf_op jit(solution)/shard_map/ppermute | solution.py:416
  44.0 2.9 %collective-permute-done.10.refs_11_ = bf16[4,6,16,128]{3,2,1,0:T(8,128)(2,1)S(1)} collective-permute-done((bf16[4,6,16,128]{3,2,1,0:T(8,128)(2,1)S(1)}, bf16[4,6,16,128]{3,2,1,0:T(8,128)(2,1)S(1)}, u32[]{:S(2)}, u32[]{:S(2)}) %collective-permute-start.10) | collective-permute-done | bytes 98336 | tf_op jit(solution)/shard_map/ppermute | solution.py:416
  46.9 0.4 collective-permute-start.11
  47.3 2.8 %collective-permute-start.8 = (bf16[4,6,16,128]{3,2,1,0:T(8,128)(2,1)S(1)}, bf16[4,6,16,128]{3,2,1,0:T(8,128)(2,1)S(1)}, u32[]{:S(2)}, u32[]{:S(2)}) collective-permute-start(bf16[4,6,16,128]{3,2,1,0:T(8,128)(2,1)S(1)} %collective-permute-done.7.refs_6_), channel_id=1, source_target_pairs={{0,28},{1,29},{2,30},{3,31},{4,0},{5,1},{6,2},{7,3},{8,4},{9,5},{1... | collective-permute-start | bytes 294920 | tf_op jit(solution)/shard_map/ppermute | solution.py:416
  50.1 1.2 collective-permute-done.refs_1_
  51.3 0.9 collective-permute-start.1
  52.2 2.7 %collective-permute-done.1.refs_2_ = s32[1,4]{1,0:T(1,128)S(1)} collective-permute-done((s32[1,4]{1,0:T(1,128)S(1)}, s32[1,4]{1,0:T(1,128)S(1)}, u32[]{:S(2)}, u32[]{:S(2)}) %collective-permute-start.1) | collective-permute-done | bytes 48 | tf_op jit(solution)/shard_map/ppermute | solution.py:412
  54.8 3.0 %collective-permute-done.2.refs_3_ = s32[1,4]{1,0:T(1,128)S(1)} collective-permute-done((s32[1,4]{1,0:T(1,128)S(1)}, s32[1,4]{1,0:T(1,128)S(1)}, u32[]{:S(2)}, u32[]{:S(2)}) %collective-permute-start.2) | collective-permute-done | bytes 48 | tf_op jit(solution)/shard_map/ppermute | solution.py:412
  57.9 0.5 copy-done.36
  58.4 0.1 copy-done.11
  58.5 0.7 copy-done.12
  59.2 2.4 %select.3 = (bf16[4,11,16,128]{3,2,1,0:T(8,128)(2,1)}, bf16[4,11,16,128]{3,2,1,0:T(8,128)(2,1)}, bf16[4,11,16,128]{3,2,1,0:T(8,128)(2,1)}, bf16[4,11,16,128]{3,2,1,0:T(8,128)(2,1)}) custom-call(s32[1,4]{1,0:T(1,128)} %refs_0_.3, s32[1,4]{1,0:T(1,128)} %copy-done.34, s32[1,4]{1,0:T(1,128)} %copy-done.35, s32[1,4]{1,0:T(1,128)} %copy-done.36, ...), custom_call_target="tpu_custom_call" | custom-call | tf_op jit(solution)/shard_map/select/pallas_call | solution.py:231
  61.9 3.2 %collective-permute-start.9 = (bf16[4,6,16,128]{3,2,1,0:T(8,128)(2,1)S(1)}, bf16[4,6,16,128]{3,2,1,0:T(8,128)(2,1)S(1)}, u32[]{:S(2)}, u32[]{:S(2)}) collective-permute-start(bf16[4,6,16,128]{3,2,1,0:T(8,128)(2,1)S(1)} %collective-permute-done.8.refs_7_), channel_id=1, source_target_pairs={{0,28},{1,29},{2,30},{3,31},{4,0},{5,1},{6,2},{7,3},{8,4},{9,5},{1... | collective-permute-start | bytes 294920 | tf_op jit(solution)/shard_map/ppermute | solution.py:416
  65.1 0.9 collective-permute-start.27
  66.0 0.3 collective-permute-start.28
  66.3 1.9 %collective-permute-done.12.refs_9_ = bf16[4,6,16,128]{3,2,1,0:T(8,128)(2,1)S(1)} collective-permute-done((bf16[4,6,16,128]{3,2,1,0:T(8,128)(2,1)S(1)}, bf16[4,6,16,128]{3,2,1,0:T(8,128)(2,1)S(1)}, u32[]{:S(2)}, u32[]{:S(2)}) %collective-permute-start.12) | collective-permute-done | bytes 98336 | tf_op jit(solution)/shard_map/ppermute | solution.py:416
  68.2 0.6 copy-done.23
  68.8 0.6 copy-done.24
  69.4 2.1 %select.2 = (bf16[4,6,16,128]{3,2,1,0:T(8,128)(2,1)}, bf16[4,6,16,128]{3,2,1,0:T(8,128)(2,1)}, bf16[4,6,16,128]{3,2,1,0:T(8,128)(2,1)}, bf16[4,6,16,128]{3,2,1,0:T(8,128)(2,1)}) custom-call(s32[1,4]{1,0:T(1,128)} %refs_0_.3, s32[1,4]{1,0:T(1,128)} %copy-done.34, s32[1,4]{1,0:T(1,128)} %copy-done.35, s32[1,4]{1,0:T(1,128)} %copy-done.36, ...), custom_call_target="tpu_custom_call" | custom-call | tf_op jit(solution)/shard_map/select/pallas_call | solution.py:231
  71.6 1.0 collective-permute-start.14
  72.6 0.9 collective-permute-start.15
  74.1 0.5 collective-permute-done.28.refs_7_
  74.6 0.2 copy-done.13
  74.8 0.5 copy-done.14
  75.3 5.4 %shard_map.82 = (f32[256,384]{1,0:T(8,128)}, f32[256,128]{1,0:T(8,128)}) custom-call(f32[1]{0:T(128)S(6)} %copy.9.decay_ref, bf16[11,16,128]{2,1,0:T(8,128)(2,1)} %get-tuple-element.39.refs_0_, bf16[11,16,128]{2,1,0:T(8,128)(2,1)} %get-tuple-element.40.refs_1_, bf16[11,16,128]{2,1,0:T(8,128)(2,1)} %get-tuple-element.41.refs_2_, ...), custom_call_target="tpu_custom_call" | custom-call | tf_op jit(solution)/shard_map/pallas_call | solution.py:340
  80.7 0.6 copy-done.20
  81.3 3.9 %shard_map.83 = (bf16[72,384]{1,0:T(8,128)(2,1)}, bf16[72,384]{1,0:T(8,128)(2,1)}, bf16[72,384]{1,0:T(8,128)(2,1)}, bf16[72,384]{1,0:T(8,128)(2,1)}) custom-call(f32[1]{0:T(128)S(6)} %copy.9.decay_ref, bf16[6,16,128]{2,1,0:T(8,128)(2,1)} %get-tuple-element.31.refs_0_, bf16[6,16,128]{2,1,0:T(8,128)(2,1)} %get-tuple-element.32.refs_1_, ...), custom_call_target="tpu_custom_call" | custom-call | tf_op jit(solution)/shard_map/pallas_call | solution.py:340
  85.2 0.8 collective-permute-start.29
  86.0 1.1 collective-permute-start.30
  87.1 2.8 %collective-permute-start.31 = (bf16[72,384]{1,0:T(8,128)(2,1)}, bf16[72,384]{1,0:T(8,128)(2,1)S(1)}, u32[]{:S(2)}, u32[]{:S(2)}) collective-permute-start(bf16[72,384]{1,0:T(8,128)(2,1)} %get-tuple-element.52), channel_id=1, source_target_pairs={{0,96},{32,64},{64,32},{96,0},{128,224},{160,192},{192,160},{224,1... | collective-permute-start | bytes 165896 | tf_op jit(solution)/shard_map/ppermute | solution.py:412
  89.9 2.6 %collective-permute-done.30.refs_2_ = bf16[72,384]{1,0:T(8,128)(2,1)S(1)} collective-permute-done((bf16[72,384]{1,0:T(8,128)(2,1)}, bf16[72,384]{1,0:T(8,128)(2,1)S(1)}, u32[]{:S(2)}, u32[]{:S(2)}) %collective-permute-start.30) | collective-permute-done | bytes 55328 | tf_op jit(solution)/shard_map/ppermute | solution.py:412
  92.5 1.2 %collective-permute-done.31.refs_3_ = bf16[72,384]{1,0:T(8,128)(2,1)S(1)} collective-permute-done((bf16[72,384]{1,0:T(8,128)(2,1)}, bf16[72,384]{1,0:T(8,128)(2,1)S(1)}, u32[]{:S(2)}, u32[]{:S(2)}) %collective-permute-start.31) | collective-permute-done | bytes 55328 | tf_op jit(solution)/shard_map/ppermute | solution.py:412
  93.7 0.6 copy-done.4
  94.3 1.6 %scan.1 = bf16[64,384]{1,0:T(8,128)(2,1)} custom-call(bf16[72,384]{1,0:T(8,128)(2,1)} %get-tuple-element.49.refs_0_, bf16[72,384]{1,0:T(8,128)(2,1)} %copy-done.2, bf16[72,384]{1,0:T(8,128)(2,1)} %copy-done.3, bf16[72,384]{1,0:T(8,128)(2,1)} %copy-done.4), custom_call_target="tpu_custom_call" | custom-call | tf_op jit(solution)/shard_map/scan/pallas_call | solution.py:380
  95.9 4.8 %collective-permute-start.32 = (bf16[64,384]{1,0:T(8,128)(2,1)}, bf16[64,384]{1,0:T(8,128)(2,1)S(1)}, u32[]{:S(2)}, u32[]{:S(2)}) collective-permute-start(bf16[64,384]{1,0:T(8,128)(2,1)} %scan.1), channel_id=1, source_target_pairs={{0,128},{32,160},{64,192},{96,224},{1,129},{33,161},{65,193},{97,2... | collective-permute-start | bytes 147464 | tf_op jit(solution)/shard_map/ppermute | solution.py:445
  100.7 2.0 %collective-permute-done.32.refs_4_ = bf16[64,384]{1,0:T(8,128)(2,1)S(1)} collective-permute-done((bf16[64,384]{1,0:T(8,128)(2,1)}, bf16[64,384]{1,0:T(8,128)(2,1)S(1)}, u32[]{:S(2)}, u32[]{:S(2)}) %collective-permute-start.32) | collective-permute-done | bytes 49184 | tf_op jit(solution)/shard_map/ppermute | solution.py:445
  102.7 0.6 copy-done.29
  103.3 1.7 %rescan.1 = (bf16[64,384]{1,0:T(8,128)(2,1)}, bf16[64,384]{1,0:T(8,128)(2,1)}, bf16[64,384]{1,0:T(8,128)(2,1)}, bf16[64,384]{1,0:T(8,128)(2,1)}) custom-call(bf16[72,384]{1,0:T(8,128)(2,1)} %get-tuple-element.49.refs_0_, bf16[72,384]{1,0:T(8,128)(2,1)} %copy-done.2, bf16[72,384]{1,0:T(8,128)(2,1)} %copy-done.3, bf16[72,384]{1,0:T(8,128)(2,1)} %copy-done.4, ...), custom_call_target="tpu_custom_call" | custom-call | tf_op jit(solution)/shard_map/rescan/pallas_call | solution.py:380
  105.0 0.2 collective-permute-start.33
  105.2 3.4 %collective-permute-start.34 = (bf16[64,384]{1,0:T(8,128)(2,1)}, bf16[64,384]{1,0:T(8,128)(2,1)S(1)}, u32[]{:S(2)}, u32[]{:S(2)}) collective-permute-start(bf16[64,384]{1,0:T(8,128)(2,1)} %get-tuple-element.55), channel_id=1, source_target_pairs={{0,64},{32,96},{64,0},{96,32},{128,192},{160,224},{192,128},{224,1... | collective-permute-start | bytes 147464 | tf_op jit(solution)/shard_map/ppermute | solution.py:412
  108.6 1.1 collective-permute-start.35
  109.7 1.7 %collective-permute-done.34.refs_2_ = bf16[64,384]{1,0:T(8,128)(2,1)S(1)} collective-permute-done((bf16[64,384]{1,0:T(8,128)(2,1)}, bf16[64,384]{1,0:T(8,128)(2,1)S(1)}, u32[]{:S(2)}, u32[]{:S(2)}) %collective-permute-start.34) | collective-permute-done | bytes 49184 | tf_op jit(solution)/shard_map/ppermute | solution.py:412
  111.4 2.7 %collective-permute-done.35.refs_3_ = bf16[64,384]{1,0:T(8,128)(2,1)S(1)} collective-permute-done((bf16[64,384]{1,0:T(8,128)(2,1)}, bf16[64,384]{1,0:T(8,128)(2,1)S(1)}, u32[]{:S(2)}, u32[]{:S(2)}) %collective-permute-start.35) | collective-permute-done | bytes 49184 | tf_op jit(solution)/shard_map/ppermute | solution.py:412
  114.1 0.6 copy-done.28
  114.7 1.6 %gather.1 = bf16[4,64,384]{2,1,0:T(8,128)(2,1)} custom-call(bf16[64,384]{1,0:T(8,128)(2,1)} %get-tuple-element.53.refs_0_, bf16[64,384]{1,0:T(8,128)(2,1)} %copy-done.26, bf16[64,384]{1,0:T(8,128)(2,1)} %copy-done.27, bf16[64,384]{1,0:T(8,128)(2,1)} %copy-done.28), custom_call_target="tpu_custom_call" | custom-call | tf_op jit(solution)/shard_map/gather/pallas_call | solution.py:402
  (92 shorter events, 0.7 us)
Async XLA Ops:
  4.8 1.9 %collective-permute-start.16 = (bf16[11,16,128]{2,1,0:T(8,128)(2,1)}, bf16[11,16,128]{2,1,0:T(8,128)(2,1)S(1)}, u32[]{:S(2)}, u32[]{:S(2)}) collective-permute-start(bf16[11,16,128]{2,1,0:T(8,128)(2,1)} %get-tuple-element.40.refs_1_), channel_id=1, source_target_pairs={{0,1},{1,0},{2,3},{3,2},{4,5},{5,4},{6,7},{7,6},{8,9},{9,8},{10,11... | collective-permute-start | bytes 135176 | tf_op jit(solution)/shard_map/ppermute | solution.py:412
  4.9 4.3 %collective-permute-start.17 = (bf16[11,16,128]{2,1,0:T(8,128)(2,1)}, bf16[11,16,128]{2,1,0:T(8,128)(2,1)S(1)}, u32[]{:S(2)}, u32[]{:S(2)}) collective-permute-start(bf16[11,16,128]{2,1,0:T(8,128)(2,1)} %get-tuple-element.41.refs_2_), channel_id=1, source_target_pairs={{0,2},{1,3},{2,0},{3,1},{4,6},{5,7},{6,4},{7,5},{8,10},{9,11},{10,... | collective-permute-start | bytes 135176 | tf_op jit(solution)/shard_map/ppermute | solution.py:412
  6.5 3.9 %collective-permute-start.18 = (bf16[11,16,128]{2,1,0:T(8,128)(2,1)}, bf16[11,16,128]{2,1,0:T(8,128)(2,1)S(1)}, u32[]{:S(2)}, u32[]{:S(2)}) collective-permute-start(bf16[11,16,128]{2,1,0:T(8,128)(2,1)} %get-tuple-element.42.refs_3_), channel_id=1, source_target_pairs={{0,3},{1,2},{2,1},{3,0},{4,7},{5,6},{6,5},{7,4},{8,11},{9,10},{10,... | collective-permute-start | bytes 135176 | tf_op jit(solution)/shard_map/ppermute | solution.py:412
  10.4 18.9 %copy-start.30 = (bf16[6,16,128]{2,1,0:T(8,128)(2,1)S(1)}, bf16[6,16,128]{2,1,0:T(8,128)(2,1)}, u32[]{:S(2)}) copy-start(bf16[6,16,128]{2,1,0:T(8,128)(2,1)} %get-tuple-element.32.refs_1_) | copy-start | bytes 73732
  10.4 19.0 %copy-start.31 = (bf16[6,16,128]{2,1,0:T(8,128)(2,1)S(1)}, bf16[6,16,128]{2,1,0:T(8,128)(2,1)}, u32[]{:S(2)}) copy-start(bf16[6,16,128]{2,1,0:T(8,128)(2,1)} %get-tuple-element.33.refs_2_) | copy-start | bytes 73732
  10.4 20.2 %copy-start.32 = (bf16[6,16,128]{2,1,0:T(8,128)(2,1)S(1)}, bf16[6,16,128]{2,1,0:T(8,128)(2,1)}, u32[]{:S(2)}) copy-start(bf16[6,16,128]{2,1,0:T(8,128)(2,1)} %get-tuple-element.34.refs_3_) | copy-start | bytes 73732
  10.4 23.5 %copy-start.25 = (bf16[6,16,128]{2,1,0:T(8,128)(2,1)S(1)}, bf16[6,16,128]{2,1,0:T(8,128)(2,1)}, u32[]{:S(2)}) copy-start(bf16[6,16,128]{2,1,0:T(8,128)(2,1)} %get-tuple-element.31.refs_0_) | copy-start | bytes 73732
  11.3 46.6 %copy-start = (bf16[4,11,16,128]{3,2,1,0:T(8,128)(2,1)}, bf16[4,11,16,128]{3,2,1,0:T(8,128)(2,1)S(1)}, u32[]{:S(2)}) copy-start(bf16[4,11,16,128]{3,2,1,0:T(8,128)(2,1)S(1)} %pad_maximum_fusion.refs_4_) | copy-start | bytes 540676
  11.3 10.8 %collective-permute-start.22 = (bf16[4,11,16,128]{3,2,1,0:T(8,128)(2,1)S(1)}, bf16[4,11,16,128]{3,2,1,0:T(8,128)(2,1)S(1)}, u32[]{:S(2)}, u32[]{:S(2)}) collective-permute-start(bf16[4,11,16,128]{3,2,1,0:T(8,128)(2,1)S(1)} %pad_maximum_fusion.refs_4_), channel_id=1, source_target_pairs={{0,4},{1,5},{2,6},{3,7},{4,8},{5,9},{6,10},{7,11},{8,12},{9,13},{1... | collective-permute-start | bytes 540680 | tf_op jit(solution)/shard_map/ppermute | solution.py:416
  13.3 8.8 %collective-permute-start.19 = (bf16[4,11,16,128]{3,2,1,0:T(8,128)(2,1)S(1)}, bf16[4,11,16,128]{3,2,1,0:T(8,128)(2,1)S(1)}, u32[]{:S(2)}, u32[]{:S(2)}) collective-permute-start(bf16[4,11,16,128]{3,2,1,0:T(8,128)(2,1)S(1)} %pad_maximum_fusion.refs_4_), channel_id=1, source_target_pairs={{0,28},{1,29},{2,30},{3,31},{4,0},{5,1},{6,2},{7,3},{8,4},{9,5},{1... | collective-permute-start | bytes 540680 | tf_op jit(solution)/shard_map/ppermute | solution.py:416
  22.1 35.8 %copy-start.5 = (bf16[4,11,16,128]{3,2,1,0:T(8,128)(2,1)}, bf16[4,11,16,128]{3,2,1,0:T(8,128)(2,1)S(1)}, u32[]{:S(2)}) copy-start(bf16[4,11,16,128]{3,2,1,0:T(8,128)(2,1)S(1)} %collective-permute-done.22.refs_11_) | copy-start | bytes 540676
  22.1 7.2 %collective-permute-start.23 = (bf16[4,11,16,128]{3,2,1,0:T(8,128)(2,1)S(1)}, bf16[4,11,16,128]{3,2,1,0:T(8,128)(2,1)S(1)}, u32[]{:S(2)}, u32[]{:S(2)}) collective-permute-start(bf16[4,11,16,128]{3,2,1,0:T(8,128)(2,1)S(1)} %collective-permute-done.22.refs_11_), channel_id=1, source_target_pairs={{0,4},{1,5},{2,6},{3,7},{4,8},{5,9},{6,10},{7,11},{8,12},{9,13},{1... | collective-permute-start | bytes 540680 | tf_op jit(solution)/shard_map/ppermute | solution.py:416
  22.1 35.8 %copy-start.6 = (bf16[4,11,16,128]{3,2,1,0:T(8,128)(2,1)}, bf16[4,11,16,128]{3,2,1,0:T(8,128)(2,1)S(1)}, u32[]{:S(2)}) copy-start(bf16[4,11,16,128]{3,2,1,0:T(8,128)(2,1)S(1)} %collective-permute-done.19.refs_5_) | copy-start | bytes 540676
  22.1 15.0 %collective-permute-start.20 = (bf16[4,11,16,128]{3,2,1,0:T(8,128)(2,1)S(1)}, bf16[4,11,16,128]{3,2,1,0:T(8,128)(2,1)S(1)}, u32[]{:S(2)}, u32[]{:S(2)}) collective-permute-start(bf16[4,11,16,128]{3,2,1,0:T(8,128)(2,1)S(1)} %collective-permute-done.19.refs_5_), channel_id=1, source_target_pairs={{0,28},{1,29},{2,30},{3,31},{4,0},{5,1},{6,2},{7,3},{8,4},{9,5},{1... | collective-permute-start | bytes 540680 | tf_op jit(solution)/shard_map/ppermute | solution.py:416
  29.3 28.6 %copy-start.7 = (bf16[4,11,16,128]{3,2,1,0:T(8,128)(2,1)}, bf16[4,11,16,128]{3,2,1,0:T(8,128)(2,1)S(1)}, u32[]{:S(2)}) copy-start(bf16[4,11,16,128]{3,2,1,0:T(8,128)(2,1)S(1)} %collective-permute-done.23.refs_10_) | copy-start | bytes 540676
  29.3 7.9 %collective-permute-start.24 = (bf16[4,11,16,128]{3,2,1,0:T(8,128)(2,1)S(1)}, bf16[4,11,16,128]{3,2,1,0:T(8,128)(2,1)S(1)}, u32[]{:S(2)}, u32[]{:S(2)}) collective-permute-start(bf16[4,11,16,128]{3,2,1,0:T(8,128)(2,1)S(1)} %collective-permute-done.23.refs_10_), channel_id=1, source_target_pairs={{0,4},{1,5},{2,6},{3,7},{4,8},{5,9},{6,10},{7,11},{8,12},{9,13},{1... | collective-permute-start | bytes 540680 | tf_op jit(solution)/shard_map/ppermute | solution.py:416
  29.3 2.0 %collective-permute-start.3 = (bf16[6,16,128]{2,1,0:T(8,128)(2,1)S(1)}, bf16[6,16,128]{2,1,0:T(8,128)(2,1)S(1)}, u32[]{:S(2)}, u32[]{:S(2)}) collective-permute-start(bf16[6,16,128]{2,1,0:T(8,128)(2,1)S(1)} %copy-done.30), channel_id=1, source_target_pairs={{0,1},{1,0},{2,3},{3,2},{4,5},{5,4},{6,7},{7,6},{8,9},{9,8},{10,11... | collective-permute-start | bytes 73736 | tf_op jit(solution)/shard_map/ppermute | solution.py:412
  29.4 3.9 %collective-permute-start.4 = (bf16[6,16,128]{2,1,0:T(8,128)(2,1)S(1)}, bf16[6,16,128]{2,1,0:T(8,128)(2,1)S(1)}, u32[]{:S(2)}, u32[]{:S(2)}) collective-permute-start(bf16[6,16,128]{2,1,0:T(8,128)(2,1)S(1)} %copy-done.31), channel_id=1, source_target_pairs={{0,2},{1,3},{2,0},{3,1},{4,6},{5,7},{6,4},{7,5},{8,10},{9,11},{10,... | collective-permute-start | bytes 73736 | tf_op jit(solution)/shard_map/ppermute | solution.py:412
  30.6 3.3 %collective-permute-start.5 = (bf16[6,16,128]{2,1,0:T(8,128)(2,1)S(1)}, bf16[6,16,128]{2,1,0:T(8,128)(2,1)S(1)}, u32[]{:S(2)}, u32[]{:S(2)}) collective-permute-start(bf16[6,16,128]{2,1,0:T(8,128)(2,1)S(1)} %copy-done.32), channel_id=1, source_target_pairs={{0,3},{1,2},{2,1},{3,0},{4,7},{5,6},{6,5},{7,4},{8,11},{9,10},{10,... | collective-permute-start | bytes 73736 | tf_op jit(solution)/shard_map/ppermute | solution.py:412
  33.9 16.2 %copy-start.33 = (s32[1,4]{1,0:T(1,128)S(1)}, s32[1,4]{1,0:T(1,128)}, u32[]{:S(2)}) copy-start(s32[1,4]{1,0:T(1,128)} %refs_0_.3) | copy-start | bytes 52
  33.9 27.7 %copy-start.1 = (bf16[4,6,16,128]{3,2,1,0:T(8,128)(2,1)}, bf16[4,6,16,128]{3,2,1,0:T(8,128)(2,1)S(1)}, u32[]{:S(2)}) copy-start(bf16[4,6,16,128]{3,2,1,0:T(8,128)(2,1)S(1)} %pad_maximum_fusion.1.refs_4_) | copy-start | bytes 294916
  33.9 6.4 %collective-permute-start.6 = (bf16[4,6,16,128]{3,2,1,0:T(8,128)(2,1)S(1)}, bf16[4,6,16,128]{3,2,1,0:T(8,128)(2,1)S(1)}, u32[]{:S(2)}, u32[]{:S(2)}) collective-permute-start(bf16[4,6,16,128]{3,2,1,0:T(8,128)(2,1)S(1)} %pad_maximum_fusion.1.refs_4_), channel_id=1, source_target_pairs={{0,28},{1,29},{2,30},{3,31},{4,0},{5,1},{6,2},{7,3},{8,4},{9,5},{1... | collective-permute-start | bytes 294920 | tf_op jit(solution)/shard_map/ppermute | solution.py:416
  37.1 20.8 %copy-start.8 = (bf16[4,11,16,128]{3,2,1,0:T(8,128)(2,1)}, bf16[4,11,16,128]{3,2,1,0:T(8,128)(2,1)S(1)}, u32[]{:S(2)}) copy-start(bf16[4,11,16,128]{3,2,1,0:T(8,128)(2,1)S(1)} %collective-permute-done.20.refs_6_) | copy-start | bytes 540676
  37.1 20.7 %collective-permute-start.21 = (bf16[4,11,16,128]{3,2,1,0:T(8,128)(2,1)S(1)}, bf16[4,11,16,128]{3,2,1,0:T(8,128)(2,1)S(1)}, u32[]{:S(2)}, u32[]{:S(2)}) collective-permute-start(bf16[4,11,16,128]{3,2,1,0:T(8,128)(2,1)S(1)} %collective-permute-done.20.refs_6_), channel_id=1, source_target_pairs={{0,28},{1,29},{2,30},{3,31},{4,0},{5,1},{6,2},{7,3},{8,4},{9,5},{1... | collective-permute-start | bytes 540680 | tf_op jit(solution)/shard_map/ppermute | solution.py:416
  37.2 20.7 %copy-start.9 = (bf16[4,11,16,128]{3,2,1,0:T(8,128)(2,1)}, bf16[4,11,16,128]{3,2,1,0:T(8,128)(2,1)S(1)}, u32[]{:S(2)}) copy-start(bf16[4,11,16,128]{3,2,1,0:T(8,128)(2,1)S(1)} %collective-permute-done.24.refs_9_) | copy-start | bytes 540676
  37.2 20.6 %collective-permute-start.25 = (bf16[4,11,16,128]{3,2,1,0:T(8,128)(2,1)S(1)}, bf16[4,11,16,128]{3,2,1,0:T(8,128)(2,1)S(1)}, u32[]{:S(2)}, u32[]{:S(2)}) collective-permute-start(bf16[4,11,16,128]{3,2,1,0:T(8,128)(2,1)S(1)} %collective-permute-done.24.refs_9_), channel_id=1, source_target_pairs={{0,4},{1,5},{2,6},{3,7},{4,8},{5,9},{6,10},{7,11},{8,12},{9,13},{1... | collective-permute-start | bytes 540680 | tf_op jit(solution)/shard_map/ppermute | solution.py:416
  39.1 7.7 %collective-permute-start.10 = (bf16[4,6,16,128]{3,2,1,0:T(8,128)(2,1)S(1)}, bf16[4,6,16,128]{3,2,1,0:T(8,128)(2,1)S(1)}, u32[]{:S(2)}, u32[]{:S(2)}) collective-permute-start(bf16[4,6,16,128]{3,2,1,0:T(8,128)(2,1)S(1)} %pad_maximum_fusion.1.refs_4_), channel_id=1, source_target_pairs={{0,4},{1,5},{2,6},{3,7},{4,8},{5,9},{6,10},{7,11},{8,12},{9,13},{1... | collective-permute-start | bytes 294920 | tf_op jit(solution)/shard_map/ppermute | solution.py:416
  40.3 21.3 %copy-start.15 = (bf16[4,6,16,128]{3,2,1,0:T(8,128)(2,1)}, bf16[4,6,16,128]{3,2,1,0:T(8,128)(2,1)S(1)}, u32[]{:S(2)}) copy-start(bf16[4,6,16,128]{3,2,1,0:T(8,128)(2,1)S(1)} %collective-permute-done.6.refs_5_) | copy-start | bytes 294916
  40.3 7.0 %collective-permute-start.7 = (bf16[4,6,16,128]{3,2,1,0:T(8,128)(2,1)S(1)}, bf16[4,6,16,128]{3,2,1,0:T(8,128)(2,1)S(1)}, u32[]{:S(2)}, u32[]{:S(2)}) collective-permute-start(bf16[4,6,16,128]{3,2,1,0:T(8,128)(2,1)S(1)} %collective-permute-done.6.refs_5_), channel_id=1, source_target_pairs={{0,28},{1,29},{2,30},{3,31},{4,0},{5,1},{6,2},{7,3},{8,4},{9,5},{1... | collective-permute-start | bytes 294920 | tf_op jit(solution)/shard_map/ppermute | solution.py:416
  46.9 14.8 %copy-start.16 = (bf16[4,6,16,128]{3,2,1,0:T(8,128)(2,1)}, bf16[4,6,16,128]{3,2,1,0:T(8,128)(2,1)S(1)}, u32[]{:S(2)}) copy-start(bf16[4,6,16,128]{3,2,1,0:T(8,128)(2,1)S(1)} %collective-permute-done.10.refs_11_) | copy-start | bytes 294916
  46.9 14.9 %collective-permute-start.11 = (bf16[4,6,16,128]{3,2,1,0:T(8,128)(2,1)S(1)}, bf16[4,6,16,128]{3,2,1,0:T(8,128)(2,1)S(1)}, u32[]{:S(2)}, u32[]{:S(2)}) collective-permute-start(bf16[4,6,16,128]{3,2,1,0:T(8,128)(2,1)S(1)} %collective-permute-done.10.refs_11_), channel_id=1, source_target_pairs={{0,4},{1,5},{2,6},{3,7},{4,8},{5,9},{6,10},{7,11},{8,12},{9,13},{1... | collective-permute-start | bytes 294920 | tf_op jit(solution)/shard_map/ppermute | solution.py:416
  47.3 14.3 %copy-start.17 = (bf16[4,6,16,128]{3,2,1,0:T(8,128)(2,1)}, bf16[4,6,16,128]{3,2,1,0:T(8,128)(2,1)S(1)}, u32[]{:S(2)}) copy-start(bf16[4,6,16,128]{3,2,1,0:T(8,128)(2,1)S(1)} %collective-permute-done.7.refs_6_) | copy-start | bytes 294916
  47.3 14.6 %collective-permute-start.8 = (bf16[4,6,16,128]{3,2,1,0:T(8,128)(2,1)S(1)}, bf16[4,6,16,128]{3,2,1,0:T(8,128)(2,1)S(1)}, u32[]{:S(2)}, u32[]{:S(2)}) collective-permute-start(bf16[4,6,16,128]{3,2,1,0:T(8,128)(2,1)S(1)} %collective-permute-done.7.refs_6_), channel_id=1, source_target_pairs={{0,28},{1,29},{2,30},{3,31},{4,0},{5,1},{6,2},{7,3},{8,4},{9,5},{1... | collective-permute-start | bytes 294920 | tf_op jit(solution)/shard_map/ppermute | solution.py:416
  50.1 1.2 collective-permute-start
  51.3 6.6 %copy-start.34 = (s32[1,4]{1,0:T(1,128)}, s32[1,4]{1,0:T(1,128)S(1)}, u32[]{:S(2)}) copy-start(s32[1,4]{1,0:T(1,128)S(1)} %collective-permute-done.refs_1_) | copy-start | bytes 52
  51.3 3.6 %collective-permute-start.1 = (s32[1,4]{1,0:T(1,128)S(1)}, s32[1,4]{1,0:T(1,128)S(1)}, u32[]{:S(2)}, u32[]{:S(2)}) collective-permute-start(s32[1,4]{1,0:T(1,128)S(1)} %copy-done.33), channel_id=1, source_target_pairs={{0,2},{1,3},{2,0},{3,1},{4,6},{5,7},{6,4},{7,5},{8,10},{9,11},{10,... | collective-permute-start | bytes 56 | tf_op jit(solution)/shard_map/ppermute | solution.py:412
  54.8 3.1 %copy-start.35 = (s32[1,4]{1,0:T(1,128)}, s32[1,4]{1,0:T(1,128)S(1)}, u32[]{:S(2)}) copy-start(s32[1,4]{1,0:T(1,128)S(1)} %collective-permute-done.1.refs_2_) | copy-start | bytes 52
  54.8 3.0 %collective-permute-start.2 = (s32[1,4]{1,0:T(1,128)S(1)}, s32[1,4]{1,0:T(1,128)S(1)}, u32[]{:S(2)}, u32[]{:S(2)}) collective-permute-start(s32[1,4]{1,0:T(1,128)S(1)} %copy-done.33), channel_id=1, source_target_pairs={{0,3},{1,2},{2,1},{3,0},{4,7},{5,6},{6,5},{7,4},{8,11},{9,10},{10,... | collective-permute-start | bytes 56 | tf_op jit(solution)/shard_map/ppermute | solution.py:412
  57.8 0.7 copy-start.11
  58.5 0.7 copy-start.12
  61.6 10.9 %collective-permute-start.26 = (bf16[4,11,16,128]{3,2,1,0:T(8,128)(2,1)}, bf16[4,11,16,128]{3,2,1,0:T(8,128)(2,1)S(1)}, u32[]{:S(2)}, u32[]{:S(2)}) collective-permute-start(bf16[4,11,16,128]{3,2,1,0:T(8,128)(2,1)} %get-tuple-element.44), channel_id=1, source_target_pairs={{0,1},{1,0},{2,3},{3,2},{4,5},{5,4},{6,7},{7,6},{8,9},{9,8},{10,11... | collective-permute-start | bytes 540680 | tf_op jit(solution)/shard_map/ppermute | solution.py:412
  61.8 6.4 %copy-start.18 = (bf16[4,6,16,128]{3,2,1,0:T(8,128)(2,1)}, bf16[4,6,16,128]{3,2,1,0:T(8,128)(2,1)S(1)}, u32[]{:S(2)}) copy-start(bf16[4,6,16,128]{3,2,1,0:T(8,128)(2,1)S(1)} %collective-permute-done.11.refs_10_) | copy-start | bytes 294916
  61.8 6.4 %collective-permute-start.12 = (bf16[4,6,16,128]{3,2,1,0:T(8,128)(2,1)S(1)}, bf16[4,6,16,128]{3,2,1,0:T(8,128)(2,1)S(1)}, u32[]{:S(2)}, u32[]{:S(2)}) collective-permute-start(bf16[4,6,16,128]{3,2,1,0:T(8,128)(2,1)S(1)} %collective-permute-done.11.refs_10_), channel_id=1, source_target_pairs={{0,4},{1,5},{2,6},{3,7},{4,8},{5,9},{6,10},{7,11},{8,12},{9,13},{1... | collective-permute-start | bytes 294920 | tf_op jit(solution)/shard_map/ppermute | solution.py:416
  61.9 6.3 %copy-start.19 = (bf16[4,6,16,128]{3,2,1,0:T(8,128)(2,1)}, bf16[4,6,16,128]{3,2,1,0:T(8,128)(2,1)S(1)}, u32[]{:S(2)}) copy-start(bf16[4,6,16,128]{3,2,1,0:T(8,128)(2,1)S(1)} %collective-permute-done.8.refs_7_) | copy-start | bytes 294916
  61.9 6.3 %collective-permute-start.9 = (bf16[4,6,16,128]{3,2,1,0:T(8,128)(2,1)S(1)}, bf16[4,6,16,128]{3,2,1,0:T(8,128)(2,1)S(1)}, u32[]{:S(2)}, u32[]{:S(2)}) collective-permute-start(bf16[4,6,16,128]{3,2,1,0:T(8,128)(2,1)S(1)} %collective-permute-done.8.refs_7_), channel_id=1, source_target_pairs={{0,28},{1,29},{2,30},{3,31},{4,0},{5,1},{6,2},{7,3},{8,4},{9,5},{1... | collective-permute-start | bytes 294920 | tf_op jit(solution)/shard_map/ppermute | solution.py:416
  65.1 9.0 %collective-permute-start.27 = (bf16[4,11,16,128]{3,2,1,0:T(8,128)(2,1)}, bf16[4,11,16,128]{3,2,1,0:T(8,128)(2,1)S(1)}, u32[]{:S(2)}, u32[]{:S(2)}) collective-permute-start(bf16[4,11,16,128]{3,2,1,0:T(8,128)(2,1)} %get-tuple-element.45), channel_id=1, source_target_pairs={{0,2},{1,3},{2,0},{3,1},{4,6},{5,7},{6,4},{7,5},{8,10},{9,11},{10,... | collective-permute-start | bytes 540680 | tf_op jit(solution)/shard_map/ppermute | solution.py:412
  66.0 8.6 %collective-permute-start.28 = (bf16[4,11,16,128]{3,2,1,0:T(8,128)(2,1)}, bf16[4,11,16,128]{3,2,1,0:T(8,128)(2,1)S(1)}, u32[]{:S(2)}, u32[]{:S(2)}) collective-permute-start(bf16[4,11,16,128]{3,2,1,0:T(8,128)(2,1)} %get-tuple-element.46), channel_id=1, source_target_pairs={{0,3},{1,2},{2,1},{3,0},{4,7},{5,6},{6,5},{7,4},{8,11},{9,10},{10,... | collective-permute-start | bytes 540680 | tf_op jit(solution)/shard_map/ppermute | solution.py:412
  71.6 9.0 %collective-permute-start.13 = (bf16[4,6,16,128]{3,2,1,0:T(8,128)(2,1)}, bf16[4,6,16,128]{3,2,1,0:T(8,128)(2,1)S(1)}, u32[]{:S(2)}, u32[]{:S(2)}) collective-permute-start(bf16[4,6,16,128]{3,2,1,0:T(8,128)(2,1)} %get-tuple-element.36), channel_id=1, source_target_pairs={{0,1},{1,0},{2,3},{3,2},{4,5},{5,4},{6,7},{7,6},{8,9},{9,8},{10,11... | collective-permute-start | bytes 294920 | tf_op jit(solution)/shard_map/ppermute | solution.py:412
  71.6 9.1 %collective-permute-start.14 = (bf16[4,6,16,128]{3,2,1,0:T(8,128)(2,1)}, bf16[4,6,16,128]{3,2,1,0:T(8,128)(2,1)S(1)}, u32[]{:S(2)}, u32[]{:S(2)}) collective-permute-start(bf16[4,6,16,128]{3,2,1,0:T(8,128)(2,1)} %get-tuple-element.37), channel_id=1, source_target_pairs={{0,2},{1,3},{2,0},{3,1},{4,6},{5,7},{6,4},{7,5},{8,10},{9,11},{10,... | collective-permute-start | bytes 294920 | tf_op jit(solution)/shard_map/ppermute | solution.py:412
  72.6 2.0 %copy-start.10 = (bf16[4,11,16,128]{3,2,1,0:T(8,128)(2,1)}, bf16[4,11,16,128]{3,2,1,0:T(8,128)(2,1)S(1)}, u32[]{:S(2)}) copy-start(bf16[4,11,16,128]{3,2,1,0:T(8,128)(2,1)S(1)} %collective-permute-done.26.refs_5_) | copy-start | bytes 540676
  72.6 8.1 %collective-permute-start.15 = (bf16[4,6,16,128]{3,2,1,0:T(8,128)(2,1)}, bf16[4,6,16,128]{3,2,1,0:T(8,128)(2,1)S(1)}, u32[]{:S(2)}, u32[]{:S(2)}) collective-permute-start(bf16[4,6,16,128]{3,2,1,0:T(8,128)(2,1)} %get-tuple-element.38), channel_id=1, source_target_pairs={{0,3},{1,2},{2,1},{3,0},{4,7},{5,6},{6,5},{7,4},{8,11},{9,10},{10,... | collective-permute-start | bytes 294920 | tf_op jit(solution)/shard_map/ppermute | solution.py:412
  74.1 0.7 copy-start.13
  74.6 0.7 copy-start.14
  85.2 4.7 %collective-permute-start.29 = (bf16[72,384]{1,0:T(8,128)(2,1)}, bf16[72,384]{1,0:T(8,128)(2,1)S(1)}, u32[]{:S(2)}, u32[]{:S(2)}) collective-permute-start(bf16[72,384]{1,0:T(8,128)(2,1)} %get-tuple-element.50), channel_id=1, source_target_pairs={{0,32},{32,0},{64,96},{96,64},{128,160},{160,128},{192,224},{224,1... | collective-permute-start | bytes 165896 | tf_op jit(solution)/shard_map/ppermute | solution.py:412
  86.0 6.5 %collective-permute-start.30 = (bf16[72,384]{1,0:T(8,128)(2,1)}, bf16[72,384]{1,0:T(8,128)(2,1)S(1)}, u32[]{:S(2)}, u32[]{:S(2)}) collective-permute-start(bf16[72,384]{1,0:T(8,128)(2,1)} %get-tuple-element.51), channel_id=1, source_target_pairs={{0,64},{32,96},{64,0},{96,32},{128,192},{160,224},{192,128},{224,1... | collective-permute-start | bytes 165896 | tf_op jit(solution)/shard_map/ppermute | solution.py:412
  87.1 6.5 %collective-permute-start.31 = (bf16[72,384]{1,0:T(8,128)(2,1)}, bf16[72,384]{1,0:T(8,128)(2,1)S(1)}, u32[]{:S(2)}, u32[]{:S(2)}) collective-permute-start(bf16[72,384]{1,0:T(8,128)(2,1)} %get-tuple-element.52), channel_id=1, source_target_pairs={{0,96},{32,64},{64,32},{96,0},{128,224},{160,192},{192,160},{224,1... | collective-permute-start | bytes 165896 | tf_op jit(solution)/shard_map/ppermute | solution.py:412
  89.9 3.8 %copy-start.2 = (bf16[72,384]{1,0:T(8,128)(2,1)}, bf16[72,384]{1,0:T(8,128)(2,1)S(1)}, u32[]{:S(2)}) copy-start(bf16[72,384]{1,0:T(8,128)(2,1)S(1)} %collective-permute-done.29.refs_1_) | copy-start | bytes 165892
  92.5 1.2 %copy-start.3 = (bf16[72,384]{1,0:T(8,128)(2,1)}, bf16[72,384]{1,0:T(8,128)(2,1)S(1)}, u32[]{:S(2)}) copy-start(bf16[72,384]{1,0:T(8,128)(2,1)S(1)} %collective-permute-done.30.refs_2_) | copy-start | bytes 165892
  95.9 6.8 %collective-permute-start.32 = (bf16[64,384]{1,0:T(8,128)(2,1)}, bf16[64,384]{1,0:T(8,128)(2,1)S(1)}, u32[]{:S(2)}, u32[]{:S(2)}) collective-permute-start(bf16[64,384]{1,0:T(8,128)(2,1)} %scan.1), channel_id=1, source_target_pairs={{0,128},{32,160},{64,192},{96,224},{1,129},{33,161},{65,193},{97,2... | collective-permute-start | bytes 147464 | tf_op jit(solution)/shard_map/ppermute | solution.py:445
  105.0 4.7 %collective-permute-start.33 = (bf16[64,384]{1,0:T(8,128)(2,1)}, bf16[64,384]{1,0:T(8,128)(2,1)S(1)}, u32[]{:S(2)}, u32[]{:S(2)}) collective-permute-start(bf16[64,384]{1,0:T(8,128)(2,1)} %get-tuple-element.54), channel_id=1, source_target_pairs={{0,32},{32,0},{64,96},{96,64},{128,160},{160,128},{192,224},{224,1... | collective-permute-start | bytes 147464 | tf_op jit(solution)/shard_map/ppermute | solution.py:412
  105.2 6.2 %collective-permute-start.34 = (bf16[64,384]{1,0:T(8,128)(2,1)}, bf16[64,384]{1,0:T(8,128)(2,1)S(1)}, u32[]{:S(2)}, u32[]{:S(2)}) collective-permute-start(bf16[64,384]{1,0:T(8,128)(2,1)} %get-tuple-element.55), channel_id=1, source_target_pairs={{0,64},{32,96},{64,0},{96,32},{128,192},{160,224},{192,128},{224,1... | collective-permute-start | bytes 147464 | tf_op jit(solution)/shard_map/ppermute | solution.py:412
  108.6 5.5 %collective-permute-start.35 = (bf16[64,384]{1,0:T(8,128)(2,1)}, bf16[64,384]{1,0:T(8,128)(2,1)S(1)}, u32[]{:S(2)}, u32[]{:S(2)}) collective-permute-start(bf16[64,384]{1,0:T(8,128)(2,1)} %get-tuple-element.56), channel_id=1, source_target_pairs={{0,96},{32,64},{64,32},{96,0},{128,224},{160,192},{192,160},{224,1... | collective-permute-start | bytes 147464 | tf_op jit(solution)/shard_map/ppermute | solution.py:412
  109.7 4.4 %copy-start.26 = (bf16[64,384]{1,0:T(8,128)(2,1)}, bf16[64,384]{1,0:T(8,128)(2,1)S(1)}, u32[]{:S(2)}) copy-start(bf16[64,384]{1,0:T(8,128)(2,1)S(1)} %collective-permute-done.33.refs_1_) | copy-start | bytes 147460
  111.4 2.7 %copy-start.27 = (bf16[64,384]{1,0:T(8,128)(2,1)}, bf16[64,384]{1,0:T(8,128)(2,1)S(1)}, u32[]{:S(2)}) copy-start(bf16[64,384]{1,0:T(8,128)(2,1)S(1)} %collective-permute-done.34.refs_2_) | copy-start | bytes 147460
  (9 other events, 5.7 us)
where the time goes:
time: 118 us; the launch traced here: 116 us
  starting transfers between devices  46.8 us (40%)
  waiting for transfers between devices  38.4 us (33%)
  Pallas kernels  23.4 us (20%)
  local copies, waits for them, and re-layouts  5.82 us (5%)
    ppermute x14, starting transfers between devices, along(): lax.ppermute(value, 'sta', [(d, (d + 4 * step) % 32) for d in range(32)])  24.8 us
    ppermute x21, waiting for transfers between devices, across(): return lax.ppermute(value, axis, [(d, d ^ r) for d in range(size)])  21.7 us
    ppermute x21, starting transfers between devices, across(): return lax.ppermute(value, axis, [(d, d ^ r) for d in range(size)])  17.3 us
    ppermute x14, waiting for transfers between devices, along(): lax.ppermute(value, 'sta', [(d, (d + 4 * step) % 32) for d in range(32)])  14.6 us
    pallas_call x2, Pallas kernels, correlate(): pl.pallas_call(functools.partial(correlate_kernel, h), out_shape=shapes,...  9.24 us
    unnamed x74, local copies, waits for them, and re-layouts  5.82 us
    pallas_call x1, Pallas kernels, spectrum(): pl.pallas_call(spectrum_kernel, out_shape=shapes, in_specs=[pl.BlockSpec(...  4.83 us
    ppermute x1, starting transfers between devices, body(): entering = lax.ppermute(total, 'section', [(d, d + 4) for d in range(4)])  4.78 us
  transfers between devices with their start and end apart: 36, of which 18 were waited for; matrix products, arithmetic and copies ran while one was open for 0% of the time, Pallas kernels for 9%

commit v1 on v0

v1 whole, which is shorter than its diff:
```python
import functools
import math

import jax
import jax.numpy as jnp
import numpy as np
from jax import lax
from jax.experimental import pallas as pl
from jax.experimental.pallas import tpu as pltpu
from jax.sharding import Mesh
from jax.sharding import PartitionSpec as P


NF = 1024
LAGS = 384
NSAMP = 4096
LS = 8
SEGS = 8
PB = 4
EPSILON = 1e-05
HALVES = 2


def twiddles():
    k = np.arange(32)[:, None]
    b = np.arange(128)[None, :]
    angle = 2.0 * np.pi * (k * b) / NSAMP
    return np.stack([np.cos(angle), np.sin(angle)]).astype(np.float32)


def second_dft():
    b = np.arange(128)[:, None]
    m = np.arange(4, 36)[None, :]
    angle = 2.0 * np.pi * ((b * m) % 128) / 128
    cos, sin = np.cos(angle) / 64, np.sin(angle) / 64
    full = np.zeros((256, 256))
    full[:128, :32] = cos
    full[128:, :32] = sin
    full[:128, 128:160] = -sin
    full[128:, 128:160] = cos
    high = full.astype(jnp.bfloat16)
    low = (full - high.astype(np.float64)).astype(jnp.bfloat16)
    return np.stack([high, low])


def lag_table():
    freq = 128 + np.arange(NF)
    shift = np.arange(LAGS) + NSAMP - LAGS // 2
    phase = (freq[:, None] * shift[None, :] % NSAMP).astype(np.float32)
    phase = phase * np.float32(2.0 * np.pi / NSAMP)
    cos = np.cos(phase) / np.float32(math.sqrt(NF))
    sin = -np.sin(phase) / np.float32(math.sqrt(NF))
    lane = np.arange(128)
    rows = []
    for c in range(8):
        f = 8 * (lane // 32) + c + 32 * (lane % 32)
        rows += [cos[f], sin[f]]
    return np.concatenate(rows).reshape(8, 256, LAGS).astype(jnp.bfloat16)


def add(a, b):
    return b if a is None else a if b is None else a + b


def sub(a, b):
    if b is None:
        return a
    return -b if a is None else a - b


def real_fft(xs):
    n = len(xs)
    if n == 1:
        return [(xs[0], None)]
    if n == 2:
        return [(xs[0] + xs[1], None), (xs[0] - xs[1], None)]
    even, odd = real_fft(xs[0::2]), real_fft(xs[1::2])
    out = [None] * (n // 2 + 1)
    for k in range(n // 4 + 1):
        (er, ei), (orr, oi) = even[k], odd[k]
        if k == 0:
            tr, ti = orr, oi
        elif 4 * k == n:
            tr, ti = oi, None if orr is None else -orr
        else:
            c, s = math.cos(2 * math.pi * k / n), math.sin(2 * math.pi * k / n)
            if oi is None:
                tr, ti = orr * c, orr * (-s)
            else:
                tr, ti = orr * c + oi * s, oi * c - orr * s
        out[k] = (add(er, tr), add(ei, ti))
        out[n // 2 - k] = (sub(er, tr), sub(ti, ei))
    return out


def spots():
    return lax.axis_index("section"), lax.axis_index("z"), lax.axis_index("mate")


def spectrum_kernel(mask_ref, wave_ref, turn_ref, dft_ref, *refs):
    outs, (mid, bins, white, marks) = refs[:-4], refs[-4:]
    lane_at = lax.broadcasted_iota(jnp.int32, (LS, 128), 1)
    row_at = lax.broadcasted_iota(jnp.int32, (LS, 128), 0)

    def station(i, carry):
        xs = [wave_ref[i, :, 128 * a : 128 * (a + 1)].astype(jnp.float32) for a in range(32)]
        half = real_fft(xs)
        for k in range(32):
            re, im = half[k] if k <= 16 else half[32 - k]
            if k > 16 and im is not None:
                im = -im
            if k:
                cos, sin = turn_ref[0, k : k + 1, :], turn_ref[1, k : k + 1, :]
                if im is None:
                    re, im = re * cos, -(re * sin)
                else:
                    re, im = re * cos + im * sin, im * cos - re * sin
            klo, c = divmod(k, 8)
            rows = pl.ds(pl.multiple_of(c * 64 + i * 8, 8), 8)
            mid[klo, rows, :128] = re
            mid[klo, rows, 128:] = jnp.zeros_like(re) if im is None else im
        mark = jnp.zeros((SEGS, 128), jnp.float32)
        for e in range(SEGS):
            valid = mask_ref[0, i, e].astype(jnp.float32)
            mark = jnp.where(row_at == e, valid, mark)
            carry = jnp.where((row_at == i) & (lane_at == e), valid, carry)
        marks[pl.ds(pl.multiple_of(i * 8, 8), 8), :] = mark
        return carry

    table = lax.fori_loop(0, LS, station, jnp.zeros((LS, 128), jnp.float32))
    dot = functools.partial(jnp.dot, preferred_element_type=jnp.float32)
    bins[...] = jnp.zeros_like(bins)

    def second(klo, carry):
        weights = []
        for part in range(2):
            base = dft_ref[part].astype(jnp.float32)
            sides = [pltpu.roll(base[:, at : at + 128], 32 * klo, 1) for at in (0, 128)]
            weights.append(jnp.concatenate(sides, axis=1).astype(jnp.bfloat16))
        wh, wl = weights
        value = mid[klo]
        high = value.astype(jnp.bfloat16)
        low = (value - high.astype(jnp.float32)).astype(jnp.bfloat16)
        bins[...] += dot(high, wh) + (dot(low, wh) + dot(high, wl))
        return carry

    lax.fori_loop(0, 4, second, 0)
    re, im = bins[:, :128], bins[:, 128:]
    amp = jnp.sqrt(re * re + im * im)
    amps = [amp[64 * c : 64 * (c + 1)] for c in range(8)]
    before, after = [amps[0]], [amps[7]]
    for c in range(1, 8):
        before.append(before[-1] + amps[c])
        after.append(after[-1] + amps[7 - c])
    after = after[::-1]
    total = before[7]
    lane = lax.broadcasted_iota(jnp.int32, (64, 128), 1)
    klo = lane // 32
    m = lane % 32
    turned = [pltpu.roll(total, 32 * d, 1) for d in (1, 2, 3)]
    zero = jnp.zeros_like(total)
    all_klo = total + turned[0] + turned[1] + turned[2]
    lower = upper = zero
    for d in (1, 2, 3):
        lower = lower + jnp.where(klo >= d, turned[d - 1], zero)
        upper = upper + jnp.where(klo + d <= 3, turned[3 - d], zero)
    for c in range(8):
        left = pltpu.roll(after[c] + upper, 1, 1)
        right = pltpu.roll(before[c] + lower, 127, 1)
        smooth = all_klo + jnp.where(m >= 1, left, zero) + jnp.where(m <= 30, right, zero)
        scale = marks[...] / (smooth * (1.0 / 65) + EPSILON)
        rows = slice(64 * c, 64 * (c + 1))
        white[0, rows, :] = re[rows] * scale
        white[1, rows, :] = im[rows] * scale
    mate = spots()[2]
    for r in range(4):
        for h in range(HALVES):
            out = outs[r * HALVES + h]
            first = 64 * (2 * (mate ^ r) + h)
            for seg in range(SEGS):
                at = pl.ds(first + seg, 8, stride=8)
                tile = jnp.concatenate([white[0, at, :], white[1, at, :]], axis=0)
                out[16 * seg : 16 * seg + 16, :] = tile.astype(jnp.bfloat16)
        outs[r * HALVES][128:136, :] = table.astype(jnp.bfloat16)


def rows_of(h):
    return 128 + 8 * (h == 0)


def spectrum(waves, mask):
    shapes = [
        jax.ShapeDtypeStruct((rows_of(h), 128), jnp.bfloat16)
        for _ in range(4)
        for h in range(HALVES)
    ]
    vmem = pl.BlockSpec(memory_space=pltpu.VMEM)
    return pl.pallas_call(
        spectrum_kernel,
        out_shape=shapes,
        in_specs=[pl.BlockSpec(memory_space=pltpu.SMEM)] + [vmem] * 3,
        out_specs=[vmem] * len(shapes),
        scratch_shapes=[
            pltpu.VMEM((4, 512, 256), jnp.float32),
            pltpu.VMEM((512, 256), jnp.float32),
            pltpu.VMEM((2, 512, 128), jnp.float32),
            pltpu.VMEM((64, 128), jnp.float32),
        ],
        name="spectrum",
    )(mask, waves, jnp.asarray(twiddles()), jnp.asarray(second_dft()))


def correlate_kernel(h, decay_ref, *refs):
    last = h == HALVES - 1
    refs = list(refs)
    take = lambda n: [refs.pop(0) for _ in range(n)]
    pairs, planes = take(4), take(8)
    (table_hbm,) = take(1)
    before = take(2) if h else None
    outs = take(1) if last else take(2)
    held, cross, inverse, total, table, sem = take(6)
    _, z, mate = spots()
    fetch = pltpu.make_async_copy(table_hbm.at[2 * mate + h], table, sem)
    fetch.start()
    for dz in range(8):
        for r in range(4):
            held[4 * dz + r] = planes[dz][r].astype(jnp.float32)

    def block_of(q, k):
        p = pairs[0][0, k]
        for r in range(1, 4):
            p = jnp.where((q ^ mate) == r, pairs[r][0, k], p)
        dz = ((p // 4) - z + 8) % 8
        return 4 * dz + ((p % 4) ^ mate)

    def out_rows(i, q, k):
        return pl.ds(pl.multiple_of(i * 128 + q * 32 + k * 8, 8), 8)

    if h:
        inverse[...] = before[1][...]
    else:

        def per_count(step, carry):
            q, k = step // PB, step % PB
            there = held[block_of(q, k), 128:136, :]
            for i in range(LS):
                here = held[q ^ mate, 128 + i : 129 + i, :]
                inverse[out_rows(i, q, k), :] = here * there
            return carry

        lax.fori_loop(0, 4 * PB, per_count, 0)
        ones = jnp.ones((128, 128), jnp.bfloat16)
        count = jnp.dot(
            inverse[...].astype(jnp.bfloat16), ones, preferred_element_type=jnp.float32
        )
        inverse[...] = 1.0 / jnp.maximum(count, 1.0)

    def per_pair(step, carry):
        q, k = step // PB, step % PB
        theirs, mine = block_of(q, k), q ^ mate
        there = [held[theirs, 8 * e : 8 * e + 8, :] for e in range(2 * SEGS)]
        for i in range(LS):
            real, imag = None, None
            for e in range(SEGS):
                pr, pi = there[2 * e], there[2 * e + 1]
                at = 16 * e + i
                mr = jnp.broadcast_to(held[mine, at : at + 1, :], (8, 128))
                mi = jnp.broadcast_to(held[mine, at + 8 : at + 9, :], (8, 128))
                real = add(real, mr * pr)
                real = add(real, mi * pi)
                imag = add(imag, mr * pi)
                imag = sub(imag, mi * pr)
            at = out_rows(i, q, k)
            part = inverse[at, :]
            cross[at, :128] = real * part
            cross[at, 128:] = imag * part
        return carry

    lax.fori_loop(0, 4 * PB, per_pair, 0)
    fetch.wait()

    def per_rows(step, carry):
        at = pl.ds(pl.multiple_of(step * 256, 256), 256)
        spectra = cross[at, :].astype(jnp.bfloat16)
        part = jnp.dot(spectra, table[...], preferred_element_type=jnp.float32)
        total[at, :] = part + before[0][at, :] if h else part
        return carry

    lax.fori_loop(0, 4, per_rows, 0)
    if not last:
        outs[0][...] = total[...]
        outs[1][...] = inverse[...]
        return
    decay = jnp.full((8, 128), decay_ref[0], jnp.float32)
    high = decay.astype(jnp.bfloat16)
    low = (decay - high.astype(jnp.float32)).astype(jnp.bfloat16)
    both = jnp.where(row_of(8) < 4, high.astype(jnp.float32), low.astype(jnp.float32))

    def per_part(n, carry):
        at = pl.ds(pl.multiple_of(n * 32, 32), 32)
        for g in range(3):
            value = total[at, 128 * g : 128 * (g + 1)]
            outs[0][n, 32 * g : 32 * (g + 1), :] = value.astype(jnp.bfloat16)
        outs[0][n, 96:104, :] = both.astype(jnp.bfloat16)
        return carry

    lax.fori_loop(0, 32, per_part, 0)


def row_of(n):
    return lax.broadcasted_iota(jnp.int32, (n, 128), 0)


def correlate(h, decay, pairs, planes, table, carried):
    last = h == HALVES - 1
    smem, vmem = pl.BlockSpec(memory_space=pltpu.SMEM), pl.BlockSpec(memory_space=pltpu.VMEM)
    if last:
        shapes = [jax.ShapeDtypeStruct((32, 104, 128), jnp.bfloat16)]
    else:
        shapes = [
            jax.ShapeDtypeStruct((1024, LAGS), jnp.float32),
            jax.ShapeDtypeStruct((1024, 128), jnp.float32),
        ]
    return pl.pallas_call(
        functools.partial(correlate_kernel, h),
        out_shape=shapes,
        in_specs=[smem] * 5
        + [vmem] * 8
        + [pl.BlockSpec(memory_space=pl.ANY)]
        + [vmem] * len(carried),
        out_specs=[vmem] * len(shapes),
        scratch_shapes=[
            pltpu.VMEM((32, rows_of(h), 128), jnp.float32),
            pltpu.VMEM((1024, 256), jnp.float32),
            pltpu.VMEM((1024, 128), jnp.float32),
            pltpu.VMEM((1024, LAGS), jnp.float32),
            pltpu.VMEM((256, LAGS), jnp.bfloat16),
            pltpu.SemaphoreType.DMA,
        ],
    )(decay, *pairs, *planes, table, *carried)


def scan_kernel(parts, out):
    state = [jnp.zeros((32, 128), jnp.float32)] * 3
    for w in range(8):
        marks = parts[4 * w, 96:104, :].astype(jnp.float32)
        decay = marks[:1] + marks[4:5]
        for g in range(3):
            at = slice(32 * g, 32 * (g + 1))
            lagged = sum(parts[4 * w + q, at, :].astype(jnp.float32) for q in range(4))
            state[g] = decay * state[g] + lagged
            out[w, :, 128 * g : 128 * (g + 1)] = state[g].astype(jnp.bfloat16)


def scan_windows(parts):
    vmem = pl.BlockSpec(memory_space=pltpu.VMEM)
    return pl.pallas_call(
        scan_kernel,
        out_shape=jax.ShapeDtypeStruct((8, 32, LAGS), jnp.bfloat16),
        in_specs=[vmem],
        out_specs=vmem,
        name="scan",
    )(parts)


def across(value, r):
    return lax.ppermute(value, "mate", [(d, d ^ r) for d in range(4)])


def along(value, step):
    return lax.ppermute(value, "z", [(d, (d + step) % 8) for d in range(8)])


def body(waveforms, segment_mask, pair_blocks, window_decay):
    pairs = [pair_blocks] + [across(pair_blocks, r) for r in (1, 2, 3)]
    flat = spectrum(waveforms[0], segment_mask)
    table = jnp.asarray(lag_table())
    carried = []
    for h in range(HALVES):
        mine = [flat[r * HALVES + h] for r in range(4)]
        plane = jnp.stack([mine[0]] + [across(mine[r], r) for r in (1, 2, 3)])
        planes = [plane] + [None] * 7
        ahead = back = plane
        for step in range(1, 5):
            if step < 4 or h % 2 == 0:
                ahead = along(ahead, 1)
                planes[8 - step] = ahead
            if step < 4 or h % 2 == 1:
                back = along(back, -1)
                planes[step] = back
        carried = correlate(h, window_decay, pairs, planes, table, carried)
    parts = lax.all_to_all(carried[0], ("section", "mate"), 0, 0)
    states = lax.all_to_all(scan_windows(parts), "section", 0, 0)
    return states[None]


def solution(mesh):
    split = Mesh(mesh.devices.reshape(8, 8, 4), ("section", "z", "mate"))
    sta = ("z", "mate")
    placed = (P("section", sta, None, None), P("section", sta, None), P(sta, None), P("section"))

    return jax.shard_map(
        body,
        mesh=split,
        in_specs=placed,
        out_specs=P("section", sta, None, None),
        check_vma=False,
    )
```

time: 118 us -> 101 us (0.86)
  blocking collectives: 0 us -> 33 us
  waiting for transfers between devices: 38.4 us -> 14.8 us
  starting transfers between devices: 46.8 us -> 27.6 us
  Pallas kernels: 23.4 us -> 18.6 us
  local copies, waits for them, and re-layouts: 5.82 us -> 2.57 us
    all_to_all x0 -> x2, blocking collectives: none -> 33 us  [the longest x1 20.7 us: body(): parts = lax.all_to_all(carried[0], ('section', 'mate'), 0, 0)]
    ppermute x36 -> x23, waiting for transfers between devices: 38.4 us -> 14.8 us  [the longest x9 8.77 us: across(): return lax.ppermute(value, 'mate', [(d, d ^ r) for d in range(4)])]
    ppermute x36 -> x23, starting transfers between devices: 46.8 us -> 27.6 us  [the longest x14 23.5 us: along(): return lax.ppermute(value, 'z', [(d, (d + step) % 8) for d in range(8)])]
    pallas_call x5 -> x1, Pallas kernels: 9.35 us -> 1.97 us  [scan_windows(): pl.pallas_call(scan_kernel, out_shape=jax.ShapeDtypeStruct((8, 32, LAGS),...]
    unnamed x74 -> x39, local copies, waits for them, and re-layouts: 5.82 us -> 2.57 us
    pallas_call x2, Pallas kernels: 9.24 us -> 11.8 us  [correlate(): pl.pallas_call(functools.partial(correlate_kernel, h), out_shape=shapes,...]
  transfers between devices with their start and end apart: 36 -> 23, of which waited for: 18 -> 10; matrix products, arithmetic and copies ran while one was open for 0% -> 2% of each run, Pallas kernels for 9% -> 6%
where the time goes in v1:
time: 101 us; the launch traced here: 99 us
  blocking collectives  33 us (33%)
  starting transfers between devices  27.6 us (27%)
  Pallas kernels  18.6 us (18%)
  waiting for transfers between devices  14.8 us (15%)
  local copies, waits for them, and re-layouts  2.57 us (3%)
  other arithmetic  1.56 us (2%)
    ppermute x14, starting transfers between devices, along(): return lax.ppermute(value, 'z', [(d, (d + step) % 8) for d in range(8)])  23.5 us
    all_to_all x1, blocking collectives, body(): parts = lax.all_to_all(carried[0], ('section', 'mate'), 0, 0)  20.7 us
    all_to_all x1, blocking collectives, body(): states = lax.all_to_all(scan_windows(parts), 'section', 0, 0)  12.2 us
    pallas_call x2, Pallas kernels, correlate(): pl.pallas_call(functools.partial(correlate_kernel, h), out_shape=shapes,...  11.8 us
    ppermute x9, waiting for transfers between devices, across(): return lax.ppermute(value, 'mate', [(d, d ^ r) for d in range(4)])  8.77 us
    ppermute x14, waiting for transfers between devices, along(): return lax.ppermute(value, 'z', [(d, (d + step) % 8) for d in range(8)])  6.06 us
    pallas_call x1, Pallas kernels, spectrum(): pl.pallas_call(spectrum_kernel, out_shape=shapes, in_specs=[pl.BlockSpec(...  4.84 us
    ppermute x9, starting transfers between devices, across(): return lax.ppermute(value, 'mate', [(d, d ^ r) for d in range(4)])  4.06 us
  transfers between devices with their start and end apart: 23, of which 10 were waited for; matrix products, arithmetic and copies ran while one was open for 2% of the time, Pallas kernels for 6%

profile of v1, /device:TPU:6, one launch (start us, length us, event | category | flops | bytes accessed | tf_op | source)
XLA Modules:
  0.0 99.0 jit_solution(9879808124020837030)
XLA Ops:
  0.0 4.8 %spectrum.1 = (bf16[136,128]{1,0:T(8,128)(2,1)}, bf16[128,128]{1,0:T(8,128)(2,1)}, bf16[136,128]{1,0:T(8,128)(2,1)}, bf16[128,128]{1,0:T(8,128)(2,1)}, bf16[136,...) custom-call(s32[1,8,8]{2,1,0:T(8,128)} %mask_ref.1, ...), custom_call_target="tpu_custom_call" | custom-call | tf_op jit(solution)/shard_map/spectrum/pallas_call | solution.py:198
  4.8 0.1 collective-permute-start.13
  4.9 1.7 %collective-permute-start.14 = (bf16[136,128]{1,0:T(8,128)(2,1)}, bf16[136,128]{1,0:T(8,128)(2,1)S(1)}, u32[]{:S(2)}, u32[]{:S(2)}) collective-permute-start(bf16[136,128]{1,0:T(8,128)(2,1)} %get-tuple-element.21), channel_id=1, source_target_pairs={{0,2},{1,3},{2,0},{3,1},{4,6},{5,7},{6,4},{7,5},{8,10},{9,11},{10,... | collective-permute-start | bytes 104456 | tf_op jit(solution)/shard_map/ppermute | solution.py:367
  6.6 0.2 collective-permute-start.15
  6.8 0.4 collective-permute-start.3
  7.1 1.6 %collective-permute-start.4 = (bf16[128,128]{1,0:T(8,128)(2,1)}, bf16[128,128]{1,0:T(8,128)(2,1)S(1)}, u32[]{:S(2)}, u32[]{:S(2)}) collective-permute-start(bf16[128,128]{1,0:T(8,128)(2,1)} %get-tuple-element.17), channel_id=1, source_target_pairs={{0,2},{1,3},{2,0},{3,1},{4,6},{5,7},{6,4},{7,5},{8,10},{9,11},{10,... | collective-permute-start | bytes 98312 | tf_op jit(solution)/shard_map/ppermute | solution.py:367
  8.7 0.0 collective-permute-done.13
  8.7 0.0 collective-permute-start.5
  8.7 0.4 collective-permute-done.14
  9.1 1.1 %collective-permute-done.15 = bf16[136,128]{1,0:T(8,128)(2,1)S(1)} collective-permute-done((bf16[136,128]{1,0:T(8,128)(2,1)}, bf16[136,128]{1,0:T(8,128)(2,1)S(1)}, u32[]{:S(2)}, u32[]{:S(2)}) %collective-permute-start.15) | collective-permute-done | bytes 34848 | tf_op jit(solution)/shard_map/ppermute | solution.py:367
  10.2 0.8 pad_maximum_fusion.refs_4_
  11.0 0.0 copy-start
  11.0 2.0 %collective-permute-start.19 = (bf16[4,136,128]{2,1,0:T(8,128)(2,1)S(1)}, bf16[4,136,128]{2,1,0:T(8,128)(2,1)S(1)}, u32[]{:S(2)}, u32[]{:S(2)}) collective-permute-start(bf16[4,136,128]{2,1,0:T(8,128)(2,1)S(1)} %pad_maximum_fusion.refs_4_), channel_id=1, source_target_pairs={{0,4},{4,8},{8,12},{12,16},{16,20},{20,24},{24,28},{28,0},{1,5},{5... | collective-permute-start | bytes 417800 | tf_op jit(solution)/shard_map/ppermute | solution.py:371
  13.0 0.0 collective-permute-done.3
  13.0 0.0 collective-permute-done.4
  13.0 0.0 collective-permute-done.5
  13.0 0.8 pad_maximum_fusion.1.refs_4_
  13.8 5.5 %collective-permute-start.6 = (bf16[4,128,128]{2,1,0:T(8,128)(2,1)S(1)}, bf16[4,128,128]{2,1,0:T(8,128)(2,1)S(1)}, u32[]{:S(2)}, u32[]{:S(2)}) collective-permute-start(bf16[4,128,128]{2,1,0:T(8,128)(2,1)S(1)} %pad_maximum_fusion.1.refs_4_), channel_id=1, source_target_pairs={{0,28},{4,0},{8,4},{12,8},{16,12},{20,16},{24,20},{28,24},{1,29},{... | collective-permute-start | bytes 393224 | tf_op jit(solution)/shard_map/ppermute | solution.py:371
  19.3 1.0 %collective-permute-start.16 = (bf16[4,136,128]{2,1,0:T(8,128)(2,1)S(1)}, bf16[4,136,128]{2,1,0:T(8,128)(2,1)S(1)}, u32[]{:S(2)}, u32[]{:S(2)}) collective-permute-start(bf16[4,136,128]{2,1,0:T(8,128)(2,1)S(1)} %pad_maximum_fusion.refs_4_), channel_id=1, source_target_pairs={{0,28},{4,0},{8,4},{12,8},{16,12},{20,16},{24,20},{28,24},{1,29},{... | collective-permute-start | bytes 417800 | tf_op jit(solution)/shard_map/ppermute | solution.py:371
  20.3 0.9 collective-permute-done.19.refs_11_
  21.2 0.1 collective-permute-start.20
  21.3 0.1 collective-permute-start.10
  21.4 1.8 %collective-permute-done.6.refs_5_ = bf16[4,128,128]{2,1,0:T(8,128)(2,1)S(1)} collective-permute-done((bf16[4,128,128]{2,1,0:T(8,128)(2,1)S(1)}, bf16[4,128,128]{2,1,0:T(8,128)(2,1)S(1)}, u32[]{:S(2)}, u32[]{:S(2)}) %collective-permute-start.6) | collective-permute-done | bytes 131104 | tf_op jit(solution)/shard_map/ppermute | solution.py:371
  23.2 3.7 %collective-permute-start.7 = (bf16[4,128,128]{2,1,0:T(8,128)(2,1)S(1)}, bf16[4,128,128]{2,1,0:T(8,128)(2,1)S(1)}, u32[]{:S(2)}, u32[]{:S(2)}) collective-permute-start(bf16[4,128,128]{2,1,0:T(8,128)(2,1)S(1)} %collective-permute-done.6.refs_5_), channel_id=1, source_target_pairs={{0,28},{4,0},{8,4},{12,8},{16,12},{20,16},{24,20},{28,24},{1,29},{... | collective-permute-start | bytes 393224 | tf_op jit(solution)/shard_map/ppermute | solution.py:371
  26.9 0.0 collective-permute-done.16.refs_5_
  26.9 2.1 %collective-permute-start.17 = (bf16[4,136,128]{2,1,0:T(8,128)(2,1)S(1)}, bf16[4,136,128]{2,1,0:T(8,128)(2,1)S(1)}, u32[]{:S(2)}, u32[]{:S(2)}) collective-permute-start(bf16[4,136,128]{2,1,0:T(8,128)(2,1)S(1)} %collective-permute-done.16.refs_5_), channel_id=1, source_target_pairs={{0,28},{4,0},{8,4},{12,8},{16,12},{20,16},{24,20},{28,24},{1,29},{... | collective-permute-start | bytes 417800 | tf_op jit(solution)/shard_map/ppermute | solution.py:371
  29.0 0.0 collective-permute-done.20.refs_10_
  29.0 0.0 collective-permute-start.21
  29.0 1.6 %collective-permute-done.10.refs_11_ = bf16[4,128,128]{2,1,0:T(8,128)(2,1)S(1)} collective-permute-done((bf16[4,128,128]{2,1,0:T(8,128)(2,1)S(1)}, bf16[4,128,128]{2,1,0:T(8,128)(2,1)S(1)}, u32[]{:S(2)}, u32[]{:S(2)}) %collective-permute-start.10) | collective-permute-done | bytes 131104 | tf_op jit(solution)/shard_map/ppermute | solution.py:371
  30.7 0.0 collective-permute-start.11
  30.7 0.0 collective-permute-done.7.refs_6_
  30.7 3.3 %collective-permute-start.8 = (bf16[4,128,128]{2,1,0:T(8,128)(2,1)S(1)}, bf16[4,128,128]{2,1,0:T(8,128)(2,1)S(1)}, u32[]{:S(2)}, u32[]{:S(2)}) collective-permute-start(bf16[4,128,128]{2,1,0:T(8,128)(2,1)S(1)} %collective-permute-done.7.refs_6_), channel_id=1, source_target_pairs={{0,28},{4,0},{8,4},{12,8},{16,12},{20,16},{24,20},{28,24},{1,29},{... | collective-permute-start | bytes 393224 | tf_op jit(solution)/shard_map/ppermute | solution.py:371
  34.0 0.0 collective-permute-done.17.refs_6_
  34.0 2.0 %collective-permute-start.18 = (bf16[4,136,128]{2,1,0:T(8,128)(2,1)S(1)}, bf16[4,136,128]{2,1,0:T(8,128)(2,1)S(1)}, u32[]{:S(2)}, u32[]{:S(2)}) collective-permute-start(bf16[4,136,128]{2,1,0:T(8,128)(2,1)S(1)} %collective-permute-done.17.refs_6_), channel_id=1, source_target_pairs={{0,28},{4,0},{8,4},{12,8},{16,12},{20,16},{24,20},{28,24},{1,29},{... | collective-permute-start | bytes 417800 | tf_op jit(solution)/shard_map/ppermute | solution.py:371
  36.0 0.3 collective-permute-done.21.refs_9_
  36.4 0.0 collective-permute-start.22
  36.4 1.4 %collective-permute-done.11.refs_10_ = bf16[4,128,128]{2,1,0:T(8,128)(2,1)S(1)} collective-permute-done((bf16[4,128,128]{2,1,0:T(8,128)(2,1)S(1)}, bf16[4,128,128]{2,1,0:T(8,128)(2,1)S(1)}, u32[]{:S(2)}, u32[]{:S(2)}) %collective-permute-start.11) | collective-permute-done | bytes 131104 | tf_op jit(solution)/shard_map/ppermute | solution.py:371
  37.8 0.0 collective-permute-start.12
  37.8 0.0 collective-permute-done.8.refs_7_
  37.8 3.6 %collective-permute-start.9 = (bf16[4,128,128]{2,1,0:T(8,128)(2,1)S(1)}, bf16[4,128,128]{2,1,0:T(8,128)(2,1)S(1)}, u32[]{:S(2)}, u32[]{:S(2)}) collective-permute-start(bf16[4,128,128]{2,1,0:T(8,128)(2,1)S(1)} %collective-permute-done.8.refs_7_), channel_id=1, source_target_pairs={{0,28},{4,0},{8,4},{12,8},{16,12},{20,16},{24,20},{28,24},{1,29},{... | collective-permute-start | bytes 393224 | tf_op jit(solution)/shard_map/ppermute | solution.py:371
  41.5 0.0 collective-permute-start
  42.1 0.6 collective-permute-done.refs_1_
  42.8 0.2 collective-permute-start.1
  42.9 3.5 %collective-permute-done.1.refs_2_ = s32[1,4]{1,0:T(1,128)S(1)} collective-permute-done((s32[1,4]{1,0:T(1,128)}, s32[1,4]{1,0:T(1,128)S(1)}, u32[]{:S(2)}, u32[]{:S(2)}) %collective-permute-start.1) | collective-permute-done | bytes 48 | tf_op jit(solution)/shard_map/ppermute | solution.py:367
  46.5 0.0 collective-permute-start.2
  46.5 3.1 %collective-permute-done.2.refs_3_ = s32[1,4]{1,0:T(1,128)S(1)} collective-permute-done((s32[1,4]{1,0:T(1,128)}, s32[1,4]{1,0:T(1,128)S(1)}, u32[]{:S(2)}, u32[]{:S(2)}) %collective-permute-start.2) | collective-permute-done | bytes 48 | tf_op jit(solution)/shard_map/ppermute | solution.py:367
  49.6 0.0 collective-permute-done.18.refs_7_
  49.6 0.0 collective-permute-done.22.refs_8_
  49.6 0.0 copy-done
  49.6 0.0 copy-done.2
  49.7 0.4 copy-done.18
  50.1 0.1 copy-done.7
  50.2 0.7 copy-done.8
  50.9 6.0 %shard_map.73 = (f32[1024,384]{1,0:T(8,128)}, f32[1024,128]{1,0:T(8,128)}) custom-call(f32[1]{0:T(128)S(6)} %copy.9.decay_ref, s32[1,4]{1,0:T(1,128)} %refs_0_.3, s32[1,4]{1,0:T(1,128)} %copy-done.16, s32[1,4]{1,0:T(1,128)} %copy-done.17, s32[1,4]{1,0:T(1,128)} %copy-done.18, bf16[4,136,128]{2,1,0:T(8,128)(2,1)} %copy-done, bf16[4,136,128]{2,1,0:T(8,128)(2,1)} %copy-done.3, ...), custom_call_target="tpu_custom_call" | custom-call | tf_op jit(solution)/shard_map/pallas_call | solution.py:324
  56.9 0.0 collective-permute-done.12.refs_9_
  57.0 0.0 collective-permute-done.9.refs_8_
  57.0 0.0 copy-start.15
  57.0 0.6 copy-done.14
  57.6 0.0 copy-done.15
  57.6 5.8 %shard_map.74 = bf16[32,104,128]{2,1,0:T(8,128)(2,1)} custom-call(f32[1]{0:T(128)S(6)} %copy.9.decay_ref, s32[1,4]{1,0:T(1,128)} %refs_0_.3, s32[1,4]{1,0:T(1,128)} %copy-done.16, s32[1,4]{1,0:T(1,128)} %copy-done.17, s32[1,4]{1,0:T(1,128)} %copy-done.18, bf16[4,128,128]{2,1,0:T(8,128)(2,1)} %copy-done.1, bf16[4,128,128]{2,1,0:T(8,128)(2,1)} %copy-done.9, ...), custom_call_target="tpu_custom_call" | custom-call | tf_op jit(solution)/shard_map/pallas_call | solution.py:324
  63.4 20.7 %all_to_all.10.parts = bf16[32,104,128]{2,1,0:T(8,128)(2,1)} all-to-all(bf16[32,104,128]{2,1,0:T(8,128)(2,1)} %shard_map.74), channel_id=1, replica_groups=mesh['section'=8,'z'=8,'mate'=4] {'section','mate'}, dimensions={0} | all-to-all | bytes 1703936 | tf_op jit(solution)/shard_map/all_to_all | solution.py:392
  84.1 2.0 %scan.1 = bf16[8,32,384]{2,1,0:T(8,128)(2,1)} custom-call(bf16[32,104,128]{2,1,0:T(8,128)(2,1)} %all_to_all.10.parts), custom_call_target="tpu_custom_call" | custom-call | tf_op jit(solution)/shard_map/scan/pallas_call | solution.py:357
  86.1 12.2 %all_to_all.11 = bf16[8,32,384]{2,1,0:T(8,128)(2,1)S(1)} all-to-all(bf16[8,32,384]{2,1,0:T(8,128)(2,1)} %scan.1), channel_id=1, replica_groups=mesh['section'=8,'z'=8,'mate'=4] {'section'}, dimensions={0} | all-to-all | bytes 393216 | tf_op jit(solution)/shard_map/all_to_all | solution.py:393
  98.4 0.7 copy.10
  (29 shorter events, 0.1 us)
Async XLA Ops:
  4.8 3.9 %collective-permute-start.13 = (bf16[136,128]{1,0:T(8,128)(2,1)}, bf16[136,128]{1,0:T(8,128)(2,1)S(1)}, u32[]{:S(2)}, u32[]{:S(2)}) collective-permute-start(bf16[136,128]{1,0:T(8,128)(2,1)} %get-tuple-element.20), channel_id=1, source_target_pairs={{0,1},{1,0},{2,3},{3,2},{4,5},{5,4},{6,7},{7,6},{8,9},{9,8},{10,11... | collective-permute-start | bytes 104456 | tf_op jit(solution)/shard_map/ppermute | solution.py:367
  4.9 4.2 %collective-permute-start.14 = (bf16[136,128]{1,0:T(8,128)(2,1)}, bf16[136,128]{1,0:T(8,128)(2,1)S(1)}, u32[]{:S(2)}, u32[]{:S(2)}) collective-permute-start(bf16[136,128]{1,0:T(8,128)(2,1)} %get-tuple-element.21), channel_id=1, source_target_pairs={{0,2},{1,3},{2,0},{3,1},{4,6},{5,7},{6,4},{7,5},{8,10},{9,11},{10,... | collective-permute-start | bytes 104456 | tf_op jit(solution)/shard_map/ppermute | solution.py:367
  6.6 3.6 %collective-permute-start.15 = (bf16[136,128]{1,0:T(8,128)(2,1)}, bf16[136,128]{1,0:T(8,128)(2,1)S(1)}, u32[]{:S(2)}, u32[]{:S(2)}) collective-permute-start(bf16[136,128]{1,0:T(8,128)(2,1)} %get-tuple-element.22), channel_id=1, source_target_pairs={{0,3},{1,2},{2,1},{3,0},{4,7},{5,6},{6,5},{7,4},{8,11},{9,10},{10,... | collective-permute-start | bytes 104456 | tf_op jit(solution)/shard_map/ppermute | solution.py:367
  6.8 6.2 %collective-permute-start.3 = (bf16[128,128]{1,0:T(8,128)(2,1)}, bf16[128,128]{1,0:T(8,128)(2,1)S(1)}, u32[]{:S(2)}, u32[]{:S(2)}) collective-permute-start(bf16[128,128]{1,0:T(8,128)(2,1)} %get-tuple-element.16), channel_id=1, source_target_pairs={{0,1},{1,0},{2,3},{3,2},{4,5},{5,4},{6,7},{7,6},{8,9},{9,8},{10,11... | collective-permute-start | bytes 98312 | tf_op jit(solution)/shard_map/ppermute | solution.py:367
  7.1 5.9 %collective-permute-start.4 = (bf16[128,128]{1,0:T(8,128)(2,1)}, bf16[128,128]{1,0:T(8,128)(2,1)S(1)}, u32[]{:S(2)}, u32[]{:S(2)}) collective-permute-start(bf16[128,128]{1,0:T(8,128)(2,1)} %get-tuple-element.17), channel_id=1, source_target_pairs={{0,2},{1,3},{2,0},{3,1},{4,6},{5,7},{6,4},{7,5},{8,10},{9,11},{10,... | collective-permute-start | bytes 98312 | tf_op jit(solution)/shard_map/ppermute | solution.py:367
  8.7 4.3 %collective-permute-start.5 = (bf16[128,128]{1,0:T(8,128)(2,1)}, bf16[128,128]{1,0:T(8,128)(2,1)S(1)}, u32[]{:S(2)}, u32[]{:S(2)}) collective-permute-start(bf16[128,128]{1,0:T(8,128)(2,1)} %get-tuple-element.18), channel_id=1, source_target_pairs={{0,3},{1,2},{2,1},{3,0},{4,7},{5,6},{6,5},{7,4},{8,11},{9,10},{10,... | collective-permute-start | bytes 98312 | tf_op jit(solution)/shard_map/ppermute | solution.py:367
  11.0 38.6 %copy-start = (bf16[4,136,128]{2,1,0:T(8,128)(2,1)}, bf16[4,136,128]{2,1,0:T(8,128)(2,1)S(1)}, u32[]{:S(2)}) copy-start(bf16[4,136,128]{2,1,0:T(8,128)(2,1)S(1)} %pad_maximum_fusion.refs_4_) | copy-start | bytes 417796
  11.0 10.2 %collective-permute-start.19 = (bf16[4,136,128]{2,1,0:T(8,128)(2,1)S(1)}, bf16[4,136,128]{2,1,0:T(8,128)(2,1)S(1)}, u32[]{:S(2)}, u32[]{:S(2)}) collective-permute-start(bf16[4,136,128]{2,1,0:T(8,128)(2,1)S(1)} %pad_maximum_fusion.refs_4_), channel_id=1, source_target_pairs={{0,4},{4,8},{8,12},{12,16},{16,20},{20,24},{24,28},{28,0},{1,5},{5... | collective-permute-start | bytes 417800 | tf_op jit(solution)/shard_map/ppermute | solution.py:371
  13.8 43.2 %copy-start.1 = (bf16[4,128,128]{2,1,0:T(8,128)(2,1)}, bf16[4,128,128]{2,1,0:T(8,128)(2,1)S(1)}, u32[]{:S(2)}) copy-start(bf16[4,128,128]{2,1,0:T(8,128)(2,1)S(1)} %pad_maximum_fusion.1.refs_4_) | copy-start | bytes 393220
  13.8 9.4 %collective-permute-start.6 = (bf16[4,128,128]{2,1,0:T(8,128)(2,1)S(1)}, bf16[4,128,128]{2,1,0:T(8,128)(2,1)S(1)}, u32[]{:S(2)}, u32[]{:S(2)}) collective-permute-start(bf16[4,128,128]{2,1,0:T(8,128)(2,1)S(1)} %pad_maximum_fusion.1.refs_4_), channel_id=1, source_target_pairs={{0,28},{4,0},{8,4},{12,8},{16,12},{20,16},{24,20},{28,24},{1,29},{... | collective-permute-start | bytes 393224 | tf_op jit(solution)/shard_map/ppermute | solution.py:371
  19.3 7.6 %collective-permute-start.16 = (bf16[4,136,128]{2,1,0:T(8,128)(2,1)S(1)}, bf16[4,136,128]{2,1,0:T(8,128)(2,1)S(1)}, u32[]{:S(2)}, u32[]{:S(2)}) collective-permute-start(bf16[4,136,128]{2,1,0:T(8,128)(2,1)S(1)} %pad_maximum_fusion.refs_4_), channel_id=1, source_target_pairs={{0,28},{4,0},{8,4},{12,8},{16,12},{20,16},{24,20},{28,24},{1,29},{... | collective-permute-start | bytes 417800 | tf_op jit(solution)/shard_map/ppermute | solution.py:371
  21.2 28.4 %copy-start.2 = (bf16[4,136,128]{2,1,0:T(8,128)(2,1)}, bf16[4,136,128]{2,1,0:T(8,128)(2,1)S(1)}, u32[]{:S(2)}) copy-start(bf16[4,136,128]{2,1,0:T(8,128)(2,1)S(1)} %collective-permute-done.19.refs_11_) | copy-start | bytes 417796
  21.2 7.8 %collective-permute-start.20 = (bf16[4,136,128]{2,1,0:T(8,128)(2,1)S(1)}, bf16[4,136,128]{2,1,0:T(8,128)(2,1)S(1)}, u32[]{:S(2)}, u32[]{:S(2)}) collective-permute-start(bf16[4,136,128]{2,1,0:T(8,128)(2,1)S(1)} %collective-permute-done.19.refs_11_), channel_id=1, source_target_pairs={{0,4},{4,8},{8,12},{12,16},{16,20},{20,24},{24,28},{28,0},{1,5},{5... | collective-permute-start | bytes 417800 | tf_op jit(solution)/shard_map/ppermute | solution.py:371
  21.3 9.3 %collective-permute-start.10 = (bf16[4,128,128]{2,1,0:T(8,128)(2,1)S(1)}, bf16[4,128,128]{2,1,0:T(8,128)(2,1)S(1)}, u32[]{:S(2)}, u32[]{:S(2)}) collective-permute-start(bf16[4,128,128]{2,1,0:T(8,128)(2,1)S(1)} %pad_maximum_fusion.1.refs_4_), channel_id=1, source_target_pairs={{0,4},{4,8},{8,12},{12,16},{16,20},{20,24},{24,28},{28,0},{1,5},{5... | collective-permute-start | bytes 393224 | tf_op jit(solution)/shard_map/ppermute | solution.py:371
  23.2 33.8 %copy-start.9 = (bf16[4,128,128]{2,1,0:T(8,128)(2,1)}, bf16[4,128,128]{2,1,0:T(8,128)(2,1)S(1)}, u32[]{:S(2)}) copy-start(bf16[4,128,128]{2,1,0:T(8,128)(2,1)S(1)} %collective-permute-done.6.refs_5_) | copy-start | bytes 393220
  23.2 7.5 %collective-permute-start.7 = (bf16[4,128,128]{2,1,0:T(8,128)(2,1)S(1)}, bf16[4,128,128]{2,1,0:T(8,128)(2,1)S(1)}, u32[]{:S(2)}, u32[]{:S(2)}) collective-permute-start(bf16[4,128,128]{2,1,0:T(8,128)(2,1)S(1)} %collective-permute-done.6.refs_5_), channel_id=1, source_target_pairs={{0,28},{4,0},{8,4},{12,8},{16,12},{20,16},{24,20},{28,24},{1,29},{... | collective-permute-start | bytes 393224 | tf_op jit(solution)/shard_map/ppermute | solution.py:371
  26.9 22.7 %copy-start.3 = (bf16[4,136,128]{2,1,0:T(8,128)(2,1)}, bf16[4,136,128]{2,1,0:T(8,128)(2,1)S(1)}, u32[]{:S(2)}) copy-start(bf16[4,136,128]{2,1,0:T(8,128)(2,1)S(1)} %collective-permute-done.16.refs_5_) | copy-start | bytes 417796
  26.9 7.2 %collective-permute-start.17 = (bf16[4,136,128]{2,1,0:T(8,128)(2,1)S(1)}, bf16[4,136,128]{2,1,0:T(8,128)(2,1)S(1)}, u32[]{:S(2)}, u32[]{:S(2)}) collective-permute-start(bf16[4,136,128]{2,1,0:T(8,128)(2,1)S(1)} %collective-permute-done.16.refs_5_), channel_id=1, source_target_pairs={{0,28},{4,0},{8,4},{12,8},{16,12},{20,16},{24,20},{28,24},{1,29},{... | collective-permute-start | bytes 417800 | tf_op jit(solution)/shard_map/ppermute | solution.py:371
  29.0 20.6 %copy-start.4 = (bf16[4,136,128]{2,1,0:T(8,128)(2,1)}, bf16[4,136,128]{2,1,0:T(8,128)(2,1)S(1)}, u32[]{:S(2)}) copy-start(bf16[4,136,128]{2,1,0:T(8,128)(2,1)S(1)} %collective-permute-done.20.refs_10_) | copy-start | bytes 417796
  29.0 7.4 %collective-permute-start.21 = (bf16[4,136,128]{2,1,0:T(8,128)(2,1)S(1)}, bf16[4,136,128]{2,1,0:T(8,128)(2,1)S(1)}, u32[]{:S(2)}, u32[]{:S(2)}) collective-permute-start(bf16[4,136,128]{2,1,0:T(8,128)(2,1)S(1)} %collective-permute-done.20.refs_10_), channel_id=1, source_target_pairs={{0,4},{4,8},{8,12},{12,16},{16,20},{20,24},{24,28},{28,0},{1,5},{5... | collective-permute-start | bytes 417800 | tf_op jit(solution)/shard_map/ppermute | solution.py:371
  30.7 26.3 %copy-start.10 = (bf16[4,128,128]{2,1,0:T(8,128)(2,1)}, bf16[4,128,128]{2,1,0:T(8,128)(2,1)S(1)}, u32[]{:S(2)}) copy-start(bf16[4,128,128]{2,1,0:T(8,128)(2,1)S(1)} %collective-permute-done.10.refs_11_) | copy-start | bytes 393220
  30.7 7.1 %collective-permute-start.11 = (bf16[4,128,128]{2,1,0:T(8,128)(2,1)S(1)}, bf16[4,128,128]{2,1,0:T(8,128)(2,1)S(1)}, u32[]{:S(2)}, u32[]{:S(2)}) collective-permute-start(bf16[4,128,128]{2,1,0:T(8,128)(2,1)S(1)} %collective-permute-done.10.refs_11_), channel_id=1, source_target_pairs={{0,4},{4,8},{8,12},{12,16},{16,20},{20,24},{24,28},{28,0},{1,5},{5... | collective-permute-start | bytes 393224 | tf_op jit(solution)/shard_map/ppermute | solution.py:371
  30.7 26.3 %copy-start.11 = (bf16[4,128,128]{2,1,0:T(8,128)(2,1)}, bf16[4,128,128]{2,1,0:T(8,128)(2,1)S(1)}, u32[]{:S(2)}) copy-start(bf16[4,128,128]{2,1,0:T(8,128)(2,1)S(1)} %collective-permute-done.7.refs_6_) | copy-start | bytes 393220
  30.7 7.1 %collective-permute-start.8 = (bf16[4,128,128]{2,1,0:T(8,128)(2,1)S(1)}, bf16[4,128,128]{2,1,0:T(8,128)(2,1)S(1)}, u32[]{:S(2)}, u32[]{:S(2)}) collective-permute-start(bf16[4,128,128]{2,1,0:T(8,128)(2,1)S(1)} %collective-permute-done.7.refs_6_), channel_id=1, source_target_pairs={{0,28},{4,0},{8,4},{12,8},{16,12},{20,16},{24,20},{28,24},{1,29},{... | collective-permute-start | bytes 393224 | tf_op jit(solution)/shard_map/ppermute | solution.py:371
  34.0 15.6 %copy-start.5 = (bf16[4,136,128]{2,1,0:T(8,128)(2,1)}, bf16[4,136,128]{2,1,0:T(8,128)(2,1)S(1)}, u32[]{:S(2)}) copy-start(bf16[4,136,128]{2,1,0:T(8,128)(2,1)S(1)} %collective-permute-done.17.refs_6_) | copy-start | bytes 417796
  34.0 15.5 %collective-permute-start.18 = (bf16[4,136,128]{2,1,0:T(8,128)(2,1)S(1)}, bf16[4,136,128]{2,1,0:T(8,128)(2,1)S(1)}, u32[]{:S(2)}, u32[]{:S(2)}) collective-permute-start(bf16[4,136,128]{2,1,0:T(8,128)(2,1)S(1)} %collective-permute-done.17.refs_6_), channel_id=1, source_target_pairs={{0,28},{4,0},{8,4},{12,8},{16,12},{20,16},{24,20},{28,24},{1,29},{... | collective-permute-start | bytes 417800 | tf_op jit(solution)/shard_map/ppermute | solution.py:371
  36.4 13.3 %copy-start.6 = (bf16[4,136,128]{2,1,0:T(8,128)(2,1)}, bf16[4,136,128]{2,1,0:T(8,128)(2,1)S(1)}, u32[]{:S(2)}) copy-start(bf16[4,136,128]{2,1,0:T(8,128)(2,1)S(1)} %collective-permute-done.21.refs_9_) | copy-start | bytes 417796
  36.4 13.2 %collective-permute-start.22 = (bf16[4,136,128]{2,1,0:T(8,128)(2,1)S(1)}, bf16[4,136,128]{2,1,0:T(8,128)(2,1)S(1)}, u32[]{:S(2)}, u32[]{:S(2)}) collective-permute-start(bf16[4,136,128]{2,1,0:T(8,128)(2,1)S(1)} %collective-permute-done.21.refs_9_), channel_id=1, source_target_pairs={{0,4},{4,8},{8,12},{12,16},{16,20},{20,24},{24,28},{28,0},{1,5},{5... | collective-permute-start | bytes 417800 | tf_op jit(solution)/shard_map/ppermute | solution.py:371
  37.8 19.2 %copy-start.12 = (bf16[4,128,128]{2,1,0:T(8,128)(2,1)}, bf16[4,128,128]{2,1,0:T(8,128)(2,1)S(1)}, u32[]{:S(2)}) copy-start(bf16[4,128,128]{2,1,0:T(8,128)(2,1)S(1)} %collective-permute-done.11.refs_10_) | copy-start | bytes 393220
  37.8 19.1 %collective-permute-start.12 = (bf16[4,128,128]{2,1,0:T(8,128)(2,1)S(1)}, bf16[4,128,128]{2,1,0:T(8,128)(2,1)S(1)}, u32[]{:S(2)}, u32[]{:S(2)}) collective-permute-start(bf16[4,128,128]{2,1,0:T(8,128)(2,1)S(1)} %collective-permute-done.11.refs_10_), channel_id=1, source_target_pairs={{0,4},{4,8},{8,12},{12,16},{16,20},{20,24},{24,28},{28,0},{1,5},{5... | collective-permute-start | bytes 393224 | tf_op jit(solution)/shard_map/ppermute | solution.py:371
  37.8 19.2 %copy-start.13 = (bf16[4,128,128]{2,1,0:T(8,128)(2,1)}, bf16[4,128,128]{2,1,0:T(8,128)(2,1)S(1)}, u32[]{:S(2)}) copy-start(bf16[4,128,128]{2,1,0:T(8,128)(2,1)S(1)} %collective-permute-done.8.refs_7_) | copy-start | bytes 393220
  37.8 19.1 %collective-permute-start.9 = (bf16[4,128,128]{2,1,0:T(8,128)(2,1)S(1)}, bf16[4,128,128]{2,1,0:T(8,128)(2,1)S(1)}, u32[]{:S(2)}, u32[]{:S(2)}) collective-permute-start(bf16[4,128,128]{2,1,0:T(8,128)(2,1)S(1)} %collective-permute-done.8.refs_7_), channel_id=1, source_target_pairs={{0,28},{4,0},{8,4},{12,8},{16,12},{20,16},{24,20},{28,24},{1,29},{... | collective-permute-start | bytes 393224 | tf_op jit(solution)/shard_map/ppermute | solution.py:371
  41.5 1.3 %collective-permute-start = (s32[1,4]{1,0:T(1,128)}, s32[1,4]{1,0:T(1,128)S(1)}, u32[]{:S(2)}, u32[]{:S(2)}) collective-permute-start(s32[1,4]{1,0:T(1,128)} %refs_0_.3), channel_id=1, source_target_pairs={{0,1},{1,0},{2,3},{3,2},{4,5},{5,4},{6,7},{7,6},{8,9},{9,8},{10,11... | collective-permute-start | bytes 56 | tf_op jit(solution)/shard_map/ppermute | solution.py:367
  42.7 6.9 %copy-start.16 = (s32[1,4]{1,0:T(1,128)}, s32[1,4]{1,0:T(1,128)S(1)}, u32[]{:S(2)}) copy-start(s32[1,4]{1,0:T(1,128)S(1)} %collective-permute-done.refs_1_) | copy-start | bytes 52
  42.8 3.7 %collective-permute-start.1 = (s32[1,4]{1,0:T(1,128)}, s32[1,4]{1,0:T(1,128)S(1)}, u32[]{:S(2)}, u32[]{:S(2)}) collective-permute-start(s32[1,4]{1,0:T(1,128)} %refs_0_.3), channel_id=1, source_target_pairs={{0,2},{1,3},{2,0},{3,1},{4,6},{5,7},{6,4},{7,5},{8,10},{9,11},{10,... | collective-permute-start | bytes 56 | tf_op jit(solution)/shard_map/ppermute | solution.py:367
  46.5 3.2 %copy-start.17 = (s32[1,4]{1,0:T(1,128)}, s32[1,4]{1,0:T(1,128)S(1)}, u32[]{:S(2)}) copy-start(s32[1,4]{1,0:T(1,128)S(1)} %collective-permute-done.1.refs_2_) | copy-start | bytes 52
  46.5 3.1 %collective-permute-start.2 = (s32[1,4]{1,0:T(1,128)}, s32[1,4]{1,0:T(1,128)S(1)}, u32[]{:S(2)}, u32[]{:S(2)}) collective-permute-start(s32[1,4]{1,0:T(1,128)} %refs_0_.3), channel_id=1, source_target_pairs={{0,3},{1,2},{2,1},{3,0},{4,7},{5,6},{6,5},{7,4},{8,11},{9,10},{10,... | collective-permute-start | bytes 56 | tf_op jit(solution)/shard_map/ppermute | solution.py:367
  49.6 0.5 copy-start.18
  49.6 0.7 copy-start.7
  50.2 0.7 copy-start.8
  56.9 0.7 copy-start.14
  57.0 0.7 copy-start.15

commit v2 on v1

--- a/solution.py
+++ b/solution.py
@@ -181,11 +181,11 @@
                 at = pl.ds(first + seg, 8, stride=8)
                 tile = jnp.concatenate([white[0, at, :], white[1, at, :]], axis=0)
                 out[16 * seg : 16 * seg + 16, :] = tile.astype(jnp.bfloat16)
-        outs[r * HALVES][128:136, :] = table.astype(jnp.bfloat16)
+        outs[r * HALVES + HALVES - 1][128:136, :] = table.astype(jnp.bfloat16)
 
 
 def rows_of(h):
-    return 128 + 8 * (h == 0)
+    return 128 + 8 * (h == HALVES - 1)
 
 
 def spectrum(waves, mask):
@@ -216,49 +216,27 @@
     take = lambda n: [refs.pop(0) for _ in range(n)]
     pairs, planes = take(4), take(8)
     (table_hbm,) = take(1)
-    before = take(2) if h else None
-    outs = take(1) if last else take(2)
-    held, cross, inverse, total, table, sem = take(6)
+    before = take(1)[0] if h else None
+    (out,) = take(1)
+    held, cross, total, inverse, table, spot, sem = take(7)
     _, z, mate = spots()
     fetch = pltpu.make_async_copy(table_hbm.at[2 * mate + h], table, sem)
     fetch.start()
+    for r in range(4):
+        for k in range(PB):
+            p = pairs[r][0, k]
+            dz = ((p // 4) - z + 8) % 8
+            spot[(mate ^ r) * PB + k] = 4 * dz + ((p % 4) ^ mate)
     for dz in range(8):
         for r in range(4):
             held[4 * dz + r] = planes[dz][r].astype(jnp.float32)
 
-    def block_of(q, k):
-        p = pairs[0][0, k]
-        for r in range(1, 4):
-            p = jnp.where((q ^ mate) == r, pairs[r][0, k], p)
-        dz = ((p // 4) - z + 8) % 8
-        return 4 * dz + ((p % 4) ^ mate)
-
-    def out_rows(i, q, k):
-        return pl.ds(pl.multiple_of(i * 128 + q * 32 + k * 8, 8), 8)
-
-    if h:
-        inverse[...] = before[1][...]
-    else:
-
-        def per_count(step, carry):
-            q, k = step // PB, step % PB
-            there = held[block_of(q, k), 128:136, :]
-            for i in range(LS):
-                here = held[q ^ mate, 128 + i : 129 + i, :]
-                inverse[out_rows(i, q, k), :] = here * there
-            return carry
-
-        lax.fori_loop(0, 4 * PB, per_count, 0)
-        ones = jnp.ones((128, 128), jnp.bfloat16)
-        count = jnp.dot(
-            inverse[...].astype(jnp.bfloat16), ones, preferred_element_type=jnp.float32
-        )
-        inverse[...] = 1.0 / jnp.maximum(count, 1.0)
-
     def per_pair(step, carry):
         q, k = step // PB, step % PB
-        theirs, mine = block_of(q, k), q ^ mate
+        theirs, mine = spot[step], q ^ mate
         there = [held[theirs, 8 * e : 8 * e + 8, :] for e in range(2 * SEGS)]
+        if last:
+            marks = held[theirs, 128:136, :]
         for i in range(LS):
             real, imag = None, None
             for e in range(SEGS):
@@ -270,26 +248,32 @@
                 real = add(real, mi * pi)
                 imag = add(imag, mr * pi)
                 imag = sub(imag, mi * pr)
-            at = out_rows(i, q, k)
-            part = inverse[at, :]
-            cross[at, :128] = real * part
-            cross[at, 128:] = imag * part
+            at = pl.ds(pl.multiple_of(i * 128 + q * 32 + k * 8, 8), 8)
+            cross[at, :128] = real
+            cross[at, 128:] = imag
+            if last:
+                inverse[at, :] = held[mine, 128 + i : 129 + i, :] * marks
         return carry
 
     lax.fori_loop(0, 4 * PB, per_pair, 0)
+    if last:
+        ones = jnp.ones((128, 128), jnp.bfloat16)
+        count = jnp.dot(
+            inverse[...].astype(jnp.bfloat16), ones, preferred_element_type=jnp.float32
+        )
+        inverse[...] = 1.0 / jnp.maximum(count, 1.0)
     fetch.wait()
+    lagged = total if last else out
 
     def per_rows(step, carry):
         at = pl.ds(pl.multiple_of(step * 256, 256), 256)
         spectra = cross[at, :].astype(jnp.bfloat16)
         part = jnp.dot(spectra, table[...], preferred_element_type=jnp.float32)
-        total[at, :] = part + before[0][at, :] if h else part
+        lagged[at, :] = part + before[at, :] if h else part
         return carry
 
     lax.fori_loop(0, 4, per_rows, 0)
     if not last:
-        outs[0][...] = total[...]
-        outs[1][...] = inverse[...]
         return
     decay = jnp.full((8, 128), decay_ref[0], jnp.float32)
     high = decay.astype(jnp.bfloat16)
@@ -298,10 +282,11 @@
 
     def per_part(n, carry):
         at = pl.ds(pl.multiple_of(n * 32, 32), 32)
+        part = inverse[at, :]
         for g in range(3):
-            value = total[at, 128 * g : 128 * (g + 1)]
-            outs[0][n, 32 * g : 32 * (g + 1), :] = value.astype(jnp.bfloat16)
-        outs[0][n, 96:104, :] = both.astype(jnp.bfloat16)
+            value = total[at, 128 * g : 128 * (g + 1)] * part
+            out[n, 32 * g : 32 * (g + 1), :] = value.astype(jnp.bfloat16)
+        out[n, 96:104, :] = both.astype(jnp.bfloat16)
         return carry
 
     lax.fori_loop(0, 32, per_part, 0)
@@ -317,10 +302,7 @@
     if last:
         shapes = [jax.ShapeDtypeStruct((32, 104, 128), jnp.bfloat16)]
     else:
-        shapes = [
-            jax.ShapeDtypeStruct((1024, LAGS), jnp.float32),
-            jax.ShapeDtypeStruct((1024, 128), jnp.float32),
-        ]
+        shapes = [jax.ShapeDtypeStruct((1024, LAGS), jnp.float32)]
     return pl.pallas_call(
         functools.partial(correlate_kernel, h),
         out_shape=shapes,
@@ -332,9 +314,10 @@
         scratch_shapes=[
             pltpu.VMEM((32, rows_of(h), 128), jnp.float32),
             pltpu.VMEM((1024, 256), jnp.float32),
-            pltpu.VMEM((1024, 128), jnp.float32),
-            pltpu.VMEM((1024, LAGS), jnp.float32),
+            pltpu.VMEM((1024 if last else 8, LAGS), jnp.float32),
+            pltpu.VMEM((1024 if last else 8, 128), jnp.float32),
             pltpu.VMEM((256, LAGS), jnp.bfloat16),
+            pltpu.SMEM((4 * PB,), jnp.int32),
             pltpu.SemaphoreType.DMA,
         ],
     )(decay, *pairs, *planes, table, *carried)

time: 101 us -> 99.1 us (0.981)
  starting transfers between devices: 27.6 us -> 25.6 us
  waiting for transfers between devices: 14.8 us -> 16.2 us
  Pallas kernels: 18.6 us -> 17.3 us
    ppermute x14, starting transfers between devices: 23.5 us -> 21.8 us  [along(): return lax.ppermute(value, 'z', [(d, (d + step) % 8) for d in range(8)])]
    pallas_call x2, Pallas kernels: 11.8 us -> 10.5 us  [correlate(): pl.pallas_call(functools.partial(correlate_kernel, h), out_shape=shapes,...]
    ppermute x14, waiting for transfers between devices: 6.06 us -> 7.22 us  [along(): return lax.ppermute(value, 'z', [(d, (d + step) % 8) for d in range(8)])]
  transfers between devices with their start and end apart: 23 -> 23, of which waited for: 10 -> 12; matrix products, arithmetic and copies ran while one was open for 2% -> 2% of each run, Pallas kernels for 6% -> 5%
where the time goes in v2:
time: 99.1 us; the launch traced here: 97.3 us
  blocking collectives  32.5 us (33%)
  starting transfers between devices  25.6 us (26%)
  Pallas kernels  17.3 us (17%)
  waiting for transfers between devices  16.2 us (16%)
  local copies, waits for them, and re-layouts  3.25 us (3%)
  other arithmetic  1.56 us (2%)
    ppermute x14, starting transfers between devices, along(): return lax.ppermute(value, 'z', [(d, (d + step) % 8) for d in range(8)])  21.8 us
    all_to_all x1, blocking collectives, body(): parts = lax.all_to_all(carried[0], ('section', 'mate'), 0, 0)  20.3 us
    all_to_all x1, blocking collectives, body(): states = lax.all_to_all(scan_windows(parts), 'section', 0, 0)  12.2 us
    pallas_call x2, Pallas kernels, correlate(): pl.pallas_call(functools.partial(correlate_kernel, h), out_shape=shapes,...  10.5 us
    ppermute x9, waiting for transfers between devices, across(): return lax.ppermute(value, 'mate', [(d, d ^ r) for d in range(4)])  8.95 us
    ppermute x14, waiting for transfers between devices, along(): return lax.ppermute(value, 'z', [(d, (d + step) % 8) for d in range(8)])  7.22 us
    pallas_call x1, Pallas kernels, spectrum(): pl.pallas_call(spectrum_kernel, out_shape=shapes, in_specs=[pl.BlockSpec(...  4.84 us
    ppermute x9, starting transfers between devices, across(): return lax.ppermute(value, 'mate', [(d, d ^ r) for d in range(4)])  3.86 us
  transfers between devices with their start and end apart: 23, of which 12 were waited for; matrix products, arithmetic and copies ran while one was open for 2% of the time, Pallas kernels for 5%

profile of v2, /device:TPU:6, one launch (start us, length us, event | category | flops | bytes accessed | tf_op | source)
XLA Modules:
  0.0 97.3 jit_solution(5050857072080038411)
XLA Ops:
  0.0 4.8 %spectrum.1 = (bf16[128,128]{1,0:T(8,128)(2,1)}, bf16[136,128]{1,0:T(8,128)(2,1)}, bf16[128,128]{1,0:T(8,128)(2,1)}, bf16[136,128]{1,0:T(8,128)(2,1)}, bf16[128,...) custom-call(s32[1,8,8]{2,1,0:T(8,128)} %mask_ref.1, ...), custom_call_target="tpu_custom_call" | custom-call | tf_op jit(solution)/shard_map/spectrum/pallas_call | solution.py:198
  4.8 0.0 collective-permute-start.3
  4.9 1.7 %collective-permute-start.4 = (bf16[136,128]{1,0:T(8,128)(2,1)}, bf16[136,128]{1,0:T(8,128)(2,1)S(1)}, u32[]{:S(2)}, u32[]{:S(2)}) collective-permute-start(bf16[136,128]{1,0:T(8,128)(2,1)} %get-tuple-element.15), channel_id=1, source_target_pairs={{0,2},{1,3},{2,0},{3,1},{4,6},{5,7},{6,4},{7,5},{8,10},{9,11},{10,... | collective-permute-start | bytes 104456 | tf_op jit(solution)/shard_map/ppermute | solution.py:350
  6.6 0.2 collective-permute-start.5
  6.7 0.4 collective-permute-start.13
  7.1 1.6 %collective-permute-start.14 = (bf16[128,128]{1,0:T(8,128)(2,1)}, bf16[128,128]{1,0:T(8,128)(2,1)S(1)}, u32[]{:S(2)}, u32[]{:S(2)}) collective-permute-start(bf16[128,128]{1,0:T(8,128)(2,1)} %get-tuple-element.19), channel_id=1, source_target_pairs={{0,2},{1,3},{2,0},{3,1},{4,6},{5,7},{6,4},{7,5},{8,10},{9,11},{10,... | collective-permute-start | bytes 98312 | tf_op jit(solution)/shard_map/ppermute | solution.py:350
  8.7 0.0 collective-permute-done.3
  8.7 0.0 collective-permute-start.15
  8.7 0.4 collective-permute-done.4
  9.1 1.1 %collective-permute-done.5 = bf16[136,128]{1,0:T(8,128)(2,1)S(1)} collective-permute-done((bf16[136,128]{1,0:T(8,128)(2,1)}, bf16[136,128]{1,0:T(8,128)(2,1)S(1)}, u32[]{:S(2)}, u32[]{:S(2)}) %collective-permute-start.5) | collective-permute-done | bytes 34848 | tf_op jit(solution)/shard_map/ppermute | solution.py:350
  10.2 0.8 pad_maximum_fusion.refs_4_
  11.0 0.0 copy-start
  11.0 5.9 %collective-permute-start.6 = (bf16[4,136,128]{2,1,0:T(8,128)(2,1)S(1)}, bf16[4,136,128]{2,1,0:T(8,128)(2,1)S(1)}, u32[]{:S(2)}, u32[]{:S(2)}) collective-permute-start(bf16[4,136,128]{2,1,0:T(8,128)(2,1)S(1)} %pad_maximum_fusion.refs_4_), channel_id=1, source_target_pairs={{0,28},{4,0},{8,4},{12,8},{16,12},{20,16},{24,20},{28,24},{1,29},{... | collective-permute-start | bytes 417800 | tf_op jit(solution)/shard_map/ppermute | solution.py:354
  16.9 0.0 collective-permute-done.13
  16.9 0.0 collective-permute-done.14
  16.9 0.0 collective-permute-done.15
  16.9 0.8 pad_maximum_fusion.1.refs_4_
  17.7 0.0 copy-start.1
  17.7 0.1 collective-permute-start.19
  17.8 0.1 collective-permute-start.10
  17.9 2.6 %collective-permute-done.6.refs_5_ = bf16[4,136,128]{2,1,0:T(8,128)(2,1)S(1)} collective-permute-done((bf16[4,136,128]{2,1,0:T(8,128)(2,1)S(1)}, bf16[4,136,128]{2,1,0:T(8,128)(2,1)S(1)}, u32[]{:S(2)}, u32[]{:S(2)}) %collective-permute-start.6) | collective-permute-done | bytes 139296 | tf_op jit(solution)/shard_map/ppermute | solution.py:354
  20.5 3.7 %collective-permute-start.7 = (bf16[4,136,128]{2,1,0:T(8,128)(2,1)S(1)}, bf16[4,136,128]{2,1,0:T(8,128)(2,1)S(1)}, u32[]{:S(2)}, u32[]{:S(2)}) collective-permute-start(bf16[4,136,128]{2,1,0:T(8,128)(2,1)S(1)} %collective-permute-done.6.refs_5_), channel_id=1, source_target_pairs={{0,28},{4,0},{8,4},{12,8},{16,12},{20,16},{24,20},{28,24},{1,29},{... | collective-permute-start | bytes 417800 | tf_op jit(solution)/shard_map/ppermute | solution.py:354
  24.2 0.0 collective-permute-start.16
  24.2 1.2 %collective-permute-done.19.refs_11_ = bf16[4,128,128]{2,1,0:T(8,128)(2,1)S(1)} collective-permute-done((bf16[4,128,128]{2,1,0:T(8,128)(2,1)S(1)}, bf16[4,128,128]{2,1,0:T(8,128)(2,1)S(1)}, u32[]{:S(2)}, u32[]{:S(2)}) %collective-permute-start.19) | collective-permute-done | bytes 131104 | tf_op jit(solution)/shard_map/ppermute | solution.py:354
  25.4 0.8 collective-permute-start.20
  26.2 1.4 %collective-permute-done.10.refs_11_ = bf16[4,136,128]{2,1,0:T(8,128)(2,1)S(1)} collective-permute-done((bf16[4,136,128]{2,1,0:T(8,128)(2,1)S(1)}, bf16[4,136,128]{2,1,0:T(8,128)(2,1)S(1)}, u32[]{:S(2)}, u32[]{:S(2)}) %collective-permute-start.10) | collective-permute-done | bytes 139296 | tf_op jit(solution)/shard_map/ppermute | solution.py:354
  27.6 0.0 collective-permute-start.11
  27.6 0.6 collective-permute-done.7.refs_6_
  28.2 3.7 %collective-permute-start.8 = (bf16[4,136,128]{2,1,0:T(8,128)(2,1)S(1)}, bf16[4,136,128]{2,1,0:T(8,128)(2,1)S(1)}, u32[]{:S(2)}, u32[]{:S(2)}) collective-permute-start(bf16[4,136,128]{2,1,0:T(8,128)(2,1)S(1)} %collective-permute-done.7.refs_6_), channel_id=1, source_target_pairs={{0,28},{4,0},{8,4},{12,8},{16,12},{20,16},{24,20},{28,24},{1,29},{... | collective-permute-start | bytes 417800 | tf_op jit(solution)/shard_map/ppermute | solution.py:354
  31.9 0.0 collective-permute-done.16.refs_5_
  31.9 1.4 %collective-permute-start.17 = (bf16[4,128,128]{2,1,0:T(8,128)(2,1)S(1)}, bf16[4,128,128]{2,1,0:T(8,128)(2,1)S(1)}, u32[]{:S(2)}, u32[]{:S(2)}) collective-permute-start(bf16[4,128,128]{2,1,0:T(8,128)(2,1)S(1)} %collective-permute-done.16.refs_5_), channel_id=1, source_target_pairs={{0,28},{4,0},{8,4},{12,8},{16,12},{20,16},{24,20},{28,24},{1,29},{... | collective-permute-start | bytes 393224 | tf_op jit(solution)/shard_map/ppermute | solution.py:354
  33.3 0.0 collective-permute-done.20.refs_10_
  33.3 0.6 collective-permute-start.21
  33.9 0.6 collective-permute-done.11.refs_10_
  34.5 0.0 collective-permute-start.12
  34.6 0.5 collective-permute-done.8.refs_7_
  35.1 3.7 %collective-permute-start.9 = (bf16[4,136,128]{2,1,0:T(8,128)(2,1)S(1)}, bf16[4,136,128]{2,1,0:T(8,128)(2,1)S(1)}, u32[]{:S(2)}, u32[]{:S(2)}) collective-permute-start(bf16[4,136,128]{2,1,0:T(8,128)(2,1)S(1)} %collective-permute-done.8.refs_7_), channel_id=1, source_target_pairs={{0,28},{4,0},{8,4},{12,8},{16,12},{20,16},{24,20},{28,24},{1,29},{... | collective-permute-start | bytes 417800 | tf_op jit(solution)/shard_map/ppermute | solution.py:354
  38.8 0.0 collective-permute-done.17.refs_6_
  38.8 1.4 %collective-permute-start.18 = (bf16[4,128,128]{2,1,0:T(8,128)(2,1)S(1)}, bf16[4,128,128]{2,1,0:T(8,128)(2,1)S(1)}, u32[]{:S(2)}, u32[]{:S(2)}) collective-permute-start(bf16[4,128,128]{2,1,0:T(8,128)(2,1)S(1)} %collective-permute-done.17.refs_6_), channel_id=1, source_target_pairs={{0,28},{4,0},{8,4},{12,8},{16,12},{20,16},{24,20},{28,24},{1,29},{... | collective-permute-start | bytes 393224 | tf_op jit(solution)/shard_map/ppermute | solution.py:354
  40.2 0.3 collective-permute-done.21.refs_9_
  40.5 0.3 collective-permute-start.22
  40.8 0.0 collective-permute-start
  41.5 0.6 collective-permute-done.refs_1_
  42.1 0.0 collective-permute-start.1
  42.1 3.7 %collective-permute-done.1.refs_2_ = s32[1,4]{1,0:T(1,128)S(1)} collective-permute-done((s32[1,4]{1,0:T(1,128)}, s32[1,4]{1,0:T(1,128)S(1)}, u32[]{:S(2)}, u32[]{:S(2)}) %collective-permute-start.1) | collective-permute-done | bytes 48 | tf_op jit(solution)/shard_map/ppermute | solution.py:350
  45.8 0.0 collective-permute-start.2
  45.8 3.1 %collective-permute-done.2.refs_3_ = s32[1,4]{1,0:T(1,128)S(1)} collective-permute-done((s32[1,4]{1,0:T(1,128)}, s32[1,4]{1,0:T(1,128)S(1)}, u32[]{:S(2)}, u32[]{:S(2)}) %collective-permute-start.2) | collective-permute-done | bytes 48 | tf_op jit(solution)/shard_map/ppermute | solution.py:350
  48.9 0.0 collective-permute-done.18.refs_7_
  48.9 0.0 collective-permute-done.22.refs_8_
  49.0 0.0 copy-done.1
  49.0 0.0 copy-done.9
  49.0 0.4 copy-done.18
  49.5 0.1 copy-done.14
  49.6 0.7 copy-done.15
  50.2 4.8 %shard_map.73.refs_13_ = f32[1024,384]{1,0:T(8,128)} custom-call(f32[1]{0:T(128)S(6)} %copy.9.decay_ref, s32[1,4]{1,0:T(1,128)} %refs_0_.3, s32[1,4]{1,0:T(1,128)} %copy-done.16, s32[1,4]{1,0:T(1,128)} %copy-done.17, s32[1,4]{1,0:T(1,128)} %copy-done.18, bf16[4,128,128]{2,1,0:T(8,128)(2,1)} %copy-done.1, bf16[4,128,128]{2,1,0:T(8,128)(2,1)} %copy-done.10, ...), custom_call_target="tpu_custom_call" | custom-call | tf_op jit(solution)/shard_map/pallas_call | solution.py:306
  55.1 0.0 collective-permute-done.12.refs_9_
  55.2 0.0 collective-permute-done.9.refs_8_
  55.2 0.7 copy-done.7
  55.8 0.6 copy-done.8
  56.5 5.7 %shard_map.74 = bf16[32,104,128]{2,1,0:T(8,128)(2,1)} custom-call(f32[1]{0:T(128)S(6)} %copy.9.decay_ref, s32[1,4]{1,0:T(1,128)} %refs_0_.3, s32[1,4]{1,0:T(1,128)} %copy-done.16, s32[1,4]{1,0:T(1,128)} %copy-done.17, s32[1,4]{1,0:T(1,128)} %copy-done.18, bf16[4,136,128]{2,1,0:T(8,128)(2,1)} %copy-done, bf16[4,136,128]{2,1,0:T(8,128)(2,1)} %copy-done.2, ...), custom_call_target="tpu_custom_call" | custom-call | tf_op jit(solution)/shard_map/pallas_call | solution.py:306
  62.2 20.3 %all_to_all.10.parts = bf16[32,104,128]{2,1,0:T(8,128)(2,1)} all-to-all(bf16[32,104,128]{2,1,0:T(8,128)(2,1)} %shard_map.74), channel_id=1, replica_groups=mesh['section'=8,'z'=8,'mate'=4] {'section','mate'}, dimensions={0} | all-to-all | bytes 1703936 | tf_op jit(solution)/shard_map/all_to_all | solution.py:375
  82.5 2.0 %scan.1 = bf16[8,32,384]{2,1,0:T(8,128)(2,1)} custom-call(bf16[32,104,128]{2,1,0:T(8,128)(2,1)} %all_to_all.10.parts), custom_call_target="tpu_custom_call" | custom-call | tf_op jit(solution)/shard_map/scan/pallas_call | solution.py:340
  84.4 12.2 %all_to_all.11 = bf16[8,32,384]{2,1,0:T(8,128)(2,1)S(1)} all-to-all(bf16[8,32,384]{2,1,0:T(8,128)(2,1)} %scan.1), channel_id=1, replica_groups=mesh['section'=8,'z'=8,'mate'=4] {'section'}, dimensions={0} | all-to-all | bytes 393216 | tf_op jit(solution)/shard_map/all_to_all | solution.py:376
  96.7 0.7 copy.10
  (29 shorter events, 0.1 us)
Async XLA Ops:
  4.8 3.9 %collective-permute-start.3 = (bf16[136,128]{1,0:T(8,128)(2,1)}, bf16[136,128]{1,0:T(8,128)(2,1)S(1)}, u32[]{:S(2)}, u32[]{:S(2)}) collective-permute-start(bf16[136,128]{1,0:T(8,128)(2,1)} %get-tuple-element.14), channel_id=1, source_target_pairs={{0,1},{1,0},{2,3},{3,2},{4,5},{5,4},{6,7},{7,6},{8,9},{9,8},{10,11... | collective-permute-start | bytes 104456 | tf_op jit(solution)/shard_map/ppermute | solution.py:350
  4.9 4.2 %collective-permute-start.4 = (bf16[136,128]{1,0:T(8,128)(2,1)}, bf16[136,128]{1,0:T(8,128)(2,1)S(1)}, u32[]{:S(2)}, u32[]{:S(2)}) collective-permute-start(bf16[136,128]{1,0:T(8,128)(2,1)} %get-tuple-element.15), channel_id=1, source_target_pairs={{0,2},{1,3},{2,0},{3,1},{4,6},{5,7},{6,4},{7,5},{8,10},{9,11},{10,... | collective-permute-start | bytes 104456 | tf_op jit(solution)/shard_map/ppermute | solution.py:350
  6.6 3.6 %collective-permute-start.5 = (bf16[136,128]{1,0:T(8,128)(2,1)}, bf16[136,128]{1,0:T(8,128)(2,1)S(1)}, u32[]{:S(2)}, u32[]{:S(2)}) collective-permute-start(bf16[136,128]{1,0:T(8,128)(2,1)} %get-tuple-element.16), channel_id=1, source_target_pairs={{0,3},{1,2},{2,1},{3,0},{4,7},{5,6},{6,5},{7,4},{8,11},{9,10},{10,... | collective-permute-start | bytes 104456 | tf_op jit(solution)/shard_map/ppermute | solution.py:350
  6.7 10.2 %collective-permute-start.13 = (bf16[128,128]{1,0:T(8,128)(2,1)}, bf16[128,128]{1,0:T(8,128)(2,1)S(1)}, u32[]{:S(2)}, u32[]{:S(2)}) collective-permute-start(bf16[128,128]{1,0:T(8,128)(2,1)} %get-tuple-element.18), channel_id=1, source_target_pairs={{0,1},{1,0},{2,3},{3,2},{4,5},{5,4},{6,7},{7,6},{8,9},{9,8},{10,11... | collective-permute-start | bytes 98312 | tf_op jit(solution)/shard_map/ppermute | solution.py:350
  7.1 9.8 %collective-permute-start.14 = (bf16[128,128]{1,0:T(8,128)(2,1)}, bf16[128,128]{1,0:T(8,128)(2,1)S(1)}, u32[]{:S(2)}, u32[]{:S(2)}) collective-permute-start(bf16[128,128]{1,0:T(8,128)(2,1)} %get-tuple-element.19), channel_id=1, source_target_pairs={{0,2},{1,3},{2,0},{3,1},{4,6},{5,7},{6,4},{7,5},{8,10},{9,11},{10,... | collective-permute-start | bytes 98312 | tf_op jit(solution)/shard_map/ppermute | solution.py:350
  8.7 8.2 %collective-permute-start.15 = (bf16[128,128]{1,0:T(8,128)(2,1)}, bf16[128,128]{1,0:T(8,128)(2,1)S(1)}, u32[]{:S(2)}, u32[]{:S(2)}) collective-permute-start(bf16[128,128]{1,0:T(8,128)(2,1)} %get-tuple-element.20), channel_id=1, source_target_pairs={{0,3},{1,2},{2,1},{3,0},{4,7},{5,6},{6,5},{7,4},{8,11},{9,10},{10,... | collective-permute-start | bytes 98312 | tf_op jit(solution)/shard_map/ppermute | solution.py:350
  11.0 44.1 %copy-start = (bf16[4,136,128]{2,1,0:T(8,128)(2,1)}, bf16[4,136,128]{2,1,0:T(8,128)(2,1)S(1)}, u32[]{:S(2)}) copy-start(bf16[4,136,128]{2,1,0:T(8,128)(2,1)S(1)} %pad_maximum_fusion.refs_4_) | copy-start | bytes 417796
  11.0 9.5 %collective-permute-start.6 = (bf16[4,136,128]{2,1,0:T(8,128)(2,1)S(1)}, bf16[4,136,128]{2,1,0:T(8,128)(2,1)S(1)}, u32[]{:S(2)}, u32[]{:S(2)}) collective-permute-start(bf16[4,136,128]{2,1,0:T(8,128)(2,1)S(1)} %pad_maximum_fusion.refs_4_), channel_id=1, source_target_pairs={{0,28},{4,0},{8,4},{12,8},{16,12},{20,16},{24,20},{28,24},{1,29},{... | collective-permute-start | bytes 417800 | tf_op jit(solution)/shard_map/ppermute | solution.py:354
  17.7 31.2 %copy-start.1 = (bf16[4,128,128]{2,1,0:T(8,128)(2,1)}, bf16[4,128,128]{2,1,0:T(8,128)(2,1)S(1)}, u32[]{:S(2)}) copy-start(bf16[4,128,128]{2,1,0:T(8,128)(2,1)S(1)} %pad_maximum_fusion.1.refs_4_) | copy-start | bytes 393220
  17.7 7.7 %collective-permute-start.19 = (bf16[4,128,128]{2,1,0:T(8,128)(2,1)S(1)}, bf16[4,128,128]{2,1,0:T(8,128)(2,1)S(1)}, u32[]{:S(2)}, u32[]{:S(2)}) collective-permute-start(bf16[4,128,128]{2,1,0:T(8,128)(2,1)S(1)} %pad_maximum_fusion.1.refs_4_), channel_id=1, source_target_pairs={{0,4},{4,8},{8,12},{12,16},{16,20},{20,24},{24,28},{28,0},{1,5},{5... | collective-permute-start | bytes 393224 | tf_op jit(solution)/shard_map/ppermute | solution.py:354
  17.8 9.7 %collective-permute-start.10 = (bf16[4,136,128]{2,1,0:T(8,128)(2,1)S(1)}, bf16[4,136,128]{2,1,0:T(8,128)(2,1)S(1)}, u32[]{:S(2)}, u32[]{:S(2)}) collective-permute-start(bf16[4,136,128]{2,1,0:T(8,128)(2,1)S(1)} %pad_maximum_fusion.refs_4_), channel_id=1, source_target_pairs={{0,4},{4,8},{8,12},{12,16},{16,20},{20,24},{24,28},{28,0},{1,5},{5... | collective-permute-start | bytes 417800 | tf_op jit(solution)/shard_map/ppermute | solution.py:354
  20.5 34.6 %copy-start.2 = (bf16[4,136,128]{2,1,0:T(8,128)(2,1)}, bf16[4,136,128]{2,1,0:T(8,128)(2,1)S(1)}, u32[]{:S(2)}) copy-start(bf16[4,136,128]{2,1,0:T(8,128)(2,1)S(1)} %collective-permute-done.6.refs_5_) | copy-start | bytes 417796
  20.5 7.8 %collective-permute-start.7 = (bf16[4,136,128]{2,1,0:T(8,128)(2,1)S(1)}, bf16[4,136,128]{2,1,0:T(8,128)(2,1)S(1)}, u32[]{:S(2)}, u32[]{:S(2)}) collective-permute-start(bf16[4,136,128]{2,1,0:T(8,128)(2,1)S(1)} %collective-permute-done.6.refs_5_), channel_id=1, source_target_pairs={{0,28},{4,0},{8,4},{12,8},{16,12},{20,16},{24,20},{28,24},{1,29},{... | collective-permute-start | bytes 417800 | tf_op jit(solution)/shard_map/ppermute | solution.py:354
  24.2 7.8 %collective-permute-start.16 = (bf16[4,128,128]{2,1,0:T(8,128)(2,1)S(1)}, bf16[4,128,128]{2,1,0:T(8,128)(2,1)S(1)}, u32[]{:S(2)}, u32[]{:S(2)}) collective-permute-start(bf16[4,128,128]{2,1,0:T(8,128)(2,1)S(1)} %pad_maximum_fusion.1.refs_4_), channel_id=1, source_target_pairs={{0,28},{4,0},{8,4},{12,8},{16,12},{20,16},{24,20},{28,24},{1,29},{... | collective-permute-start | bytes 393224 | tf_op jit(solution)/shard_map/ppermute | solution.py:354
  25.4 23.6 %copy-start.9 = (bf16[4,128,128]{2,1,0:T(8,128)(2,1)}, bf16[4,128,128]{2,1,0:T(8,128)(2,1)S(1)}, u32[]{:S(2)}) copy-start(bf16[4,128,128]{2,1,0:T(8,128)(2,1)S(1)} %collective-permute-done.19.refs_11_) | copy-start | bytes 393220
  25.4 8.0 %collective-permute-start.20 = (bf16[4,128,128]{2,1,0:T(8,128)(2,1)S(1)}, bf16[4,128,128]{2,1,0:T(8,128)(2,1)S(1)}, u32[]{:S(2)}, u32[]{:S(2)}) collective-permute-start(bf16[4,128,128]{2,1,0:T(8,128)(2,1)S(1)} %collective-permute-done.19.refs_11_), channel_id=1, source_target_pairs={{0,4},{4,8},{8,12},{12,16},{16,20},{20,24},{24,28},{28,0},{1,5},{5... | collective-permute-start | bytes 393224 | tf_op jit(solution)/shard_map/ppermute | solution.py:354
  27.6 27.5 %copy-start.3 = (bf16[4,136,128]{2,1,0:T(8,128)(2,1)}, bf16[4,136,128]{2,1,0:T(8,128)(2,1)S(1)}, u32[]{:S(2)}) copy-start(bf16[4,136,128]{2,1,0:T(8,128)(2,1)S(1)} %collective-permute-done.10.refs_11_) | copy-start | bytes 417796
  27.6 7.0 %collective-permute-start.11 = (bf16[4,136,128]{2,1,0:T(8,128)(2,1)S(1)}, bf16[4,136,128]{2,1,0:T(8,128)(2,1)S(1)}, u32[]{:S(2)}, u32[]{:S(2)}) collective-permute-start(bf16[4,136,128]{2,1,0:T(8,128)(2,1)S(1)} %collective-permute-done.10.refs_11_), channel_id=1, source_target_pairs={{0,4},{4,8},{8,12},{12,16},{16,20},{20,24},{24,28},{28,0},{1,5},{5... | collective-permute-start | bytes 417800 | tf_op jit(solution)/shard_map/ppermute | solution.py:354
  28.2 26.9 %copy-start.4 = (bf16[4,136,128]{2,1,0:T(8,128)(2,1)}, bf16[4,136,128]{2,1,0:T(8,128)(2,1)S(1)}, u32[]{:S(2)}) copy-start(bf16[4,136,128]{2,1,0:T(8,128)(2,1)S(1)} %collective-permute-done.7.refs_6_) | copy-start | bytes 417796
  28.2 6.9 %collective-permute-start.8 = (bf16[4,136,128]{2,1,0:T(8,128)(2,1)S(1)}, bf16[4,136,128]{2,1,0:T(8,128)(2,1)S(1)}, u32[]{:S(2)}, u32[]{:S(2)}) collective-permute-start(bf16[4,136,128]{2,1,0:T(8,128)(2,1)S(1)} %collective-permute-done.7.refs_6_), channel_id=1, source_target_pairs={{0,28},{4,0},{8,4},{12,8},{16,12},{20,16},{24,20},{28,24},{1,29},{... | collective-permute-start | bytes 417800 | tf_op jit(solution)/shard_map/ppermute | solution.py:354
  31.9 17.1 %copy-start.10 = (bf16[4,128,128]{2,1,0:T(8,128)(2,1)}, bf16[4,128,128]{2,1,0:T(8,128)(2,1)S(1)}, u32[]{:S(2)}) copy-start(bf16[4,128,128]{2,1,0:T(8,128)(2,1)S(1)} %collective-permute-done.16.refs_5_) | copy-start | bytes 393220
  31.9 6.9 %collective-permute-start.17 = (bf16[4,128,128]{2,1,0:T(8,128)(2,1)S(1)}, bf16[4,128,128]{2,1,0:T(8,128)(2,1)S(1)}, u32[]{:S(2)}, u32[]{:S(2)}) collective-permute-start(bf16[4,128,128]{2,1,0:T(8,128)(2,1)S(1)} %collective-permute-done.16.refs_5_), channel_id=1, source_target_pairs={{0,28},{4,0},{8,4},{12,8},{16,12},{20,16},{24,20},{28,24},{1,29},{... | collective-permute-start | bytes 393224 | tf_op jit(solution)/shard_map/ppermute | solution.py:354
  33.3 15.6 %copy-start.11 = (bf16[4,128,128]{2,1,0:T(8,128)(2,1)}, bf16[4,128,128]{2,1,0:T(8,128)(2,1)S(1)}, u32[]{:S(2)}) copy-start(bf16[4,128,128]{2,1,0:T(8,128)(2,1)S(1)} %collective-permute-done.20.refs_10_) | copy-start | bytes 393220
  33.3 7.1 %collective-permute-start.21 = (bf16[4,128,128]{2,1,0:T(8,128)(2,1)S(1)}, bf16[4,128,128]{2,1,0:T(8,128)(2,1)S(1)}, u32[]{:S(2)}, u32[]{:S(2)}) collective-permute-start(bf16[4,128,128]{2,1,0:T(8,128)(2,1)S(1)} %collective-permute-done.20.refs_10_), channel_id=1, source_target_pairs={{0,4},{4,8},{8,12},{12,16},{16,20},{20,24},{24,28},{28,0},{1,5},{5... | collective-permute-start | bytes 393224 | tf_op jit(solution)/shard_map/ppermute | solution.py:354
  34.5 20.6 %copy-start.5 = (bf16[4,136,128]{2,1,0:T(8,128)(2,1)}, bf16[4,136,128]{2,1,0:T(8,128)(2,1)S(1)}, u32[]{:S(2)}) copy-start(bf16[4,136,128]{2,1,0:T(8,128)(2,1)S(1)} %collective-permute-done.11.refs_10_) | copy-start | bytes 417796
  34.5 20.6 %collective-permute-start.12 = (bf16[4,136,128]{2,1,0:T(8,128)(2,1)S(1)}, bf16[4,136,128]{2,1,0:T(8,128)(2,1)S(1)}, u32[]{:S(2)}, u32[]{:S(2)}) collective-permute-start(bf16[4,136,128]{2,1,0:T(8,128)(2,1)S(1)} %collective-permute-done.11.refs_10_), channel_id=1, source_target_pairs={{0,4},{4,8},{8,12},{12,16},{16,20},{20,24},{24,28},{28,0},{1,5},{5... | collective-permute-start | bytes 417800 | tf_op jit(solution)/shard_map/ppermute | solution.py:354
  35.1 20.1 %copy-start.6 = (bf16[4,136,128]{2,1,0:T(8,128)(2,1)}, bf16[4,136,128]{2,1,0:T(8,128)(2,1)S(1)}, u32[]{:S(2)}) copy-start(bf16[4,136,128]{2,1,0:T(8,128)(2,1)S(1)} %collective-permute-done.8.refs_7_) | copy-start | bytes 417796
  35.1 20.1 %collective-permute-start.9 = (bf16[4,136,128]{2,1,0:T(8,128)(2,1)S(1)}, bf16[4,136,128]{2,1,0:T(8,128)(2,1)S(1)}, u32[]{:S(2)}, u32[]{:S(2)}) collective-permute-start(bf16[4,136,128]{2,1,0:T(8,128)(2,1)S(1)} %collective-permute-done.8.refs_7_), channel_id=1, source_target_pairs={{0,28},{4,0},{8,4},{12,8},{16,12},{20,16},{24,20},{28,24},{1,29},{... | collective-permute-start | bytes 417800 | tf_op jit(solution)/shard_map/ppermute | solution.py:354
  38.8 10.2 %copy-start.12 = (bf16[4,128,128]{2,1,0:T(8,128)(2,1)}, bf16[4,128,128]{2,1,0:T(8,128)(2,1)S(1)}, u32[]{:S(2)}) copy-start(bf16[4,128,128]{2,1,0:T(8,128)(2,1)S(1)} %collective-permute-done.17.refs_6_) | copy-start | bytes 393220
  38.8 10.2 %collective-permute-start.18 = (bf16[4,128,128]{2,1,0:T(8,128)(2,1)S(1)}, bf16[4,128,128]{2,1,0:T(8,128)(2,1)S(1)}, u32[]{:S(2)}, u32[]{:S(2)}) collective-permute-start(bf16[4,128,128]{2,1,0:T(8,128)(2,1)S(1)} %collective-permute-done.17.refs_6_), channel_id=1, source_target_pairs={{0,28},{4,0},{8,4},{12,8},{16,12},{20,16},{24,20},{28,24},{1,29},{... | collective-permute-start | bytes 393224 | tf_op jit(solution)/shard_map/ppermute | solution.py:354
  40.5 8.5 %copy-start.13 = (bf16[4,128,128]{2,1,0:T(8,128)(2,1)}, bf16[4,128,128]{2,1,0:T(8,128)(2,1)S(1)}, u32[]{:S(2)}) copy-start(bf16[4,128,128]{2,1,0:T(8,128)(2,1)S(1)} %collective-permute-done.21.refs_9_) | copy-start | bytes 393220
  40.5 8.5 %collective-permute-start.22 = (bf16[4,128,128]{2,1,0:T(8,128)(2,1)S(1)}, bf16[4,128,128]{2,1,0:T(8,128)(2,1)S(1)}, u32[]{:S(2)}, u32[]{:S(2)}) collective-permute-start(bf16[4,128,128]{2,1,0:T(8,128)(2,1)S(1)} %collective-permute-done.21.refs_9_), channel_id=1, source_target_pairs={{0,4},{4,8},{8,12},{12,16},{16,20},{20,24},{24,28},{28,0},{1,5},{5... | collective-permute-start | bytes 393224 | tf_op jit(solution)/shard_map/ppermute | solution.py:354
  40.8 1.3 %collective-permute-start = (s32[1,4]{1,0:T(1,128)}, s32[1,4]{1,0:T(1,128)S(1)}, u32[]{:S(2)}, u32[]{:S(2)}) collective-permute-start(s32[1,4]{1,0:T(1,128)} %refs_0_.3), channel_id=1, source_target_pairs={{0,1},{1,0},{2,3},{3,2},{4,5},{5,4},{6,7},{7,6},{8,9},{9,8},{10,11... | collective-permute-start | bytes 56 | tf_op jit(solution)/shard_map/ppermute | solution.py:350
  42.1 6.9 %copy-start.16 = (s32[1,4]{1,0:T(1,128)}, s32[1,4]{1,0:T(1,128)S(1)}, u32[]{:S(2)}) copy-start(s32[1,4]{1,0:T(1,128)S(1)} %collective-permute-done.refs_1_) | copy-start | bytes 52
  42.1 3.7 %collective-permute-start.1 = (s32[1,4]{1,0:T(1,128)}, s32[1,4]{1,0:T(1,128)S(1)}, u32[]{:S(2)}, u32[]{:S(2)}) collective-permute-start(s32[1,4]{1,0:T(1,128)} %refs_0_.3), channel_id=1, source_target_pairs={{0,2},{1,3},{2,0},{3,1},{4,6},{5,7},{6,4},{7,5},{8,10},{9,11},{10,... | collective-permute-start | bytes 56 | tf_op jit(solution)/shard_map/ppermute | solution.py:350
  45.8 3.2 %copy-start.17 = (s32[1,4]{1,0:T(1,128)}, s32[1,4]{1,0:T(1,128)S(1)}, u32[]{:S(2)}) copy-start(s32[1,4]{1,0:T(1,128)S(1)} %collective-permute-done.1.refs_2_) | copy-start | bytes 52
  45.8 3.1 %collective-permute-start.2 = (s32[1,4]{1,0:T(1,128)}, s32[1,4]{1,0:T(1,128)S(1)}, u32[]{:S(2)}, u32[]{:S(2)}) collective-permute-start(s32[1,4]{1,0:T(1,128)} %refs_0_.3), channel_id=1, source_target_pairs={{0,3},{1,2},{2,1},{3,0},{4,7},{5,6},{6,5},{7,4},{8,11},{9,10},{10,... | collective-permute-start | bytes 56 | tf_op jit(solution)/shard_map/ppermute | solution.py:350
  48.9 0.5 copy-start.18
  48.9 0.7 copy-start.14
  49.6 0.7 copy-start.15
  55.1 0.7 copy-start.7
  55.8 0.7 copy-start.8

commit v3 on v2

--- a/solution.py
+++ b/solution.py
@@ -94,7 +94,7 @@
 
 
 def spots():
-    return lax.axis_index("section"), lax.axis_index("z"), lax.axis_index("mate")
+    return lax.axis_index("z"), 2 * lax.axis_index("y") + lax.axis_index("c")
 
 
 def spectrum_kernel(mask_ref, wave_ref, turn_ref, dft_ref, *refs):
@@ -172,7 +172,7 @@
         rows = slice(64 * c, 64 * (c + 1))
         white[0, rows, :] = re[rows] * scale
         white[1, rows, :] = im[rows] * scale
-    mate = spots()[2]
+    mate = spots()[1]
     for r in range(4):
         for h in range(HALVES):
             out = outs[r * HALVES + h]
@@ -217,33 +217,42 @@
     pairs, planes = take(4), take(8)
     (table_hbm,) = take(1)
     before = take(1)[0] if h else None
-    (out,) = take(1)
-    held, cross, total, inverse, table, spot, sem = take(7)
-    _, z, mate = spots()
-    fetch = pltpu.make_async_copy(table_hbm.at[2 * mate + h], table, sem)
-    fetch.start()
+    outs = take(2) if last else take(1)
+    held, own, cross, total, inverse, table, spot, plane_sem, sem = take(9)
+    z, mate = spots()
+    loads = [
+        pltpu.make_async_copy(planes[dz], held.at[pl.ds(4 * dz, 4)], plane_sem.at[dz])
+        for dz in range(8)
+    ]
+    fetches = [pltpu.make_async_copy(table_hbm.at[2 * mate + h], table, sem.at[0])]
+    if h:
+        fetches.append(pltpu.make_async_copy(before, total, sem.at[1]))
+    for copy in loads + fetches:
+        copy.start()
     for r in range(4):
         for k in range(PB):
             p = pairs[r][0, k]
             dz = ((p // 4) - z + 8) % 8
             spot[(mate ^ r) * PB + k] = 4 * dz + ((p % 4) ^ mate)
-    for dz in range(8):
-        for r in range(4):
-            held[4 * dz + r] = planes[dz][r].astype(jnp.float32)
+    loads[0].wait()
+    for r in range(4):
+        own[r] = held[r].astype(jnp.float32)
+    for copy in loads[1:]:
+        copy.wait()
 
     def per_pair(step, carry):
         q, k = step // PB, step % PB
         theirs, mine = spot[step], q ^ mate
-        there = [held[theirs, 8 * e : 8 * e + 8, :] for e in range(2 * SEGS)]
+        tiles = [held[theirs, 16 * e : 16 * e + 16, :].astype(jnp.float32) for e in range(SEGS)]
         if last:
-            marks = held[theirs, 128:136, :]
+            marks = held[theirs, 128:136, :].astype(jnp.float32)
         for i in range(LS):
             real, imag = None, None
             for e in range(SEGS):
-                pr, pi = there[2 * e], there[2 * e + 1]
+                pr, pi = tiles[e][:8], tiles[e][8:]
                 at = 16 * e + i
-                mr = jnp.broadcast_to(held[mine, at : at + 1, :], (8, 128))
-                mi = jnp.broadcast_to(held[mine, at + 8 : at + 9, :], (8, 128))
+                mr = jnp.broadcast_to(own[mine, at : at + 1, :], (8, 128))
+                mi = jnp.broadcast_to(own[mine, at + 8 : at + 9, :], (8, 128))
                 real = add(real, mr * pr)
                 real = add(real, mi * pi)
                 imag = add(imag, mr * pi)
@@ -252,7 +261,7 @@
             cross[at, :128] = real
             cross[at, 128:] = imag
             if last:
-                inverse[at, :] = held[mine, 128 + i : 129 + i, :] * marks
+                inverse[at, :] = own[mine, 128 + i : 129 + i, :] * marks
         return carry
 
     lax.fori_loop(0, 4 * PB, per_pair, 0)
@@ -262,14 +271,15 @@
             inverse[...].astype(jnp.bfloat16), ones, preferred_element_type=jnp.float32
         )
         inverse[...] = 1.0 / jnp.maximum(count, 1.0)
-    fetch.wait()
-    lagged = total if last else out
+    for copy in fetches:
+        copy.wait()
+    lagged = total if last else outs[0]
 
     def per_rows(step, carry):
         at = pl.ds(pl.multiple_of(step * 256, 256), 256)
         spectra = cross[at, :].astype(jnp.bfloat16)
         part = jnp.dot(spectra, table[...], preferred_element_type=jnp.float32)
-        lagged[at, :] = part + before[at, :] if h else part
+        lagged[at, :] = part + lagged[at, :] if h else part
         return carry
 
     lax.fori_loop(0, 4, per_rows, 0)
@@ -280,16 +290,22 @@
     low = (decay - high.astype(jnp.float32)).astype(jnp.bfloat16)
     both = jnp.where(row_of(8) < 4, high.astype(jnp.float32), low.astype(jnp.float32))
 
+    core = mate % 2
+
     def per_part(n, carry):
-        at = pl.ds(pl.multiple_of(n * 32, 32), 32)
-        part = inverse[at, :]
-        for g in range(3):
-            value = total[at, 128 * g : 128 * (g + 1)] * part
-            out[n, 32 * g : 32 * (g + 1), :] = value.astype(jnp.bfloat16)
-        out[n, 96:104, :] = both.astype(jnp.bfloat16)
+        i, y = n // 2, n % 2
+        for keep in range(2):
+            q = 2 * y + (core ^ keep)
+            at = pl.ds(pl.multiple_of(i * 128 + q * 32, 32), 32)
+            part = inverse[at, :]
+            for g in range(3):
+                value = total[at, 128 * g : 128 * (g + 1)] * part
+                outs[keep][n, 32 * g : 32 * (g + 1), :] = value.astype(jnp.bfloat16)
+            marks = jnp.zeros_like(both) if keep else both
+            outs[keep][n, 96:104, :] = marks.astype(jnp.bfloat16)
         return carry
 
-    lax.fori_loop(0, 32, per_part, 0)
+    lax.fori_loop(0, 16, per_part, 0)
 
 
 def row_of(n):
@@ -300,25 +316,25 @@
     last = h == HALVES - 1
     smem, vmem = pl.BlockSpec(memory_space=pltpu.SMEM), pl.BlockSpec(memory_space=pltpu.VMEM)
     if last:
-        shapes = [jax.ShapeDtypeStruct((32, 104, 128), jnp.bfloat16)]
+        shapes = [jax.ShapeDtypeStruct((16, 104, 128), jnp.bfloat16)] * 2
     else:
         shapes = [jax.ShapeDtypeStruct((1024, LAGS), jnp.float32)]
     return pl.pallas_call(
         functools.partial(correlate_kernel, h),
         out_shape=shapes,
         in_specs=[smem] * 5
-        + [vmem] * 8
-        + [pl.BlockSpec(memory_space=pl.ANY)]
-        + [vmem] * len(carried),
+        + [pl.BlockSpec(memory_space=pl.ANY)] * (9 + len(carried)),
         out_specs=[vmem] * len(shapes),
         scratch_shapes=[
-            pltpu.VMEM((32, rows_of(h), 128), jnp.float32),
+            pltpu.VMEM((32, rows_of(h), 128), jnp.bfloat16),
+            pltpu.VMEM((4, rows_of(h), 128), jnp.float32),
             pltpu.VMEM((1024, 256), jnp.float32),
             pltpu.VMEM((1024 if last else 8, LAGS), jnp.float32),
             pltpu.VMEM((1024 if last else 8, 128), jnp.float32),
             pltpu.VMEM((256, LAGS), jnp.bfloat16),
             pltpu.SMEM((4 * PB,), jnp.int32),
-            pltpu.SemaphoreType.DMA,
+            pltpu.SemaphoreType.DMA((8,)),
+            pltpu.SemaphoreType.DMA((2,)),
         ],
     )(decay, *pairs, *planes, table, *carried)
 
@@ -326,11 +342,12 @@
 def scan_kernel(parts, out):
     state = [jnp.zeros((32, 128), jnp.float32)] * 3
     for w in range(8):
-        marks = parts[4 * w, 96:104, :].astype(jnp.float32)
+        marks = parts[2 * w, 96:104, :].astype(jnp.float32)
         decay = marks[:1] + marks[4:5]
         for g in range(3):
             at = slice(32 * g, 32 * (g + 1))
-            lagged = sum(parts[4 * w + q, at, :].astype(jnp.float32) for q in range(4))
+            lagged = parts[2 * w, at, :].astype(jnp.float32)
+            lagged = lagged + parts[2 * w + 1, at, :].astype(jnp.float32)
             state[g] = decay * state[g] + lagged
             out[w, :, 128 * g : 128 * (g + 1)] = state[g].astype(jnp.bfloat16)
 
@@ -347,7 +364,7 @@
 
 
 def across(value, r):
-    return lax.ppermute(value, "mate", [(d, d ^ r) for d in range(4)])
+    return lax.ppermute(value, ("y", "c"), [(d, d ^ r) for d in range(4)])
 
 
 def along(value, step):
@@ -372,14 +389,16 @@
                 back = along(back, -1)
                 planes[step] = back
         carried = correlate(h, window_decay, pairs, planes, table, carried)
-    parts = lax.all_to_all(carried[0], ("section", "mate"), 0, 0)
+    kept, sent = carried
+    kept = kept.astype(jnp.float32) + across(sent, 1).astype(jnp.float32)
+    parts = lax.all_to_all(kept.astype(jnp.bfloat16), ("section", "y"), 0, 0)
     states = lax.all_to_all(scan_windows(parts), "section", 0, 0)
     return states[None]
 
 
 def solution(mesh):
-    split = Mesh(mesh.devices.reshape(8, 8, 4), ("section", "z", "mate"))
-    sta = ("z", "mate")
+    split = Mesh(mesh.devices.reshape(8, 8, 2, 2), ("section", "z", "y", "c"))
+    sta = ("z", "y", "c")
     placed = (P("section", sta, None, None), P("section", sta, None), P(sta, None), P("section"))
 
     return jax.shard_map(

time: 99.1 us -> 97.2 us (0.981)
  blocking collectives: 32.5 us -> 27.1 us
  waiting for transfers between devices: 16.2 us -> 18.1 us
  other arithmetic: 1.56 us -> 2.68 us
    all_to_all x1, blocking collectives: 20.3 us -> 15 us  [body(): parts = lax.all_to_all(kept.astype(jnp.bfloat16), ('section', 'y'), 0, 0)]
    ppermute x9 -> x10, waiting for transfers between devices: 8.95 us -> 10.9 us  [across(): return lax.ppermute(value, ('y', 'c'), [(d, d ^ r) for d in range(4)])]
    convert_element_type x0 -> x1, other arithmetic: none -> 1.12 us  [body(): parts = lax.all_to_all(kept.astype(jnp.bfloat16), ('section', 'y'), 0, 0)]
    ppermute x9 -> x10, starting transfers between devices: 3.86 us -> 3.96 us  [across(): return lax.ppermute(value, ('y', 'c'), [(d, d ^ r) for d in range(4)])]
  transfers between devices with their start and end apart: 23 -> 24, of which waited for: 12 -> 13; matrix products, arithmetic and copies ran while one was open for 2% -> 2% of each run, Pallas kernels for 5% -> 6%
where the time goes in v3:
time: 97.2 us; the launch traced here: 95.7 us
  blocking collectives  27.1 us (28%)
  starting transfers between devices  25.7 us (26%)
  waiting for transfers between devices  18.1 us (19%)
  Pallas kernels  17.9 us (18%)
  local copies, waits for them, and re-layouts  3.25 us (3%)
  other arithmetic  2.68 us (3%)
    ppermute x14, starting transfers between devices, along(): return lax.ppermute(value, 'z', [(d, (d + step) % 8) for d in range(8)])  21.8 us
    all_to_all x1, blocking collectives, body(): parts = lax.all_to_all(kept.astype(jnp.bfloat16), ('section', 'y'), 0, 0)  15 us
    all_to_all x1, blocking collectives, body(): states = lax.all_to_all(scan_windows(parts), 'section', 0, 0)  12.1 us
    pallas_call x2, Pallas kernels, correlate(): pl.pallas_call(functools.partial(correlate_kernel, h), out_shape=shapes,...  11.3 us
    ppermute x10, waiting for transfers between devices, across(): return lax.ppermute(value, ('y', 'c'), [(d, d ^ r) for d in range(4)])  10.9 us
    ppermute x14, waiting for transfers between devices, along(): return lax.ppermute(value, 'z', [(d, (d + step) % 8) for d in range(8)])  7.22 us
    pallas_call x1, Pallas kernels, spectrum(): pl.pallas_call(spectrum_kernel, out_shape=shapes, in_specs=[pl.BlockSpec(...  4.84 us
    ppermute x10, starting transfers between devices, across(): return lax.ppermute(value, ('y', 'c'), [(d, d ^ r) for d in range(4)])  3.96 us
  transfers between devices with their start and end apart: 24, of which 13 were waited for; matrix products, arithmetic and copies ran while one was open for 2% of the time, Pallas kernels for 6%

profile of v3, /device:TPU:6, one launch (start us, length us, event | category | flops | bytes accessed | tf_op | source)
XLA Modules:
  0.0 95.7 jit_solution(7633696563544004798)
XLA Ops:
  0.0 4.8 %spectrum.1 = (bf16[128,128]{1,0:T(8,128)(2,1)}, bf16[136,128]{1,0:T(8,128)(2,1)}, bf16[128,128]{1,0:T(8,128)(2,1)}, bf16[136,128]{1,0:T(8,128)(2,1)}, bf16[128,...) custom-call(s32[1,8,8]{2,1,0:T(8,128)} %mask_ref.1, ...), custom_call_target="tpu_custom_call" | custom-call | tf_op jit(solution)/shard_map/spectrum/pallas_call | solution.py:198
  4.8 0.0 collective-permute-start.3
  4.9 1.7 %collective-permute-start.4 = (bf16[136,128]{1,0:T(8,128)(2,1)}, bf16[136,128]{1,0:T(8,128)(2,1)S(1)}, u32[]{:S(2)}, u32[]{:S(2)}) collective-permute-start(bf16[136,128]{1,0:T(8,128)(2,1)} %get-tuple-element.17), channel_id=1, source_target_pairs={{0,2},{1,3},{2,0},{3,1},{4,6},{5,7},{6,4},{7,5},{8,10},{9,11},{10,... | collective-permute-start | bytes 104456 | tf_op jit(solution)/shard_map/ppermute | solution.py:367
  6.6 0.2 collective-permute-start.5
  6.7 0.4 collective-permute-start.13
  7.1 1.6 %collective-permute-start.14 = (bf16[128,128]{1,0:T(8,128)(2,1)}, bf16[128,128]{1,0:T(8,128)(2,1)S(1)}, u32[]{:S(2)}, u32[]{:S(2)}) collective-permute-start(bf16[128,128]{1,0:T(8,128)(2,1)} %get-tuple-element.21), channel_id=1, source_target_pairs={{0,2},{1,3},{2,0},{3,1},{4,6},{5,7},{6,4},{7,5},{8,10},{9,11},{10,... | collective-permute-start | bytes 98312 | tf_op jit(solution)/shard_map/ppermute | solution.py:367
  8.7 0.0 collective-permute-done.3
  8.7 0.0 collective-permute-start.15
  8.7 0.4 collective-permute-done.4
  9.1 1.1 %collective-permute-done.5 = bf16[136,128]{1,0:T(8,128)(2,1)S(1)} collective-permute-done((bf16[136,128]{1,0:T(8,128)(2,1)}, bf16[136,128]{1,0:T(8,128)(2,1)S(1)}, u32[]{:S(2)}, u32[]{:S(2)}) %collective-permute-start.5) | collective-permute-done | bytes 34848 | tf_op jit(solution)/shard_map/ppermute | solution.py:367
  10.2 0.8 pad_maximum_fusion.refs_4_
  11.0 0.0 copy-start
  11.0 5.9 %collective-permute-start.6 = (bf16[4,136,128]{2,1,0:T(8,128)(2,1)S(1)}, bf16[4,136,128]{2,1,0:T(8,128)(2,1)S(1)}, u32[]{:S(2)}, u32[]{:S(2)}) collective-permute-start(bf16[4,136,128]{2,1,0:T(8,128)(2,1)S(1)} %pad_maximum_fusion.refs_4_), channel_id=1, source_target_pairs={{0,28},{4,0},{8,4},{12,8},{16,12},{20,16},{24,20},{28,24},{1,29},{... | collective-permute-start | bytes 417800 | tf_op jit(solution)/shard_map/ppermute | solution.py:371
  16.9 0.0 collective-permute-done.13
  16.9 0.0 collective-permute-done.14
  16.9 0.0 collective-permute-done.15
  16.9 0.8 pad_maximum_fusion.1.refs_4_
  17.7 0.1 collective-permute-start.19
  17.8 0.1 collective-permute-start.10
  17.9 2.6 %collective-permute-done.6.refs_5_ = bf16[4,136,128]{2,1,0:T(8,128)(2,1)S(1)} collective-permute-done((bf16[4,136,128]{2,1,0:T(8,128)(2,1)S(1)}, bf16[4,136,128]{2,1,0:T(8,128)(2,1)S(1)}, u32[]{:S(2)}, u32[]{:S(2)}) %collective-permute-start.6) | collective-permute-done | bytes 139296 | tf_op jit(solution)/shard_map/ppermute | solution.py:371
  20.5 3.7 %collective-permute-start.7 = (bf16[4,136,128]{2,1,0:T(8,128)(2,1)S(1)}, bf16[4,136,128]{2,1,0:T(8,128)(2,1)S(1)}, u32[]{:S(2)}, u32[]{:S(2)}) collective-permute-start(bf16[4,136,128]{2,1,0:T(8,128)(2,1)S(1)} %collective-permute-done.6.refs_5_), channel_id=1, source_target_pairs={{0,28},{4,0},{8,4},{12,8},{16,12},{20,16},{24,20},{28,24},{1,29},{... | collective-permute-start | bytes 417800 | tf_op jit(solution)/shard_map/ppermute | solution.py:371
  24.2 0.0 collective-permute-start.16
  24.2 1.2 %collective-permute-done.19.refs_11_ = bf16[4,128,128]{2,1,0:T(8,128)(2,1)S(1)} collective-permute-done((bf16[4,128,128]{2,1,0:T(8,128)(2,1)S(1)}, bf16[4,128,128]{2,1,0:T(8,128)(2,1)S(1)}, u32[]{:S(2)}, u32[]{:S(2)}) %collective-permute-start.19) | collective-permute-done | bytes 131104 | tf_op jit(solution)/shard_map/ppermute | solution.py:371
  25.4 0.8 collective-permute-start.20
  26.2 1.4 %collective-permute-done.10.refs_11_ = bf16[4,136,128]{2,1,0:T(8,128)(2,1)S(1)} collective-permute-done((bf16[4,136,128]{2,1,0:T(8,128)(2,1)S(1)}, bf16[4,136,128]{2,1,0:T(8,128)(2,1)S(1)}, u32[]{:S(2)}, u32[]{:S(2)}) %collective-permute-start.10) | collective-permute-done | bytes 139296 | tf_op jit(solution)/shard_map/ppermute | solution.py:371
  27.6 0.0 collective-permute-start.11
  27.6 0.6 collective-permute-done.7.refs_6_
  28.2 3.7 %collective-permute-start.8 = (bf16[4,136,128]{2,1,0:T(8,128)(2,1)S(1)}, bf16[4,136,128]{2,1,0:T(8,128)(2,1)S(1)}, u32[]{:S(2)}, u32[]{:S(2)}) collective-permute-start(bf16[4,136,128]{2,1,0:T(8,128)(2,1)S(1)} %collective-permute-done.7.refs_6_), channel_id=1, source_target_pairs={{0,28},{4,0},{8,4},{12,8},{16,12},{20,16},{24,20},{28,24},{1,29},{... | collective-permute-start | bytes 417800 | tf_op jit(solution)/shard_map/ppermute | solution.py:371
  31.9 0.0 collective-permute-done.16.refs_5_
  31.9 1.4 %collective-permute-start.17 = (bf16[4,128,128]{2,1,0:T(8,128)(2,1)S(1)}, bf16[4,128,128]{2,1,0:T(8,128)(2,1)S(1)}, u32[]{:S(2)}, u32[]{:S(2)}) collective-permute-start(bf16[4,128,128]{2,1,0:T(8,128)(2,1)S(1)} %collective-permute-done.16.refs_5_), channel_id=1, source_target_pairs={{0,28},{4,0},{8,4},{12,8},{16,12},{20,16},{24,20},{28,24},{1,29},{... | collective-permute-start | bytes 393224 | tf_op jit(solution)/shard_map/ppermute | solution.py:371
  33.3 0.0 collective-permute-done.20.refs_10_
  33.3 0.6 collective-permute-start.21
  33.9 0.6 collective-permute-done.11.refs_10_
  34.5 0.0 collective-permute-start.12
  34.6 0.5 collective-permute-done.8.refs_7_
  35.1 3.7 %collective-permute-start.9 = (bf16[4,136,128]{2,1,0:T(8,128)(2,1)S(1)}, bf16[4,136,128]{2,1,0:T(8,128)(2,1)S(1)}, u32[]{:S(2)}, u32[]{:S(2)}) collective-permute-start(bf16[4,136,128]{2,1,0:T(8,128)(2,1)S(1)} %collective-permute-done.8.refs_7_), channel_id=1, source_target_pairs={{0,28},{4,0},{8,4},{12,8},{16,12},{20,16},{24,20},{28,24},{1,29},{... | collective-permute-start | bytes 417800 | tf_op jit(solution)/shard_map/ppermute | solution.py:371
  38.8 0.0 collective-permute-done.17.refs_6_
  38.8 1.4 %collective-permute-start.18 = (bf16[4,128,128]{2,1,0:T(8,128)(2,1)S(1)}, bf16[4,128,128]{2,1,0:T(8,128)(2,1)S(1)}, u32[]{:S(2)}, u32[]{:S(2)}) collective-permute-start(bf16[4,128,128]{2,1,0:T(8,128)(2,1)S(1)} %collective-permute-done.17.refs_6_), channel_id=1, source_target_pairs={{0,28},{4,0},{8,4},{12,8},{16,12},{20,16},{24,20},{28,24},{1,29},{... | collective-permute-start | bytes 393224 | tf_op jit(solution)/shard_map/ppermute | solution.py:371
  40.2 0.3 collective-permute-done.21.refs_9_
  40.5 0.3 collective-permute-start.22
  40.8 0.0 collective-permute-start
  41.5 0.6 collective-permute-done.refs_1_
  42.1 0.0 collective-permute-start.1
  42.1 3.7 %collective-permute-done.1.refs_2_ = s32[1,4]{1,0:T(1,128)S(1)} collective-permute-done((s32[1,4]{1,0:T(1,128)}, s32[1,4]{1,0:T(1,128)S(1)}, u32[]{:S(2)}, u32[]{:S(2)}) %collective-permute-start.1) | collective-permute-done | bytes 48 | tf_op jit(solution)/shard_map/ppermute | solution.py:367
  45.8 0.0 collective-permute-start.2
  45.8 3.1 %collective-permute-done.2.refs_3_ = s32[1,4]{1,0:T(1,128)S(1)} collective-permute-done((s32[1,4]{1,0:T(1,128)}, s32[1,4]{1,0:T(1,128)S(1)}, u32[]{:S(2)}, u32[]{:S(2)}) %collective-permute-start.2) | collective-permute-done | bytes 48 | tf_op jit(solution)/shard_map/ppermute | solution.py:367
  48.9 0.0 collective-permute-done.18.refs_7_
  48.9 0.0 collective-permute-done.22.refs_8_
  49.0 0.5 copy-done.18
  49.5 0.1 copy-done.14
  49.6 0.7 copy-done.15
  50.2 5.4 %shard_map.73.refs_13_ = f32[1024,384]{1,0:T(8,128)} custom-call(f32[1]{0:T(128)S(6)} %copy.9.decay_ref, s32[1,4]{1,0:T(1,128)} %refs_0_.3, s32[1,4]{1,0:T(1,128)} %copy-done.16, s32[1,4]{1,0:T(1,128)} %copy-done.17, s32[1,4]{1,0:T(1,128)} %copy-done.18, bf16[4,128,128]{2,1,0:T(8,128)(2,1)} %copy-done.1, bf16[4,128,128]{2,1,0:T(8,128)(2,1)} %copy-done.10, ...), custom_call_target="tpu_custom_call" | custom-call | tf_op jit(solution)/shard_map/pallas_call | solution.py:322
  55.7 0.0 collective-permute-done.12.refs_9_
  55.8 0.0 collective-permute-done.9.refs_8_
  55.8 0.6 copy-done.7
  56.4 0.6 copy-done.8
  57.1 5.9 %shard_map.74 = (bf16[16,104,128]{2,1,0:T(8,128)(2,1)}, bf16[16,104,128]{2,1,0:T(8,128)(2,1)}) custom-call(f32[1]{0:T(128)S(6)} %copy.9.decay_ref, s32[1,4]{1,0:T(1,128)} %refs_0_.3, s32[1,4]{1,0:T(1,128)} %copy-done.16, s32[1,4]{1,0:T(1,128)} %copy-done.17, s32[1,4]{1,0:T(1,128)} %copy-done.18, bf16[4,136,128]{2,1,0:T(8,128)(2,1)} %copy-done, ...), custom_call_target="tpu_custom_call" | custom-call | tf_op jit(solution)/shard_map/pallas_call | solution.py:322
  62.9 0.1 collective-permute-start.23
  63.0 2.0 %collective-permute-done.23 = bf16[16,104,128]{2,1,0:T(8,128)(2,1)S(1)} collective-permute-done((bf16[16,104,128]{2,1,0:T(8,128)(2,1)}, bf16[16,104,128]{2,1,0:T(8,128)(2,1)S(1)}, u32[]{:S(2)}, u32[]{:S(2)}) %collective-permute-start.23) | collective-permute-done | bytes 426016 | tf_op jit(solution)/shard_map/ppermute | solution.py:367
  65.0 1.1 %add_convert_fusion = bf16[16,104,128]{2,1,0:T(8,128)(2,1)S(1)} fusion(bf16[16,104,128]{2,1,0:T(8,128)(2,1)S(1)} %collective-permute-done.23, bf16[16,104,128]{2,1,0:T(8,128)(2,1)} %get-tuple-element.23), kind=kLoop, calls=%fused_computation | loop fusion | flops 851968 | bytes 1277952 | tf_op jit(solution)/shard_map/convert_element_type | solution.py:394
  66.1 15.0 %all_to_all.10.parts = bf16[16,104,128]{2,1,0:T(8,128)(2,1)} all-to-all(bf16[16,104,128]{2,1,0:T(8,128)(2,1)S(1)} %add_convert_fusion), channel_id=1, replica_groups=mesh['section'=8,'z'=8,'y'=2,'c'=2] {'section','y'}, dimensions={0} | all-to-all | bytes 851968 | tf_op jit(solution)/shard_map/all_to_all | solution.py:394
  81.2 1.8 %scan.1 = bf16[8,32,384]{2,1,0:T(8,128)(2,1)} custom-call(bf16[16,104,128]{2,1,0:T(8,128)(2,1)} %all_to_all.10.parts), custom_call_target="tpu_custom_call" | custom-call | tf_op jit(solution)/shard_map/scan/pallas_call | solution.py:357
  82.9 12.1 %all_to_all.11 = bf16[8,32,384]{2,1,0:T(8,128)(2,1)S(1)} all-to-all(bf16[8,32,384]{2,1,0:T(8,128)(2,1)} %scan.1), channel_id=1, replica_groups=mesh['section'=8,'z'=8,'y'=2,'c'=2] {'section'}, dimensions={0} | all-to-all | bytes 393216 | tf_op jit(solution)/shard_map/all_to_all | solution.py:395
  95.0 0.7 copy.10
  (32 shorter events, 0.1 us)
Async XLA Ops:
  4.8 3.9 %collective-permute-start.3 = (bf16[136,128]{1,0:T(8,128)(2,1)}, bf16[136,128]{1,0:T(8,128)(2,1)S(1)}, u32[]{:S(2)}, u32[]{:S(2)}) collective-permute-start(bf16[136,128]{1,0:T(8,128)(2,1)} %get-tuple-element.16), channel_id=1, source_target_pairs={{0,1},{1,0},{2,3},{3,2},{4,5},{5,4},{6,7},{7,6},{8,9},{9,8},{10,11... | collective-permute-start | bytes 104456 | tf_op jit(solution)/shard_map/ppermute | solution.py:367
  4.9 4.2 %collective-permute-start.4 = (bf16[136,128]{1,0:T(8,128)(2,1)}, bf16[136,128]{1,0:T(8,128)(2,1)S(1)}, u32[]{:S(2)}, u32[]{:S(2)}) collective-permute-start(bf16[136,128]{1,0:T(8,128)(2,1)} %get-tuple-element.17), channel_id=1, source_target_pairs={{0,2},{1,3},{2,0},{3,1},{4,6},{5,7},{6,4},{7,5},{8,10},{9,11},{10,... | collective-permute-start | bytes 104456 | tf_op jit(solution)/shard_map/ppermute | solution.py:367
  6.6 3.6 %collective-permute-start.5 = (bf16[136,128]{1,0:T(8,128)(2,1)}, bf16[136,128]{1,0:T(8,128)(2,1)S(1)}, u32[]{:S(2)}, u32[]{:S(2)}) collective-permute-start(bf16[136,128]{1,0:T(8,128)(2,1)} %get-tuple-element.18), channel_id=1, source_target_pairs={{0,3},{1,2},{2,1},{3,0},{4,7},{5,6},{6,5},{7,4},{8,11},{9,10},{10,... | collective-permute-start | bytes 104456 | tf_op jit(solution)/shard_map/ppermute | solution.py:367
  6.7 10.2 %collective-permute-start.13 = (bf16[128,128]{1,0:T(8,128)(2,1)}, bf16[128,128]{1,0:T(8,128)(2,1)S(1)}, u32[]{:S(2)}, u32[]{:S(2)}) collective-permute-start(bf16[128,128]{1,0:T(8,128)(2,1)} %get-tuple-element.20), channel_id=1, source_target_pairs={{0,1},{1,0},{2,3},{3,2},{4,5},{5,4},{6,7},{7,6},{8,9},{9,8},{10,11... | collective-permute-start | bytes 98312 | tf_op jit(solution)/shard_map/ppermute | solution.py:367
  7.1 9.8 %collective-permute-start.14 = (bf16[128,128]{1,0:T(8,128)(2,1)}, bf16[128,128]{1,0:T(8,128)(2,1)S(1)}, u32[]{:S(2)}, u32[]{:S(2)}) collective-permute-start(bf16[128,128]{1,0:T(8,128)(2,1)} %get-tuple-element.21), channel_id=1, source_target_pairs={{0,2},{1,3},{2,0},{3,1},{4,6},{5,7},{6,4},{7,5},{8,10},{9,11},{10,... | collective-permute-start | bytes 98312 | tf_op jit(solution)/shard_map/ppermute | solution.py:367
  8.7 8.2 %collective-permute-start.15 = (bf16[128,128]{1,0:T(8,128)(2,1)}, bf16[128,128]{1,0:T(8,128)(2,1)S(1)}, u32[]{:S(2)}, u32[]{:S(2)}) collective-permute-start(bf16[128,128]{1,0:T(8,128)(2,1)} %get-tuple-element.22), channel_id=1, source_target_pairs={{0,3},{1,2},{2,1},{3,0},{4,7},{5,6},{6,5},{7,4},{8,11},{9,10},{10,... | collective-permute-start | bytes 98312 | tf_op jit(solution)/shard_map/ppermute | solution.py:367
  11.0 44.7 %copy-start = (bf16[4,136,128]{2,1,0:T(8,128)(2,1)}, bf16[4,136,128]{2,1,0:T(8,128)(2,1)S(1)}, u32[]{:S(2)}) copy-start(bf16[4,136,128]{2,1,0:T(8,128)(2,1)S(1)} %pad_maximum_fusion.refs_4_) | copy-start | bytes 417796
  11.0 9.5 %collective-permute-start.6 = (bf16[4,136,128]{2,1,0:T(8,128)(2,1)S(1)}, bf16[4,136,128]{2,1,0:T(8,128)(2,1)S(1)}, u32[]{:S(2)}, u32[]{:S(2)}) collective-permute-start(bf16[4,136,128]{2,1,0:T(8,128)(2,1)S(1)} %pad_maximum_fusion.refs_4_), channel_id=1, source_target_pairs={{0,28},{4,0},{8,4},{12,8},{16,12},{20,16},{24,20},{28,24},{1,29},{... | collective-permute-start | bytes 417800 | tf_op jit(solution)/shard_map/ppermute | solution.py:371
  17.7 31.2 %copy-start.1 = (bf16[4,128,128]{2,1,0:T(8,128)(2,1)}, bf16[4,128,128]{2,1,0:T(8,128)(2,1)S(1)}, u32[]{:S(2)}) copy-start(bf16[4,128,128]{2,1,0:T(8,128)(2,1)S(1)} %pad_maximum_fusion.1.refs_4_) | copy-start | bytes 393220
  17.7 7.7 %collective-permute-start.19 = (bf16[4,128,128]{2,1,0:T(8,128)(2,1)S(1)}, bf16[4,128,128]{2,1,0:T(8,128)(2,1)S(1)}, u32[]{:S(2)}, u32[]{:S(2)}) collective-permute-start(bf16[4,128,128]{2,1,0:T(8,128)(2,1)S(1)} %pad_maximum_fusion.1.refs_4_), channel_id=1, source_target_pairs={{0,4},{4,8},{8,12},{12,16},{16,20},{20,24},{24,28},{28,0},{1,5},{5... | collective-permute-start | bytes 393224 | tf_op jit(solution)/shard_map/ppermute | solution.py:371
  17.8 9.7 %collective-permute-start.10 = (bf16[4,136,128]{2,1,0:T(8,128)(2,1)S(1)}, bf16[4,136,128]{2,1,0:T(8,128)(2,1)S(1)}, u32[]{:S(2)}, u32[]{:S(2)}) collective-permute-start(bf16[4,136,128]{2,1,0:T(8,128)(2,1)S(1)} %pad_maximum_fusion.refs_4_), channel_id=1, source_target_pairs={{0,4},{4,8},{8,12},{12,16},{16,20},{20,24},{24,28},{28,0},{1,5},{5... | collective-permute-start | bytes 417800 | tf_op jit(solution)/shard_map/ppermute | solution.py:371
  20.5 35.2 %copy-start.2 = (bf16[4,136,128]{2,1,0:T(8,128)(2,1)}, bf16[4,136,128]{2,1,0:T(8,128)(2,1)S(1)}, u32[]{:S(2)}) copy-start(bf16[4,136,128]{2,1,0:T(8,128)(2,1)S(1)} %collective-permute-done.6.refs_5_) | copy-start | bytes 417796
  20.5 7.8 %collective-permute-start.7 = (bf16[4,136,128]{2,1,0:T(8,128)(2,1)S(1)}, bf16[4,136,128]{2,1,0:T(8,128)(2,1)S(1)}, u32[]{:S(2)}, u32[]{:S(2)}) collective-permute-start(bf16[4,136,128]{2,1,0:T(8,128)(2,1)S(1)} %collective-permute-done.6.refs_5_), channel_id=1, source_target_pairs={{0,28},{4,0},{8,4},{12,8},{16,12},{20,16},{24,20},{28,24},{1,29},{... | collective-permute-start | bytes 417800 | tf_op jit(solution)/shard_map/ppermute | solution.py:371
  24.2 7.8 %collective-permute-start.16 = (bf16[4,128,128]{2,1,0:T(8,128)(2,1)S(1)}, bf16[4,128,128]{2,1,0:T(8,128)(2,1)S(1)}, u32[]{:S(2)}, u32[]{:S(2)}) collective-permute-start(bf16[4,128,128]{2,1,0:T(8,128)(2,1)S(1)} %pad_maximum_fusion.1.refs_4_), channel_id=1, source_target_pairs={{0,28},{4,0},{8,4},{12,8},{16,12},{20,16},{24,20},{28,24},{1,29},{... | collective-permute-start | bytes 393224 | tf_op jit(solution)/shard_map/ppermute | solution.py:371
  25.4 23.6 %copy-start.9 = (bf16[4,128,128]{2,1,0:T(8,128)(2,1)}, bf16[4,128,128]{2,1,0:T(8,128)(2,1)S(1)}, u32[]{:S(2)}) copy-start(bf16[4,128,128]{2,1,0:T(8,128)(2,1)S(1)} %collective-permute-done.19.refs_11_) | copy-start | bytes 393220
  25.4 8.0 %collective-permute-start.20 = (bf16[4,128,128]{2,1,0:T(8,128)(2,1)S(1)}, bf16[4,128,128]{2,1,0:T(8,128)(2,1)S(1)}, u32[]{:S(2)}, u32[]{:S(2)}) collective-permute-start(bf16[4,128,128]{2,1,0:T(8,128)(2,1)S(1)} %collective-permute-done.19.refs_11_), channel_id=1, source_target_pairs={{0,4},{4,8},{8,12},{12,16},{16,20},{20,24},{24,28},{28,0},{1,5},{5... | collective-permute-start | bytes 393224 | tf_op jit(solution)/shard_map/ppermute | solution.py:371
  27.6 28.1 %copy-start.3 = (bf16[4,136,128]{2,1,0:T(8,128)(2,1)}, bf16[4,136,128]{2,1,0:T(8,128)(2,1)S(1)}, u32[]{:S(2)}) copy-start(bf16[4,136,128]{2,1,0:T(8,128)(2,1)S(1)} %collective-permute-done.10.refs_11_) | copy-start | bytes 417796
  27.6 7.0 %collective-permute-start.11 = (bf16[4,136,128]{2,1,0:T(8,128)(2,1)S(1)}, bf16[4,136,128]{2,1,0:T(8,128)(2,1)S(1)}, u32[]{:S(2)}, u32[]{:S(2)}) collective-permute-start(bf16[4,136,128]{2,1,0:T(8,128)(2,1)S(1)} %collective-permute-done.10.refs_11_), channel_id=1, source_target_pairs={{0,4},{4,8},{8,12},{12,16},{16,20},{20,24},{24,28},{28,0},{1,5},{5... | collective-permute-start | bytes 417800 | tf_op jit(solution)/shard_map/ppermute | solution.py:371
  28.2 27.5 %copy-start.4 = (bf16[4,136,128]{2,1,0:T(8,128)(2,1)}, bf16[4,136,128]{2,1,0:T(8,128)(2,1)S(1)}, u32[]{:S(2)}) copy-start(bf16[4,136,128]{2,1,0:T(8,128)(2,1)S(1)} %collective-permute-done.7.refs_6_) | copy-start | bytes 417796
  28.2 6.9 %collective-permute-start.8 = (bf16[4,136,128]{2,1,0:T(8,128)(2,1)S(1)}, bf16[4,136,128]{2,1,0:T(8,128)(2,1)S(1)}, u32[]{:S(2)}, u32[]{:S(2)}) collective-permute-start(bf16[4,136,128]{2,1,0:T(8,128)(2,1)S(1)} %collective-permute-done.7.refs_6_), channel_id=1, source_target_pairs={{0,28},{4,0},{8,4},{12,8},{16,12},{20,16},{24,20},{28,24},{1,29},{... | collective-permute-start | bytes 417800 | tf_op jit(solution)/shard_map/ppermute | solution.py:371
  31.9 17.1 %copy-start.10 = (bf16[4,128,128]{2,1,0:T(8,128)(2,1)}, bf16[4,128,128]{2,1,0:T(8,128)(2,1)S(1)}, u32[]{:S(2)}) copy-start(bf16[4,128,128]{2,1,0:T(8,128)(2,1)S(1)} %collective-permute-done.16.refs_5_) | copy-start | bytes 393220
  31.9 6.9 %collective-permute-start.17 = (bf16[4,128,128]{2,1,0:T(8,128)(2,1)S(1)}, bf16[4,128,128]{2,1,0:T(8,128)(2,1)S(1)}, u32[]{:S(2)}, u32[]{:S(2)}) collective-permute-start(bf16[4,128,128]{2,1,0:T(8,128)(2,1)S(1)} %collective-permute-done.16.refs_5_), channel_id=1, source_target_pairs={{0,28},{4,0},{8,4},{12,8},{16,12},{20,16},{24,20},{28,24},{1,29},{... | collective-permute-start | bytes 393224 | tf_op jit(solution)/shard_map/ppermute | solution.py:371
  33.3 15.6 %copy-start.11 = (bf16[4,128,128]{2,1,0:T(8,128)(2,1)}, bf16[4,128,128]{2,1,0:T(8,128)(2,1)S(1)}, u32[]{:S(2)}) copy-start(bf16[4,128,128]{2,1,0:T(8,128)(2,1)S(1)} %collective-permute-done.20.refs_10_) | copy-start | bytes 393220
  33.3 7.1 %collective-permute-start.21 = (bf16[4,128,128]{2,1,0:T(8,128)(2,1)S(1)}, bf16[4,128,128]{2,1,0:T(8,128)(2,1)S(1)}, u32[]{:S(2)}, u32[]{:S(2)}) collective-permute-start(bf16[4,128,128]{2,1,0:T(8,128)(2,1)S(1)} %collective-permute-done.20.refs_10_), channel_id=1, source_target_pairs={{0,4},{4,8},{8,12},{12,16},{16,20},{20,24},{24,28},{28,0},{1,5},{5... | collective-permute-start | bytes 393224 | tf_op jit(solution)/shard_map/ppermute | solution.py:371
  34.5 21.2 %copy-start.5 = (bf16[4,136,128]{2,1,0:T(8,128)(2,1)}, bf16[4,136,128]{2,1,0:T(8,128)(2,1)S(1)}, u32[]{:S(2)}) copy-start(bf16[4,136,128]{2,1,0:T(8,128)(2,1)S(1)} %collective-permute-done.11.refs_10_) | copy-start | bytes 417796
  34.5 21.2 %collective-permute-start.12 = (bf16[4,136,128]{2,1,0:T(8,128)(2,1)S(1)}, bf16[4,136,128]{2,1,0:T(8,128)(2,1)S(1)}, u32[]{:S(2)}, u32[]{:S(2)}) collective-permute-start(bf16[4,136,128]{2,1,0:T(8,128)(2,1)S(1)} %collective-permute-done.11.refs_10_), channel_id=1, source_target_pairs={{0,4},{4,8},{8,12},{12,16},{16,20},{20,24},{24,28},{28,0},{1,5},{5... | collective-permute-start | bytes 417800 | tf_op jit(solution)/shard_map/ppermute | solution.py:371
  35.1 20.7 %copy-start.6 = (bf16[4,136,128]{2,1,0:T(8,128)(2,1)}, bf16[4,136,128]{2,1,0:T(8,128)(2,1)S(1)}, u32[]{:S(2)}) copy-start(bf16[4,136,128]{2,1,0:T(8,128)(2,1)S(1)} %collective-permute-done.8.refs_7_) | copy-start | bytes 417796
  35.1 20.7 %collective-permute-start.9 = (bf16[4,136,128]{2,1,0:T(8,128)(2,1)S(1)}, bf16[4,136,128]{2,1,0:T(8,128)(2,1)S(1)}, u32[]{:S(2)}, u32[]{:S(2)}) collective-permute-start(bf16[4,136,128]{2,1,0:T(8,128)(2,1)S(1)} %collective-permute-done.8.refs_7_), channel_id=1, source_target_pairs={{0,28},{4,0},{8,4},{12,8},{16,12},{20,16},{24,20},{28,24},{1,29},{... | collective-permute-start | bytes 417800 | tf_op jit(solution)/shard_map/ppermute | solution.py:371
  38.8 10.2 %copy-start.12 = (bf16[4,128,128]{2,1,0:T(8,128)(2,1)}, bf16[4,128,128]{2,1,0:T(8,128)(2,1)S(1)}, u32[]{:S(2)}) copy-start(bf16[4,128,128]{2,1,0:T(8,128)(2,1)S(1)} %collective-permute-done.17.refs_6_) | copy-start | bytes 393220
  38.8 10.2 %collective-permute-start.18 = (bf16[4,128,128]{2,1,0:T(8,128)(2,1)S(1)}, bf16[4,128,128]{2,1,0:T(8,128)(2,1)S(1)}, u32[]{:S(2)}, u32[]{:S(2)}) collective-permute-start(bf16[4,128,128]{2,1,0:T(8,128)(2,1)S(1)} %collective-permute-done.17.refs_6_), channel_id=1, source_target_pairs={{0,28},{4,0},{8,4},{12,8},{16,12},{20,16},{24,20},{28,24},{1,29},{... | collective-permute-start | bytes 393224 | tf_op jit(solution)/shard_map/ppermute | solution.py:371
  40.5 8.5 %copy-start.13 = (bf16[4,128,128]{2,1,0:T(8,128)(2,1)}, bf16[4,128,128]{2,1,0:T(8,128)(2,1)S(1)}, u32[]{:S(2)}) copy-start(bf16[4,128,128]{2,1,0:T(8,128)(2,1)S(1)} %collective-permute-done.21.refs_9_) | copy-start | bytes 393220
  40.5 8.5 %collective-permute-start.22 = (bf16[4,128,128]{2,1,0:T(8,128)(2,1)S(1)}, bf16[4,128,128]{2,1,0:T(8,128)(2,1)S(1)}, u32[]{:S(2)}, u32[]{:S(2)}) collective-permute-start(bf16[4,128,128]{2,1,0:T(8,128)(2,1)S(1)} %collective-permute-done.21.refs_9_), channel_id=1, source_target_pairs={{0,4},{4,8},{8,12},{12,16},{16,20},{20,24},{24,28},{28,0},{1,5},{5... | collective-permute-start | bytes 393224 | tf_op jit(solution)/shard_map/ppermute | solution.py:371
  40.8 1.3 %collective-permute-start = (s32[1,4]{1,0:T(1,128)}, s32[1,4]{1,0:T(1,128)S(1)}, u32[]{:S(2)}, u32[]{:S(2)}) collective-permute-start(s32[1,4]{1,0:T(1,128)} %refs_0_.3), channel_id=1, source_target_pairs={{0,1},{1,0},{2,3},{3,2},{4,5},{5,4},{6,7},{7,6},{8,9},{9,8},{10,11... | collective-permute-start | bytes 56 | tf_op jit(solution)/shard_map/ppermute | solution.py:367
  42.1 6.9 %copy-start.16 = (s32[1,4]{1,0:T(1,128)}, s32[1,4]{1,0:T(1,128)S(1)}, u32[]{:S(2)}) copy-start(s32[1,4]{1,0:T(1,128)S(1)} %collective-permute-done.refs_1_) | copy-start | bytes 52
  42.1 3.7 %collective-permute-start.1 = (s32[1,4]{1,0:T(1,128)}, s32[1,4]{1,0:T(1,128)S(1)}, u32[]{:S(2)}, u32[]{:S(2)}) collective-permute-start(s32[1,4]{1,0:T(1,128)} %refs_0_.3), channel_id=1, source_target_pairs={{0,2},{1,3},{2,0},{3,1},{4,6},{5,7},{6,4},{7,5},{8,10},{9,11},{10,... | collective-permute-start | bytes 56 | tf_op jit(solution)/shard_map/ppermute | solution.py:367
  45.8 3.2 %copy-start.17 = (s32[1,4]{1,0:T(1,128)}, s32[1,4]{1,0:T(1,128)S(1)}, u32[]{:S(2)}) copy-start(s32[1,4]{1,0:T(1,128)S(1)} %collective-permute-done.1.refs_2_) | copy-start | bytes 52
  45.8 3.1 %collective-permute-start.2 = (s32[1,4]{1,0:T(1,128)}, s32[1,4]{1,0:T(1,128)S(1)}, u32[]{:S(2)}, u32[]{:S(2)}) collective-permute-start(s32[1,4]{1,0:T(1,128)} %refs_0_.3), channel_id=1, source_target_pairs={{0,3},{1,2},{2,1},{3,0},{4,7},{5,6},{6,5},{7,4},{8,11},{9,10},{10,... | collective-permute-start | bytes 56 | tf_op jit(solution)/shard_map/ppermute | solution.py:367
  48.9 0.6 copy-start.18
  48.9 0.6 copy-start.14
  49.6 0.7 copy-start.15
  55.8 0.7 copy-start.7
  56.4 0.6 copy-start.8
  62.9 2.1 %collective-permute-start.23 = (bf16[16,104,128]{2,1,0:T(8,128)(2,1)}, bf16[16,104,128]{2,1,0:T(8,128)(2,1)S(1)}, u32[]{:S(2)}, u32[]{:S(2)}) collective-permute-start(bf16[16,104,128]{2,1,0:T(8,128)(2,1)} %get-tuple-element.24), channel_id=1, source_target_pairs={{0,1},{1,0},{2,3},{3,2},{4,5},{5,4},{6,7},{7,6},{8,9},{9,8},{10,11... | collective-permute-start | bytes 1277960 | tf_op jit(solution)/shard_map/ppermute | solution.py:367

commit v4 on v3

--- a/solution.py
+++ b/solution.py
@@ -190,7 +190,7 @@
 
 def spectrum(waves, mask):
     shapes = [
-        jax.ShapeDtypeStruct((rows_of(h), 128), jnp.bfloat16)
+        pltpu.VMEM((rows_of(h), 128), jnp.bfloat16)
         for _ in range(4)
         for h in range(HALVES)
     ]
@@ -206,6 +206,7 @@
             pltpu.VMEM((2, 512, 128), jnp.float32),
             pltpu.VMEM((64, 128), jnp.float32),
         ],
+        compiler_params=pltpu.CompilerParams(vmem_limit_bytes=24 << 20),
         name="spectrum",
     )(mask, waves, jnp.asarray(twiddles()), jnp.asarray(second_dft()))
 
@@ -218,27 +219,20 @@
     (table_hbm,) = take(1)
     before = take(1)[0] if h else None
     outs = take(2) if last else take(1)
-    held, own, cross, total, inverse, table, spot, plane_sem, sem = take(9)
+    held, own, cross, total, inverse, table, spot, sem = take(8)
     z, mate = spots()
-    loads = [
-        pltpu.make_async_copy(planes[dz], held.at[pl.ds(4 * dz, 4)], plane_sem.at[dz])
-        for dz in range(8)
-    ]
-    fetches = [pltpu.make_async_copy(table_hbm.at[2 * mate + h], table, sem.at[0])]
-    if h:
-        fetches.append(pltpu.make_async_copy(before, total, sem.at[1]))
-    for copy in loads + fetches:
-        copy.start()
+    fetch = pltpu.make_async_copy(table_hbm.at[2 * mate + h], table, sem)
+    fetch.start()
     for r in range(4):
         for k in range(PB):
             p = pairs[r][0, k]
             dz = ((p // 4) - z + 8) % 8
             spot[(mate ^ r) * PB + k] = 4 * dz + ((p % 4) ^ mate)
-    loads[0].wait()
     for r in range(4):
-        own[r] = held[r].astype(jnp.float32)
-    for copy in loads[1:]:
-        copy.wait()
+        own[r] = planes[0][r].astype(jnp.float32)
+    for dz in range(8):
+        for r in range(4):
+            held[4 * dz + r] = planes[dz][r]
 
     def per_pair(step, carry):
         q, k = step // PB, step % PB
@@ -271,15 +265,14 @@
             inverse[...].astype(jnp.bfloat16), ones, preferred_element_type=jnp.float32
         )
         inverse[...] = 1.0 / jnp.maximum(count, 1.0)
-    for copy in fetches:
-        copy.wait()
+    fetch.wait()
     lagged = total if last else outs[0]
 
     def per_rows(step, carry):
         at = pl.ds(pl.multiple_of(step * 256, 256), 256)
         spectra = cross[at, :].astype(jnp.bfloat16)
         part = jnp.dot(spectra, table[...], preferred_element_type=jnp.float32)
-        lagged[at, :] = part + lagged[at, :] if h else part
+        lagged[at, :] = part + before[at, :] if h else part
         return carry
 
     lax.fori_loop(0, 4, per_rows, 0)
@@ -312,18 +305,24 @@
     return lax.broadcasted_iota(jnp.int32, (n, 128), 0)
 
 
+def held_in_vmem(arrays):
+    return [pltpu.with_memory_space_constraint(a, pltpu.VMEM) for a in arrays]
+
+
 def correlate(h, decay, pairs, planes, table, carried):
     last = h == HALVES - 1
     smem, vmem = pl.BlockSpec(memory_space=pltpu.SMEM), pl.BlockSpec(memory_space=pltpu.VMEM)
     if last:
-        shapes = [jax.ShapeDtypeStruct((16, 104, 128), jnp.bfloat16)] * 2
+        shapes = [pltpu.VMEM((16, 104, 128), jnp.bfloat16)] * 2
     else:
-        shapes = [jax.ShapeDtypeStruct((1024, LAGS), jnp.float32)]
+        shapes = [pltpu.VMEM((1024, LAGS), jnp.float32)]
     return pl.pallas_call(
         functools.partial(correlate_kernel, h),
         out_shape=shapes,
         in_specs=[smem] * 5
-        + [pl.BlockSpec(memory_space=pl.ANY)] * (9 + len(carried)),
+        + [vmem] * 8
+        + [pl.BlockSpec(memory_space=pl.ANY)]
+        + [vmem] * len(carried),
         out_specs=[vmem] * len(shapes),
         scratch_shapes=[
             pltpu.VMEM((32, rows_of(h), 128), jnp.bfloat16),
@@ -333,10 +332,16 @@
             pltpu.VMEM((1024 if last else 8, 128), jnp.float32),
             pltpu.VMEM((256, LAGS), jnp.bfloat16),
             pltpu.SMEM((4 * PB,), jnp.int32),
-            pltpu.SemaphoreType.DMA((8,)),
-            pltpu.SemaphoreType.DMA((2,)),
+            pltpu.SemaphoreType.DMA,
         ],
-    )(decay, *pairs, *planes, table, *carried)
+        compiler_params=pltpu.CompilerParams(vmem_limit_bytes=24 << 20),
+    )(
+        decay,
+        *pairs,
+        *held_in_vmem(planes),
+        pltpu.with_memory_space_constraint(table, pltpu.HBM),
+        *held_in_vmem(carried),
+    )
 
 
 def scan_kernel(parts, out):
@@ -359,6 +364,7 @@
         out_shape=jax.ShapeDtypeStruct((8, 32, LAGS), jnp.bfloat16),
         in_specs=[vmem],
         out_specs=vmem,
+        compiler_params=pltpu.CompilerParams(vmem_limit_bytes=24 << 20),
         name="scan",
     )(parts)
 
@@ -372,6 +378,7 @@
 
 
 def body(waveforms, segment_mask, pair_blocks, window_decay):
+    pair_blocks = jnp.maximum(pair_blocks, 0)
     pairs = [pair_blocks] + [across(pair_blocks, r) for r in (1, 2, 3)]
     flat = spectrum(waveforms[0], segment_mask)
     table = jnp.asarray(lag_table())

time: 97.2 us -> 90.6 us (0.932)
  Pallas kernels: 17.9 us -> 10.2 us
  starting transfers between devices: 25.7 us -> 27.9 us
  other arithmetic: 2.68 us -> 0.81 us
    pallas_call x2, Pallas kernels: 11.3 us -> 6.47 us  [correlate(): pl.pallas_call(functools.partial(correlate_kernel, h), out_shape=shapes,...]
    ppermute x14, starting transfers between devices: 21.8 us -> 23.8 us  [along(): return lax.ppermute(value, 'z', [(d, (d + step) % 8) for d in range(8)])]
    pallas_call x1, Pallas kernels: 1.77 us -> 0.08 us  [scan_windows(): pl.pallas_call(scan_kernel, out_shape=jax.ShapeDtypeStruct((8, 32, LAGS),...]
    another operation x2, other arithmetic: 1.56 us -> 0.04 us  [body(): plane = jnp.stack([mine[0]] + [across(mine[r], r) for r in (1, 2, 3)])]
    ppermute x14, waiting for transfers between devices: 7.22 us -> 8.61 us  [along(): return lax.ppermute(value, 'z', [(d, (d + step) % 8) for d in range(8)])]
    pallas_call x1, Pallas kernels: 4.84 us -> 3.68 us  [spectrum(): pl.pallas_call(spectrum_kernel, out_shape=shapes, in_specs=[pl.BlockSpec(...]
    convert_element_type x1, other arithmetic: 1.12 us -> 0.11 us  [body(): parts = lax.all_to_all(kept.astype(jnp.bfloat16), ('section', 'y'), 0, 0)]
    unnamed x39 -> x9, local copies, waits for them, and re-layouts: 3.25 us -> 4.11 us
  transfers between devices with their start and end apart: 24 -> 24, of which waited for: 13 -> 11; matrix products, arithmetic and copies ran while one was open for 2% -> 1% of each run, Pallas kernels for 6% -> 3%
where the time goes in v4:
time: 90.6 us; the launch traced here: 89.3 us
  starting transfers between devices  27.9 us (31%)
  blocking collectives  26.8 us (30%)
  waiting for transfers between devices  18.6 us (21%)
  Pallas kernels  10.2 us (11%)
  local copies, waits for them, and re-layouts  4.11 us (5%)
    ppermute x14, starting transfers between devices, along(): return lax.ppermute(value, 'z', [(d, (d + step) % 8) for d in range(8)])  23.8 us
    all_to_all x1, blocking collectives, body(): parts = lax.all_to_all(kept.astype(jnp.bfloat16), ('section', 'y'), 0, 0)  14.9 us
    all_to_all x1, blocking collectives, body(): states = lax.all_to_all(scan_windows(parts), 'section', 0, 0)  11.9 us
    ppermute x10, waiting for transfers between devices, across(): return lax.ppermute(value, ('y', 'c'), [(d, d ^ r) for d in range(4)])  10 us
    ppermute x14, waiting for transfers between devices, along(): return lax.ppermute(value, 'z', [(d, (d + step) % 8) for d in range(8)])  8.61 us
    pallas_call x2, Pallas kernels, correlate(): pl.pallas_call(functools.partial(correlate_kernel, h), out_shape=shapes,...  6.47 us
    unnamed x9, local copies, waits for them, and re-layouts  4.11 us
    ppermute x10, starting transfers between devices, across(): return lax.ppermute(value, ('y', 'c'), [(d, d ^ r) for d in range(4)])  4.07 us
  transfers between devices with their start and end apart: 24, of which 11 were waited for; matrix products, arithmetic and copies ran while one was open for 1% of the time, Pallas kernels for 3%

profile of v4, /device:TPU:6, one launch (start us, length us, event | category | flops | bytes accessed | tf_op | source)
XLA Modules:
  0.0 89.3 jit_solution(11908439605844247655)
XLA Ops:
  0.0 0.0 copy-start
  0.0 1.0 %copy-done = bf16[1,8,8,4096]{3,2,1,0:T(8,128)(2,1)S(1)} copy-done((bf16[1,8,8,4096]{3,2,1,0:T(8,128)(2,1)S(1)}, bf16[1,8,8,4096]{3,2,1,0:T(8,128)(2,1)}, u32[]{:S(2)}) %copy-start) | copy-done | bytes 524312
  1.0 0.0 copy-start.1
  1.0 0.9 %copy-done.1 = bf16[2,256,256]{2,1,0:T(8,128)(2,1)S(1)} copy-done((bf16[2,256,256]{2,1,0:T(8,128)(2,1)S(1)}, bf16[2,256,256]{2,1,0:T(8,128)(2,1)}, u32[]{:S(2)}) %copy-start.1) | copy-done | bytes 262168
  2.0 0.0 copy-start.2
  2.0 0.8 copy-done.2
  2.8 0.7 copy-done.3
  3.4 3.7 %spectrum.1 = (bf16[128,128]{1,0:T(8,128)(2,1)S(1)}, bf16[136,128]{1,0:T(8,128)(2,1)S(1)}, bf16[128,128]{1,0:T(8,128)(2,1)S(1)}, bf16[136,128]{1,0:T(8,128)(2,1)...) custom-call(s32[1,8,8]{2,1,0:T(8,128)S(1)} %copy-done.3, ...), custom_call_target="tpu_custom_call" | custom-call | tf_op jit(solution)/shard_map/spectrum/pallas_call | solution.py:198
  7.1 0.1 collective-permute-start.3
  7.2 1.7 %collective-permute-start.4 = (bf16[136,128]{1,0:T(8,128)(2,1)S(1)}, bf16[136,128]{1,0:T(8,128)(2,1)S(1)}, u32[]{:S(2)}, u32[]{:S(2)}) collective-permute-start(bf16[136,128]{1,0:T(8,128)(2,1)S(1)} %get-tuple-element.17), channel_id=1, source_target_pairs={{0,2},{1,3},{2,0},{3,1},{4,6},{5,7},{6,4},{7,5},{8,10},{9,11},{10,... | collective-permute-start | bytes 104456 | tf_op jit(solution)/shard_map/ppermute | solution.py:373
  8.9 0.2 collective-permute-start.5
  9.1 0.4 collective-permute-start.13
  9.5 1.6 %collective-permute-start.14 = (bf16[128,128]{1,0:T(8,128)(2,1)S(1)}, bf16[128,128]{1,0:T(8,128)(2,1)S(1)}, u32[]{:S(2)}, u32[]{:S(2)}) collective-permute-start(bf16[128,128]{1,0:T(8,128)(2,1)S(1)} %get-tuple-element.21), channel_id=1, source_target_pairs={{0,2},{1,3},{2,0},{3,1},{4,6},{5,7},{6,4},{7,5},{8,10},{9,11},{10,... | collective-permute-start | bytes 98312 | tf_op jit(solution)/shard_map/ppermute | solution.py:373
  11.0 0.0 collective-permute-done.3
  11.0 0.0 collective-permute-start.15
  11.0 0.2 collective-permute-done.4
  11.2 1.1 %collective-permute-done.5 = bf16[136,128]{1,0:T(8,128)(2,1)S(1)} collective-permute-done((bf16[136,128]{1,0:T(8,128)(2,1)S(1)}, bf16[136,128]{1,0:T(8,128)(2,1)S(1)}, u32[]{:S(2)}, u32[]{:S(2)}) %collective-permute-start.5) | collective-permute-done | bytes 34848 | tf_op jit(solution)/shard_map/ppermute | solution.py:373
  12.3 5.9 %collective-permute-start.6 = (bf16[4,136,128]{2,1,0:T(8,128)(2,1)S(1)}, bf16[4,136,128]{2,1,0:T(8,128)(2,1)S(1)}, u32[]{:S(2)}, u32[]{:S(2)}) collective-permute-start(bf16[4,136,128]{2,1,0:T(8,128)(2,1)S(1)} %pad_maximum_fusion.refs_4_), channel_id=1, source_target_pairs={{0,28},{4,0},{8,4},{12,8},{16,12},{20,16},{24,20},{28,24},{1,29},{... | collective-permute-start | bytes 417800 | tf_op jit(solution)/shard_map/ppermute | solution.py:377
  18.3 0.0 collective-permute-done.13
  18.3 0.0 collective-permute-done.14
  18.3 0.0 collective-permute-done.15
  18.3 0.1 collective-permute-start.19
  18.4 0.2 collective-permute-start.10
  18.6 3.2 %collective-permute-done.6.refs_5_ = bf16[4,136,128]{2,1,0:T(8,128)(2,1)S(1)} collective-permute-done((bf16[4,136,128]{2,1,0:T(8,128)(2,1)S(1)}, bf16[4,136,128]{2,1,0:T(8,128)(2,1)S(1)}, u32[]{:S(2)}, u32[]{:S(2)}) %collective-permute-start.6) | collective-permute-done | bytes 139296 | tf_op jit(solution)/shard_map/ppermute | solution.py:377
  21.8 3.7 %collective-permute-start.7 = (bf16[4,136,128]{2,1,0:T(8,128)(2,1)S(1)}, bf16[4,136,128]{2,1,0:T(8,128)(2,1)S(1)}, u32[]{:S(2)}, u32[]{:S(2)}) collective-permute-start(bf16[4,136,128]{2,1,0:T(8,128)(2,1)S(1)} %collective-permute-done.6.refs_5_), channel_id=1, source_target_pairs={{0,28},{4,0},{8,4},{12,8},{16,12},{20,16},{24,20},{28,24},{1,29},{... | collective-permute-start | bytes 417800 | tf_op jit(solution)/shard_map/ppermute | solution.py:377
  25.5 0.0 collective-permute-start.16
  25.5 0.4 collective-permute-done.19.refs_11_
  26.0 1.6 %collective-permute-start.20 = (bf16[4,128,128]{2,1,0:T(8,128)(2,1)S(1)}, bf16[4,128,128]{2,1,0:T(8,128)(2,1)S(1)}, u32[]{:S(2)}, u32[]{:S(2)}) collective-permute-start(bf16[4,128,128]{2,1,0:T(8,128)(2,1)S(1)} %collective-permute-done.19.refs_11_), channel_id=1, source_target_pairs={{0,4},{4,8},{8,12},{12,16},{16,20},{20,24},{24,28},{28,0},{1,5},{5... | collective-permute-start | bytes 393224 | tf_op jit(solution)/shard_map/ppermute | solution.py:377
  27.5 0.6 collective-permute-done.10.refs_11_
  28.1 0.0 collective-permute-start.11
  28.1 1.4 %collective-permute-done.7.refs_6_ = bf16[4,136,128]{2,1,0:T(8,128)(2,1)S(1)} collective-permute-done((bf16[4,136,128]{2,1,0:T(8,128)(2,1)S(1)}, bf16[4,136,128]{2,1,0:T(8,128)(2,1)S(1)}, u32[]{:S(2)}, u32[]{:S(2)}) %collective-permute-start.7) | collective-permute-done | bytes 139296 | tf_op jit(solution)/shard_map/ppermute | solution.py:377
  29.6 3.7 %collective-permute-start.8 = (bf16[4,136,128]{2,1,0:T(8,128)(2,1)S(1)}, bf16[4,136,128]{2,1,0:T(8,128)(2,1)S(1)}, u32[]{:S(2)}, u32[]{:S(2)}) collective-permute-start(bf16[4,136,128]{2,1,0:T(8,128)(2,1)S(1)} %collective-permute-done.7.refs_6_), channel_id=1, source_target_pairs={{0,28},{4,0},{8,4},{12,8},{16,12},{20,16},{24,20},{28,24},{1,29},{... | collective-permute-start | bytes 417800 | tf_op jit(solution)/shard_map/ppermute | solution.py:377
  33.3 0.0 collective-permute-done.16.refs_5_
  33.3 1.7 %collective-permute-start.17 = (bf16[4,128,128]{2,1,0:T(8,128)(2,1)S(1)}, bf16[4,128,128]{2,1,0:T(8,128)(2,1)S(1)}, u32[]{:S(2)}, u32[]{:S(2)}) collective-permute-start(bf16[4,128,128]{2,1,0:T(8,128)(2,1)S(1)} %collective-permute-done.16.refs_5_), channel_id=1, source_target_pairs={{0,28},{4,0},{8,4},{12,8},{16,12},{20,16},{24,20},{28,24},{1,29},{... | collective-permute-start | bytes 393224 | tf_op jit(solution)/shard_map/ppermute | solution.py:377
  35.0 0.0 collective-permute-done.20.refs_10_
  35.0 0.3 collective-permute-start.21
  35.3 2.9 %collective-permute-done.17.refs_6_ = bf16[4,128,128]{2,1,0:T(8,128)(2,1)S(1)} collective-permute-done((bf16[4,128,128]{2,1,0:T(8,128)(2,1)S(1)}, bf16[4,128,128]{2,1,0:T(8,128)(2,1)S(1)}, u32[]{:S(2)}, u32[]{:S(2)}) %collective-permute-start.17) | collective-permute-done | bytes 131104 | tf_op jit(solution)/shard_map/ppermute | solution.py:377
  38.2 3.3 %collective-permute-start.18 = (bf16[4,128,128]{2,1,0:T(8,128)(2,1)S(1)}, bf16[4,128,128]{2,1,0:T(8,128)(2,1)S(1)}, u32[]{:S(2)}, u32[]{:S(2)}) collective-permute-start(bf16[4,128,128]{2,1,0:T(8,128)(2,1)S(1)} %collective-permute-done.17.refs_6_), channel_id=1, source_target_pairs={{0,28},{4,0},{8,4},{12,8},{16,12},{20,16},{24,20},{28,24},{1,29},{... | collective-permute-start | bytes 393224 | tf_op jit(solution)/shard_map/ppermute | solution.py:377
  41.5 0.0 collective-permute-done.11.refs_10_
  41.5 0.0 collective-permute-start.12
  41.5 0.0 collective-permute-done.21.refs_9_
  41.5 0.1 collective-permute-start.22
  41.6 0.0 collective-permute-done.8.refs_7_
  41.6 3.2 %collective-permute-start.9 = (bf16[4,136,128]{2,1,0:T(8,128)(2,1)S(1)}, bf16[4,136,128]{2,1,0:T(8,128)(2,1)S(1)}, u32[]{:S(2)}, u32[]{:S(2)}) collective-permute-start(bf16[4,136,128]{2,1,0:T(8,128)(2,1)S(1)} %collective-permute-done.8.refs_7_), channel_id=1, source_target_pairs={{0,28},{4,0},{8,4},{12,8},{16,12},{20,16},{24,20},{28,24},{1,29},{... | collective-permute-start | bytes 417800 | tf_op jit(solution)/shard_map/ppermute | solution.py:377
  44.8 0.7 broadcast_maximum_fusion.refs_0_
  45.5 0.0 collective-permute-start
  46.2 0.5 collective-permute-done.refs_1_
  46.7 0.1 collective-permute-start.1
  46.7 3.5 %collective-permute-done.1.refs_2_ = s32[1,4]{1,0:T(1,128)S(1)} collective-permute-done((s32[1,4]{1,0:T(1,128)S(1)}, s32[1,4]{1,0:T(1,128)S(1)}, u32[]{:S(2)}, u32[]{:S(2)}) %collective-permute-start.1) | collective-permute-done | bytes 48 | tf_op jit(solution)/shard_map/ppermute | solution.py:373
  50.2 0.0 collective-permute-start.2
  50.2 3.0 %collective-permute-done.2.refs_3_ = s32[1,4]{1,0:T(1,128)S(1)} collective-permute-done((s32[1,4]{1,0:T(1,128)S(1)}, s32[1,4]{1,0:T(1,128)S(1)}, u32[]{:S(2)}, u32[]{:S(2)}) %collective-permute-start.2) | collective-permute-done | bytes 48 | tf_op jit(solution)/shard_map/ppermute | solution.py:373
  53.2 0.0 collective-permute-done.18.refs_7_
  53.2 0.0 collective-permute-done.22.refs_8_
  53.2 2.9 %shard_map.73.refs_13_ = f32[1024,384]{1,0:T(8,128)S(1)} custom-call(f32[1]{0:T(128)S(6)} %copy.9.decay_ref, s32[1,4]{1,0:T(1,128)S(1)} %broadcast_maximum_fusion.refs_0_, s32[1,4]{1,0:T(1,128)S(1)} %collective-permute-done.refs_1_, s32[1,4]{1,0:T(1,128)S(1)} %collective-permute-done.1.refs_2_, s32[1,4]{1,0:T(1,128)S(1)} %collective-permute-done.2.refs_3_, ...), custom_call_target="tpu_custom_call" | custom-call | tf_op jit(solution)/shard_map/pallas_call | solution.py:319
  56.2 0.0 collective-permute-done.12.refs_9_
  56.2 0.0 collective-permute-done.9.refs_8_
  56.2 3.5 %shard_map.74 = (bf16[16,104,128]{2,1,0:T(8,128)(2,1)S(1)}, bf16[16,104,128]{2,1,0:T(8,128)(2,1)S(1)}) custom-call(f32[1]{0:T(128)S(6)} %copy.9.decay_ref, s32[1,4]{1,0:T(1,128)S(1)} %broadcast_maximum_fusion.refs_0_, s32[1,4]{1,0:T(1,128)S(1)} %collective-permute-done.refs_1_, s32[1,4]{1,0:T(1,128)S(1)} %collective-permute-done.1.refs_2_, ...), custom_call_target="tpu_custom_call" | custom-call | tf_op jit(solution)/shard_map/pallas_call | solution.py:319
  59.7 0.1 collective-permute-start.23
  59.8 1.8 %collective-permute-done.23 = bf16[16,104,128]{2,1,0:T(8,128)(2,1)S(1)} collective-permute-done((bf16[16,104,128]{2,1,0:T(8,128)(2,1)S(1)}, bf16[16,104,128]{2,1,0:T(8,128)(2,1)S(1)}, u32[]{:S(2)}, u32[]{:S(2)}) %collective-permute-start.23) | collective-permute-done | bytes 426016 | tf_op jit(solution)/shard_map/ppermute | solution.py:373
  61.6 0.1 add_convert_fusion
  61.7 14.9 %all_to_all.10.parts = bf16[16,104,128]{2,1,0:T(8,128)(2,1)S(1)} all-to-all(bf16[16,104,128]{2,1,0:T(8,128)(2,1)S(1)} %add_convert_fusion), channel_id=1, replica_groups=mesh['section'=8,'z'=8,'y'=2,'c'=2] {'section','y'}, dimensions={0} | all-to-all | bytes 851968 | tf_op jit(solution)/shard_map/all_to_all | solution.py:401
  76.6 0.1 scan.1
  76.7 11.9 %all_to_all.11 = bf16[8,32,384]{2,1,0:T(8,128)(2,1)S(1)} all-to-all(bf16[8,32,384]{2,1,0:T(8,128)(2,1)S(1)} %scan.1), channel_id=1, replica_groups=mesh['section'=8,'z'=8,'y'=2,'c'=2] {'section'}, dimensions={0} | all-to-all | bytes 393216 | tf_op jit(solution)/shard_map/all_to_all | solution.py:402
  88.6 0.7 copy.10
  (3 shorter events, 0.0 us)
Async XLA Ops:
  0.0 1.0 %copy-start = (bf16[1,8,8,4096]{3,2,1,0:T(8,128)(2,1)S(1)}, bf16[1,8,8,4096]{3,2,1,0:T(8,128)(2,1)}, u32[]{:S(2)}) copy-start(bf16[1,8,8,4096]{3,2,1,0:T(8,128)(2,1)} %param.7) | copy-start | bytes 1572868
  1.0 0.9 %copy-start.1 = (bf16[2,256,256]{2,1,0:T(8,128)(2,1)S(1)}, bf16[2,256,256]{2,1,0:T(8,128)(2,1)}, u32[]{:S(2)}) copy-start(bf16[2,256,256]{2,1,0:T(8,128)(2,1)} %constant.9.clone.dft_ref) | copy-start | bytes 786436
  2.0 0.8 copy-start.2
  2.8 0.7 copy-start.3
  7.1 3.9 %collective-permute-start.3 = (bf16[136,128]{1,0:T(8,128)(2,1)S(1)}, bf16[136,128]{1,0:T(8,128)(2,1)S(1)}, u32[]{:S(2)}, u32[]{:S(2)}) collective-permute-start(bf16[136,128]{1,0:T(8,128)(2,1)S(1)} %get-tuple-element.16), channel_id=1, source_target_pairs={{0,1},{1,0},{2,3},{3,2},{4,5},{5,4},{6,7},{7,6},{8,9},{9,8},{10,11... | collective-permute-start | bytes 104456 | tf_op jit(solution)/shard_map/ppermute | solution.py:373
  7.2 4.0 %collective-permute-start.4 = (bf16[136,128]{1,0:T(8,128)(2,1)S(1)}, bf16[136,128]{1,0:T(8,128)(2,1)S(1)}, u32[]{:S(2)}, u32[]{:S(2)}) collective-permute-start(bf16[136,128]{1,0:T(8,128)(2,1)S(1)} %get-tuple-element.17), channel_id=1, source_target_pairs={{0,2},{1,3},{2,0},{3,1},{4,6},{5,7},{6,4},{7,5},{8,10},{9,11},{10,... | collective-permute-start | bytes 104456 | tf_op jit(solution)/shard_map/ppermute | solution.py:373
  8.9 3.4 %collective-permute-start.5 = (bf16[136,128]{1,0:T(8,128)(2,1)S(1)}, bf16[136,128]{1,0:T(8,128)(2,1)S(1)}, u32[]{:S(2)}, u32[]{:S(2)}) collective-permute-start(bf16[136,128]{1,0:T(8,128)(2,1)S(1)} %get-tuple-element.18), channel_id=1, source_target_pairs={{0,3},{1,2},{2,1},{3,0},{4,7},{5,6},{6,5},{7,4},{8,11},{9,10},{10,... | collective-permute-start | bytes 104456 | tf_op jit(solution)/shard_map/ppermute | solution.py:373
  9.1 9.2 %collective-permute-start.13 = (bf16[128,128]{1,0:T(8,128)(2,1)S(1)}, bf16[128,128]{1,0:T(8,128)(2,1)S(1)}, u32[]{:S(2)}, u32[]{:S(2)}) collective-permute-start(bf16[128,128]{1,0:T(8,128)(2,1)S(1)} %get-tuple-element.20), channel_id=1, source_target_pairs={{0,1},{1,0},{2,3},{3,2},{4,5},{5,4},{6,7},{7,6},{8,9},{9,8},{10,11... | collective-permute-start | bytes 98312 | tf_op jit(solution)/shard_map/ppermute | solution.py:373
  9.5 8.8 %collective-permute-start.14 = (bf16[128,128]{1,0:T(8,128)(2,1)S(1)}, bf16[128,128]{1,0:T(8,128)(2,1)S(1)}, u32[]{:S(2)}, u32[]{:S(2)}) collective-permute-start(bf16[128,128]{1,0:T(8,128)(2,1)S(1)} %get-tuple-element.21), channel_id=1, source_target_pairs={{0,2},{1,3},{2,0},{3,1},{4,6},{5,7},{6,4},{7,5},{8,10},{9,11},{10,... | collective-permute-start | bytes 98312 | tf_op jit(solution)/shard_map/ppermute | solution.py:373
  11.0 7.2 %collective-permute-start.15 = (bf16[128,128]{1,0:T(8,128)(2,1)S(1)}, bf16[128,128]{1,0:T(8,128)(2,1)S(1)}, u32[]{:S(2)}, u32[]{:S(2)}) collective-permute-start(bf16[128,128]{1,0:T(8,128)(2,1)S(1)} %get-tuple-element.22), channel_id=1, source_target_pairs={{0,3},{1,2},{2,1},{3,0},{4,7},{5,6},{6,5},{7,4},{8,11},{9,10},{10,... | collective-permute-start | bytes 98312 | tf_op jit(solution)/shard_map/ppermute | solution.py:373
  12.3 9.5 %collective-permute-start.6 = (bf16[4,136,128]{2,1,0:T(8,128)(2,1)S(1)}, bf16[4,136,128]{2,1,0:T(8,128)(2,1)S(1)}, u32[]{:S(2)}, u32[]{:S(2)}) collective-permute-start(bf16[4,136,128]{2,1,0:T(8,128)(2,1)S(1)} %pad_maximum_fusion.refs_4_), channel_id=1, source_target_pairs={{0,28},{4,0},{8,4},{12,8},{16,12},{20,16},{24,20},{28,24},{1,29},{... | collective-permute-start | bytes 417800 | tf_op jit(solution)/shard_map/ppermute | solution.py:377
  18.3 7.7 %collective-permute-start.19 = (bf16[4,128,128]{2,1,0:T(8,128)(2,1)S(1)}, bf16[4,128,128]{2,1,0:T(8,128)(2,1)S(1)}, u32[]{:S(2)}, u32[]{:S(2)}) collective-permute-start(bf16[4,128,128]{2,1,0:T(8,128)(2,1)S(1)} %pad_maximum_fusion.1.refs_4_), channel_id=1, source_target_pairs={{0,4},{4,8},{8,12},{12,16},{16,20},{20,24},{24,28},{28,0},{1,5},{5... | collective-permute-start | bytes 393224 | tf_op jit(solution)/shard_map/ppermute | solution.py:377
  18.4 9.7 %collective-permute-start.10 = (bf16[4,136,128]{2,1,0:T(8,128)(2,1)S(1)}, bf16[4,136,128]{2,1,0:T(8,128)(2,1)S(1)}, u32[]{:S(2)}, u32[]{:S(2)}) collective-permute-start(bf16[4,136,128]{2,1,0:T(8,128)(2,1)S(1)} %pad_maximum_fusion.refs_4_), channel_id=1, source_target_pairs={{0,4},{4,8},{8,12},{12,16},{16,20},{20,24},{24,28},{28,0},{1,5},{5... | collective-permute-start | bytes 417800 | tf_op jit(solution)/shard_map/ppermute | solution.py:377
  21.8 7.8 %collective-permute-start.7 = (bf16[4,136,128]{2,1,0:T(8,128)(2,1)S(1)}, bf16[4,136,128]{2,1,0:T(8,128)(2,1)S(1)}, u32[]{:S(2)}, u32[]{:S(2)}) collective-permute-start(bf16[4,136,128]{2,1,0:T(8,128)(2,1)S(1)} %collective-permute-done.6.refs_5_), channel_id=1, source_target_pairs={{0,28},{4,0},{8,4},{12,8},{16,12},{20,16},{24,20},{28,24},{1,29},{... | collective-permute-start | bytes 417800 | tf_op jit(solution)/shard_map/ppermute | solution.py:377
  25.5 7.8 %collective-permute-start.16 = (bf16[4,128,128]{2,1,0:T(8,128)(2,1)S(1)}, bf16[4,128,128]{2,1,0:T(8,128)(2,1)S(1)}, u32[]{:S(2)}, u32[]{:S(2)}) collective-permute-start(bf16[4,128,128]{2,1,0:T(8,128)(2,1)S(1)} %pad_maximum_fusion.1.refs_4_), channel_id=1, source_target_pairs={{0,28},{4,0},{8,4},{12,8},{16,12},{20,16},{24,20},{28,24},{1,29},{... | collective-permute-start | bytes 393224 | tf_op jit(solution)/shard_map/ppermute | solution.py:377
  26.0 9.0 %collective-permute-start.20 = (bf16[4,128,128]{2,1,0:T(8,128)(2,1)S(1)}, bf16[4,128,128]{2,1,0:T(8,128)(2,1)S(1)}, u32[]{:S(2)}, u32[]{:S(2)}) collective-permute-start(bf16[4,128,128]{2,1,0:T(8,128)(2,1)S(1)} %collective-permute-done.19.refs_11_), channel_id=1, source_target_pairs={{0,4},{4,8},{8,12},{12,16},{16,20},{20,24},{24,28},{28,0},{1,5},{5... | collective-permute-start | bytes 393224 | tf_op jit(solution)/shard_map/ppermute | solution.py:377
  28.1 13.4 %collective-permute-start.11 = (bf16[4,136,128]{2,1,0:T(8,128)(2,1)S(1)}, bf16[4,136,128]{2,1,0:T(8,128)(2,1)S(1)}, u32[]{:S(2)}, u32[]{:S(2)}) collective-permute-start(bf16[4,136,128]{2,1,0:T(8,128)(2,1)S(1)} %collective-permute-done.10.refs_11_), channel_id=1, source_target_pairs={{0,4},{4,8},{8,12},{12,16},{16,20},{20,24},{24,28},{28,0},{1,5},{5... | collective-permute-start | bytes 417800 | tf_op jit(solution)/shard_map/ppermute | solution.py:377
  29.6 12.1 %collective-permute-start.8 = (bf16[4,136,128]{2,1,0:T(8,128)(2,1)S(1)}, bf16[4,136,128]{2,1,0:T(8,128)(2,1)S(1)}, u32[]{:S(2)}, u32[]{:S(2)}) collective-permute-start(bf16[4,136,128]{2,1,0:T(8,128)(2,1)S(1)} %collective-permute-done.7.refs_6_), channel_id=1, source_target_pairs={{0,28},{4,0},{8,4},{12,8},{16,12},{20,16},{24,20},{28,24},{1,29},{... | collective-permute-start | bytes 417800 | tf_op jit(solution)/shard_map/ppermute | solution.py:377
  33.3 5.0 %collective-permute-start.17 = (bf16[4,128,128]{2,1,0:T(8,128)(2,1)S(1)}, bf16[4,128,128]{2,1,0:T(8,128)(2,1)S(1)}, u32[]{:S(2)}, u32[]{:S(2)}) collective-permute-start(bf16[4,128,128]{2,1,0:T(8,128)(2,1)S(1)} %collective-permute-done.16.refs_5_), channel_id=1, source_target_pairs={{0,28},{4,0},{8,4},{12,8},{16,12},{20,16},{24,20},{28,24},{1,29},{... | collective-permute-start | bytes 393224 | tf_op jit(solution)/shard_map/ppermute | solution.py:377
  35.0 6.6 %collective-permute-start.21 = (bf16[4,128,128]{2,1,0:T(8,128)(2,1)S(1)}, bf16[4,128,128]{2,1,0:T(8,128)(2,1)S(1)}, u32[]{:S(2)}, u32[]{:S(2)}) collective-permute-start(bf16[4,128,128]{2,1,0:T(8,128)(2,1)S(1)} %collective-permute-done.20.refs_10_), channel_id=1, source_target_pairs={{0,4},{4,8},{8,12},{12,16},{16,20},{20,24},{24,28},{28,0},{1,5},{5... | collective-permute-start | bytes 393224 | tf_op jit(solution)/shard_map/ppermute | solution.py:377
  38.2 15.0 %collective-permute-start.18 = (bf16[4,128,128]{2,1,0:T(8,128)(2,1)S(1)}, bf16[4,128,128]{2,1,0:T(8,128)(2,1)S(1)}, u32[]{:S(2)}, u32[]{:S(2)}) collective-permute-start(bf16[4,128,128]{2,1,0:T(8,128)(2,1)S(1)} %collective-permute-done.17.refs_6_), channel_id=1, source_target_pairs={{0,28},{4,0},{8,4},{12,8},{16,12},{20,16},{24,20},{28,24},{1,29},{... | collective-permute-start | bytes 393224 | tf_op jit(solution)/shard_map/ppermute | solution.py:377
  41.5 14.7 %collective-permute-start.12 = (bf16[4,136,128]{2,1,0:T(8,128)(2,1)S(1)}, bf16[4,136,128]{2,1,0:T(8,128)(2,1)S(1)}, u32[]{:S(2)}, u32[]{:S(2)}) collective-permute-start(bf16[4,136,128]{2,1,0:T(8,128)(2,1)S(1)} %collective-permute-done.11.refs_10_), channel_id=1, source_target_pairs={{0,4},{4,8},{8,12},{12,16},{16,20},{20,24},{24,28},{28,0},{1,5},{5... | collective-permute-start | bytes 417800 | tf_op jit(solution)/shard_map/ppermute | solution.py:377
  41.5 11.7 %collective-permute-start.22 = (bf16[4,128,128]{2,1,0:T(8,128)(2,1)S(1)}, bf16[4,128,128]{2,1,0:T(8,128)(2,1)S(1)}, u32[]{:S(2)}, u32[]{:S(2)}) collective-permute-start(bf16[4,128,128]{2,1,0:T(8,128)(2,1)S(1)} %collective-permute-done.21.refs_9_), channel_id=1, source_target_pairs={{0,4},{4,8},{8,12},{12,16},{16,20},{20,24},{24,28},{28,0},{1,5},{5... | collective-permute-start | bytes 393224 | tf_op jit(solution)/shard_map/ppermute | solution.py:377
  41.6 14.6 %collective-permute-start.9 = (bf16[4,136,128]{2,1,0:T(8,128)(2,1)S(1)}, bf16[4,136,128]{2,1,0:T(8,128)(2,1)S(1)}, u32[]{:S(2)}, u32[]{:S(2)}) collective-permute-start(bf16[4,136,128]{2,1,0:T(8,128)(2,1)S(1)} %collective-permute-done.8.refs_7_), channel_id=1, source_target_pairs={{0,28},{4,0},{8,4},{12,8},{16,12},{20,16},{24,20},{28,24},{1,29},{... | collective-permute-start | bytes 417800 | tf_op jit(solution)/shard_map/ppermute | solution.py:377
  45.5 1.2 %collective-permute-start = (s32[1,4]{1,0:T(1,128)S(1)}, s32[1,4]{1,0:T(1,128)S(1)}, u32[]{:S(2)}, u32[]{:S(2)}) collective-permute-start(s32[1,4]{1,0:T(1,128)S(1)} %broadcast_maximum_fusion.refs_0_), channel_id=1, source_target_pairs={{0,1},{1,0},{2,3},{3,2},{4,5},{5,4},{6,7},{7,6},{8,9},{9,8},{10,11... | collective-permute-start | bytes 56 | tf_op jit(solution)/shard_map/ppermute | solution.py:373
  46.7 3.6 %collective-permute-start.1 = (s32[1,4]{1,0:T(1,128)S(1)}, s32[1,4]{1,0:T(1,128)S(1)}, u32[]{:S(2)}, u32[]{:S(2)}) collective-permute-start(s32[1,4]{1,0:T(1,128)S(1)} %broadcast_maximum_fusion.refs_0_), channel_id=1, source_target_pairs={{0,2},{1,3},{2,0},{3,1},{4,6},{5,7},{6,4},{7,5},{8,10},{9,11},{10,... | collective-permute-start | bytes 56 | tf_op jit(solution)/shard_map/ppermute | solution.py:373
  50.2 3.0 %collective-permute-start.2 = (s32[1,4]{1,0:T(1,128)S(1)}, s32[1,4]{1,0:T(1,128)S(1)}, u32[]{:S(2)}, u32[]{:S(2)}) collective-permute-start(s32[1,4]{1,0:T(1,128)S(1)} %broadcast_maximum_fusion.refs_0_), channel_id=1, source_target_pairs={{0,3},{1,2},{2,1},{3,0},{4,7},{5,6},{6,5},{7,4},{8,11},{9,10},{10,... | collective-permute-start | bytes 56 | tf_op jit(solution)/shard_map/ppermute | solution.py:373
  59.7 1.9 %collective-permute-start.23 = (bf16[16,104,128]{2,1,0:T(8,128)(2,1)S(1)}, bf16[16,104,128]{2,1,0:T(8,128)(2,1)S(1)}, u32[]{:S(2)}, u32[]{:S(2)}) collective-permute-start(bf16[16,104,128]{2,1,0:T(8,128)(2,1)S(1)} %get-tuple-element.24), channel_id=1, source_target_pairs={{0,1},{1,0},{2,3},{3,2},{4,5},{5,4},{6,7},{7,6},{8,9},{9,8},{10,11... | collective-permute-start | bytes 1277960 | tf_op jit(solution)/shard_map/ppermute | solution.py:373

commit v5 on v4

--- a/solution.py
+++ b/solution.py
@@ -94,15 +94,34 @@
 
 
 def spots():
-    return lax.axis_index("z"), 2 * lax.axis_index("y") + lax.axis_index("c")
-
-
-def spectrum_kernel(mask_ref, wave_ref, turn_ref, dft_ref, *refs):
-    outs, (mid, bins, white, marks) = refs[:-4], refs[-4:]
+    core = lax.axis_index("c")
+    return lax.axis_index("z"), 2 * lax.axis_index("y") + core, core
+
+
+def spectrum_kernel(mask_hbm, pair_hbm, wave_hbm, turn_hbm, dft_hbm, *refs):
+    outs, (mid, bins, white, marks) = refs[:-11], refs[-11:-7]
+    mask_ref, pair_ref, wave_ref, turn_ref, dft_ref, wave_sem, sem = refs[-7:]
+    turn_copy = pltpu.make_async_copy(turn_hbm, turn_ref, sem.at[0])
+    late = [
+        pltpu.make_async_copy(mask_hbm, mask_ref, sem.at[1]),
+        pltpu.make_async_copy(pair_hbm, pair_ref, sem.at[2]),
+        pltpu.make_async_copy(dft_hbm, dft_ref, sem.at[3]),
+    ]
+
+    def wave_copy(i):
+        return pltpu.make_async_copy(wave_hbm.at[i], wave_ref.at[i], wave_sem.at[i])
+
+    turn_copy.start()
+    for i in range(LS):
+        wave_copy(i).start()
+    for copy in late:
+        copy.start()
+    turn_copy.wait()
     lane_at = lax.broadcasted_iota(jnp.int32, (LS, 128), 1)
     row_at = lax.broadcasted_iota(jnp.int32, (LS, 128), 0)
 
     def station(i, carry):
+        wave_copy(i).wait()
         xs = [wave_ref[i, :, 128 * a : 128 * (a + 1)].astype(jnp.float32) for a in range(32)]
         half = real_fft(xs)
         for k in range(32):
@@ -119,15 +138,24 @@
             rows = pl.ds(pl.multiple_of(c * 64 + i * 8, 8), 8)
             mid[klo, rows, :128] = re
             mid[klo, rows, 128:] = jnp.zeros_like(re) if im is None else im
+        return carry
+
+    lax.fori_loop(0, LS, station, 0)
+    for copy in late:
+        copy.wait()
+
+    def masks(i, table):
         mark = jnp.zeros((SEGS, 128), jnp.float32)
         for e in range(SEGS):
             valid = mask_ref[0, i, e].astype(jnp.float32)
             mark = jnp.where(row_at == e, valid, mark)
-            carry = jnp.where((row_at == i) & (lane_at == e), valid, carry)
+            table = jnp.where((row_at == i) & (lane_at == e), valid, table)
         marks[pl.ds(pl.multiple_of(i * 8, 8), 8), :] = mark
-        return carry
-
-    table = lax.fori_loop(0, LS, station, jnp.zeros((LS, 128), jnp.float32))
+        return table
+
+    table = lax.fori_loop(0, LS, masks, jnp.zeros((LS, 128), jnp.float32))
+    for k in range(PB):
+        table = jnp.where(lane_at == SEGS + k, pair_ref[0, k].astype(jnp.float32), table)
     dot = functools.partial(jnp.dot, preferred_element_type=jnp.float32)
     bins[...] = jnp.zeros_like(bins)
 
@@ -172,7 +200,7 @@
         rows = slice(64 * c, 64 * (c + 1))
         white[0, rows, :] = re[rows] * scale
         white[1, rows, :] = im[rows] * scale
-    mate = spots()[1]
+    _, mate, _ = spots()
     for r in range(4):
         for h in range(HALVES):
             out = outs[r * HALVES + h]
@@ -188,46 +216,56 @@
     return 128 + 8 * (h == HALVES - 1)
 
 
-def spectrum(waves, mask):
+def spectrum(waves, mask, pairs):
     shapes = [
         pltpu.VMEM((rows_of(h), 128), jnp.bfloat16)
         for _ in range(4)
         for h in range(HALVES)
     ]
     vmem = pl.BlockSpec(memory_space=pltpu.VMEM)
+    args = [mask, pairs, waves, jnp.asarray(twiddles()), jnp.asarray(second_dft())]
     return pl.pallas_call(
         spectrum_kernel,
         out_shape=shapes,
-        in_specs=[pl.BlockSpec(memory_space=pltpu.SMEM)] + [vmem] * 3,
+        in_specs=[pl.BlockSpec(memory_space=pl.ANY)] * 5,
         out_specs=[vmem] * len(shapes),
         scratch_shapes=[
             pltpu.VMEM((4, 512, 256), jnp.float32),
             pltpu.VMEM((512, 256), jnp.float32),
             pltpu.VMEM((2, 512, 128), jnp.float32),
             pltpu.VMEM((64, 128), jnp.float32),
+            pltpu.SMEM((1, LS, SEGS), jnp.int32),
+            pltpu.SMEM((1, PB), jnp.int32),
+            pltpu.VMEM((LS, SEGS, NSAMP), jnp.bfloat16),
+            pltpu.VMEM((2, 32, 128), jnp.float32),
+            pltpu.VMEM((2, 256, 256), jnp.bfloat16),
+            pltpu.SemaphoreType.DMA((LS,)),
+            pltpu.SemaphoreType.DMA((4,)),
         ],
         compiler_params=pltpu.CompilerParams(vmem_limit_bytes=24 << 20),
         name="spectrum",
-    )(mask, waves, jnp.asarray(twiddles()), jnp.asarray(second_dft()))
-
-
-def correlate_kernel(h, decay_ref, *refs):
+    )(*[pltpu.with_memory_space_constraint(a, pltpu.HBM) for a in args])
+
+
+def correlate_kernel(h, side, decay_ref, pair_ref, *refs):
     last = h == HALVES - 1
     refs = list(refs)
     take = lambda n: [refs.pop(0) for _ in range(n)]
-    pairs, planes = take(4), take(8)
+    planes = take(8)
     (table_hbm,) = take(1)
-    before = take(1)[0] if h else None
-    outs = take(2) if last else take(1)
+    before = take(1)[0] if last else None
+    (out,) = take(1)
     held, own, cross, total, inverse, table, spot, sem = take(8)
-    z, mate = spots()
+    z, mate, core = spots()
+    sides = 1 if last else 2
     fetch = pltpu.make_async_copy(table_hbm.at[2 * mate + h], table, sem)
     fetch.start()
     for r in range(4):
+        q = mate ^ r
         for k in range(PB):
-            p = pairs[r][0, k]
+            p = pair_ref[r, k]
             dz = ((p // 4) - z + 8) % 8
-            spot[(mate ^ r) * PB + k] = 4 * dz + ((p % 4) ^ mate)
+            spot[q * PB + k] = 4 * dz + ((p % 4) ^ mate)
     for r in range(4):
         own[r] = planes[0][r].astype(jnp.float32)
     for dz in range(8):
@@ -235,8 +273,9 @@
             held[4 * dz + r] = planes[dz][r]
 
     def per_pair(step, carry):
-        q, k = step // PB, step % PB
-        theirs, mine = spot[step], q ^ mate
+        part, y, k = (side if last else step // 8), (step // PB) % 2, step % PB
+        q = 2 * y + (core ^ part)
+        theirs, mine = spot[q * PB + k], q ^ mate
         tiles = [held[theirs, 16 * e : 16 * e + 16, :].astype(jnp.float32) for e in range(SEGS)]
         if last:
             marks = held[theirs, 128:136, :].astype(jnp.float32)
@@ -251,51 +290,48 @@
                 real = add(real, mi * pi)
                 imag = add(imag, mr * pi)
                 imag = sub(imag, mi * pr)
-            at = pl.ds(pl.multiple_of(i * 128 + q * 32 + k * 8, 8), 8)
+            at = (step // 8) * 512 + i * 64 + y * 32 + k * 8
+            at = pl.ds(pl.multiple_of(at, 8), 8)
             cross[at, :128] = real
             cross[at, 128:] = imag
             if last:
                 inverse[at, :] = own[mine, 128 + i : 129 + i, :] * marks
         return carry
 
-    lax.fori_loop(0, 4 * PB, per_pair, 0)
+    lax.fori_loop(0, 8 * sides, per_pair, 0)
     if last:
-        ones = jnp.ones((128, 128), jnp.bfloat16)
-        count = jnp.dot(
-            inverse[...].astype(jnp.bfloat16), ones, preferred_element_type=jnp.float32
-        )
+        ones = jnp.where(row_of(128) < SEGS, 1.0, 0.0).astype(jnp.bfloat16)
+        valid = inverse[...].astype(jnp.bfloat16)
+        count = jnp.dot(valid, ones, preferred_element_type=jnp.float32)
         inverse[...] = 1.0 / jnp.maximum(count, 1.0)
     fetch.wait()
-    lagged = total if last else outs[0]
+    lagged = total if last else out
 
     def per_rows(step, carry):
         at = pl.ds(pl.multiple_of(step * 256, 256), 256)
         spectra = cross[at, :].astype(jnp.bfloat16)
         part = jnp.dot(spectra, table[...], preferred_element_type=jnp.float32)
-        lagged[at, :] = part + before[at, :] if h else part
+        if last:
+            part = part + before[pl.ds(pl.multiple_of(side * 512 + step * 256, 256), 256), :]
+        lagged[at, :] = part
         return carry
 
-    lax.fori_loop(0, 4, per_rows, 0)
+    lax.fori_loop(0, 2 * sides, per_rows, 0)
     if not last:
         return
     decay = jnp.full((8, 128), decay_ref[0], jnp.float32)
-    high = decay.astype(jnp.bfloat16)
-    low = (decay - high.astype(jnp.float32)).astype(jnp.bfloat16)
-    both = jnp.where(row_of(8) < 4, high.astype(jnp.float32), low.astype(jnp.float32))
-
-    core = mate % 2
+    high = decay.astype(jnp.bfloat16).astype(jnp.float32)
+    both = jnp.where(row_of(8) < 4, high, decay - high)
+    if side:
+        both = jnp.zeros_like(both)
 
     def per_part(n, carry):
-        i, y = n // 2, n % 2
-        for keep in range(2):
-            q = 2 * y + (core ^ keep)
-            at = pl.ds(pl.multiple_of(i * 128 + q * 32, 32), 32)
-            part = inverse[at, :]
-            for g in range(3):
-                value = total[at, 128 * g : 128 * (g + 1)] * part
-                outs[keep][n, 32 * g : 32 * (g + 1), :] = value.astype(jnp.bfloat16)
-            marks = jnp.zeros_like(both) if keep else both
-            outs[keep][n, 96:104, :] = marks.astype(jnp.bfloat16)
+        at = pl.ds(pl.multiple_of(n * 32, 32), 32)
+        part = inverse[at, :]
+        for g in range(3):
+            value = total[at, 128 * g : 128 * (g + 1)] * part
+            out[n, 32 * g : 32 * (g + 1), :] = value.astype(jnp.bfloat16)
+        out[n, 96:104, :] = both.astype(jnp.bfloat16)
         return carry
 
     lax.fori_loop(0, 16, per_part, 0)
@@ -309,27 +345,28 @@
     return [pltpu.with_memory_space_constraint(a, pltpu.VMEM) for a in arrays]
 
 
-def correlate(h, decay, pairs, planes, table, carried):
+def correlate(h, side, decay, pairs, planes, table, carried):
     last = h == HALVES - 1
     smem, vmem = pl.BlockSpec(memory_space=pltpu.SMEM), pl.BlockSpec(memory_space=pltpu.VMEM)
+    rows = 512 if last else 1024
     if last:
-        shapes = [pltpu.VMEM((16, 104, 128), jnp.bfloat16)] * 2
+        shape = pltpu.VMEM((16, 104, 128), jnp.bfloat16)
     else:
-        shapes = [pltpu.VMEM((1024, LAGS), jnp.float32)]
+        shape = pltpu.VMEM((1024, LAGS), jnp.float32)
     return pl.pallas_call(
-        functools.partial(correlate_kernel, h),
-        out_shape=shapes,
-        in_specs=[smem] * 5
+        functools.partial(correlate_kernel, h, side),
+        out_shape=shape,
+        in_specs=[smem] * 2
         + [vmem] * 8
         + [pl.BlockSpec(memory_space=pl.ANY)]
         + [vmem] * len(carried),
-        out_specs=[vmem] * len(shapes),
+        out_specs=vmem,
         scratch_shapes=[
             pltpu.VMEM((32, rows_of(h), 128), jnp.bfloat16),
             pltpu.VMEM((4, rows_of(h), 128), jnp.float32),
-            pltpu.VMEM((1024, 256), jnp.float32),
-            pltpu.VMEM((1024 if last else 8, LAGS), jnp.float32),
-            pltpu.VMEM((1024 if last else 8, 128), jnp.float32),
+            pltpu.VMEM((rows, 256), jnp.float32),
+            pltpu.VMEM((rows if last else 8, LAGS), jnp.float32),
+            pltpu.VMEM((rows if last else 8, 128), jnp.float32),
             pltpu.VMEM((256, LAGS), jnp.bfloat16),
             pltpu.SMEM((4 * PB,), jnp.int32),
             pltpu.SemaphoreType.DMA,
@@ -337,7 +374,7 @@
         compiler_params=pltpu.CompilerParams(vmem_limit_bytes=24 << 20),
     )(
         decay,
-        *pairs,
+        pairs,
         *held_in_vmem(planes),
         pltpu.with_memory_space_constraint(table, pltpu.HBM),
         *held_in_vmem(carried),
@@ -378,11 +415,9 @@
 
 
 def body(waveforms, segment_mask, pair_blocks, window_decay):
-    pair_blocks = jnp.maximum(pair_blocks, 0)
-    pairs = [pair_blocks] + [across(pair_blocks, r) for r in (1, 2, 3)]
-    flat = spectrum(waveforms[0], segment_mask)
+    flat = spectrum(waveforms[0], segment_mask, pair_blocks)
     table = jnp.asarray(lag_table())
-    carried = []
+    halves = []
     for h in range(HALVES):
         mine = [flat[r * HALVES + h] for r in range(4)]
         plane = jnp.stack([mine[0]] + [across(mine[r], r) for r in (1, 2, 3)])
@@ -395,8 +430,11 @@
             if step < 4 or h % 2 == 1:
                 back = along(back, -1)
                 planes[step] = back
-        carried = correlate(h, window_decay, pairs, planes, table, carried)
-    kept, sent = carried
+        halves.append(planes)
+    pairs = halves[1][0][:, 128, SEGS : SEGS + PB].astype(jnp.int32)
+    lagged = correlate(0, 0, window_decay, pairs, halves[0], table, [])
+    sent = correlate(1, 1, window_decay, pairs, halves[1], table, [lagged])
+    kept = correlate(1, 0, window_decay, pairs, halves[1], table, [lagged])
     kept = kept.astype(jnp.float32) + across(sent, 1).astype(jnp.float32)
     parts = lax.all_to_all(kept.astype(jnp.bfloat16), ("section", "y"), 0, 0)
     states = lax.all_to_all(scan_windows(parts), "section", 0, 0)

time: 90.6 us -> 83.2 us (0.918)
  waiting for transfers between devices: 18.6 us -> 13.5 us
  local copies, waits for them, and re-layouts: 4.11 us -> 0.68 us
  Pallas kernels: 10.2 us -> 11.9 us
    ppermute x10 -> x7, waiting for transfers between devices: 10 us -> 1.29 us  [across(): return lax.ppermute(value, ('y', 'c'), [(d, d ^ r) for d in range(4)])]
    ppermute x14, waiting for transfers between devices: 8.61 us -> 12.2 us  [along(): return lax.ppermute(value, 'z', [(d, (d + step) % 8) for d in range(8)])]
    unnamed x9 -> x1, local copies, waits for them, and re-layouts: 4.11 us -> 0.68 us
    pallas_call x2 -> x3, Pallas kernels: 6.47 us -> 7.64 us  [correlate(): pl.pallas_call(functools.partial(correlate_kernel, h, side), out_shape=sh...]
    ppermute x10 -> x7, starting transfers between devices: 4.07 us -> 3.99 us  [across(): return lax.ppermute(value, ('y', 'c'), [(d, d ^ r) for d in range(4)])]
  transfers between devices with their start and end apart: 24 -> 21, of which waited for: 11 -> 9; matrix products, arithmetic and copies ran while one was open for 1% -> 0% of each run, Pallas kernels for 3% -> 7%
where the time goes in v5:
time: 83.2 us; the launch traced here: 82.1 us
  starting transfers between devices  27.8 us (33%)
  blocking collectives  27.2 us (33%)
  waiting for transfers between devices  13.5 us (16%)
  Pallas kernels  11.9 us (14%)
    ppermute x14, starting transfers between devices, along(): return lax.ppermute(value, 'z', [(d, (d + step) % 8) for d in range(8)])  23.8 us
    all_to_all x1, blocking collectives, body(): parts = lax.all_to_all(kept.astype(jnp.bfloat16), ('section', 'y'), 0, 0)  15.3 us
    ppermute x14, waiting for transfers between devices, along(): return lax.ppermute(value, 'z', [(d, (d + step) % 8) for d in range(8)])  12.2 us
    all_to_all x1, blocking collectives, body(): states = lax.all_to_all(scan_windows(parts), 'section', 0, 0)  11.9 us
    pallas_call x3, Pallas kernels, correlate(): pl.pallas_call(functools.partial(correlate_kernel, h, side), out_shape=sh...  7.64 us
    pallas_call x1, Pallas kernels, spectrum(): pl.pallas_call(spectrum_kernel, out_shape=shapes, in_specs=[pl.BlockSpec(...  4.17 us
    ppermute x7, starting transfers between devices, across(): return lax.ppermute(value, ('y', 'c'), [(d, d ^ r) for d in range(4)])  3.99 us
  transfers between devices with their start and end apart: 21, of which 9 were waited for; matrix products, arithmetic and copies ran while one was open for 0% of the time, Pallas kernels for 7%

profile of v5, /device:TPU:6, one launch (start us, length us, event | category | flops | bytes accessed | tf_op | source)
XLA Modules:
  0.0 82.1 jit_solution(10274884521113473129)
XLA Ops:
  0.0 4.2 %spectrum.1 = (bf16[128,128]{1,0:T(8,128)(2,1)S(1)}, bf16[136,128]{1,0:T(8,128)(2,1)S(1)}, bf16[128,128]{1,0:T(8,128)(2,1)S(1)}, bf16[136,128]{1,0:T(8,128)(2,1)...) custom-call(s32[1,8,8]{2,1,0:T(8,128)} %mask_hbm.1, ...), custom_call_target="tpu_custom_call" | custom-call | tf_op jit(solution)/shard_map/spectrum/pallas_call | solution.py:227
  4.2 0.1 collective-permute-start
  4.3 1.7 %collective-permute-start.1 = (bf16[136,128]{1,0:T(8,128)(2,1)S(1)}, bf16[136,128]{1,0:T(8,128)(2,1)S(1)}, u32[]{:S(2)}, u32[]{:S(2)}) collective-permute-start(bf16[136,128]{1,0:T(8,128)(2,1)S(1)} %get-tuple-element.15), channel_id=1, source_target_pairs={{0,2},{1,3},{2,0},{3,1},{4,6},{5,7},{6,4},{7,5},{8,10},{9,11},{10,... | collective-permute-start | bytes 104456 | tf_op jit(solution)/shard_map/ppermute | solution.py:410
  5.9 0.2 collective-permute-start.2
  6.1 0.4 collective-permute-start.10
  6.5 1.6 %collective-permute-start.11 = (bf16[128,128]{1,0:T(8,128)(2,1)S(1)}, bf16[128,128]{1,0:T(8,128)(2,1)S(1)}, u32[]{:S(2)}, u32[]{:S(2)}) collective-permute-start(bf16[128,128]{1,0:T(8,128)(2,1)S(1)} %get-tuple-element.19), channel_id=1, source_target_pairs={{0,2},{1,3},{2,0},{3,1},{4,6},{5,7},{6,4},{7,5},{8,10},{9,11},{10,... | collective-permute-start | bytes 98312 | tf_op jit(solution)/shard_map/ppermute | solution.py:410
  8.1 0.0 collective-permute-done
  8.1 0.0 collective-permute-start.12
  8.1 0.2 collective-permute-done.1
  8.3 1.1 %collective-permute-done.2 = bf16[136,128]{1,0:T(8,128)(2,1)S(1)} collective-permute-done((bf16[136,128]{1,0:T(8,128)(2,1)S(1)}, bf16[136,128]{1,0:T(8,128)(2,1)S(1)}, u32[]{:S(2)}, u32[]{:S(2)}) %collective-permute-start.2) | collective-permute-done | bytes 34848 | tf_op jit(solution)/shard_map/ppermute | solution.py:410
  9.4 5.9 %collective-permute-start.3 = (bf16[4,136,128]{2,1,0:T(8,128)(2,1)S(1)}, bf16[4,136,128]{2,1,0:T(8,128)(2,1)S(1)}, u32[]{:S(2)}, u32[]{:S(2)}) collective-permute-start(bf16[4,136,128]{2,1,0:T(8,128)(2,1)S(1)} %pad_maximum_fusion.refs_0_), channel_id=1, source_target_pairs={{0,28},{4,0},{8,4},{12,8},{16,12},{20,16},{24,20},{28,24},{1,29},{... | collective-permute-start | bytes 417800 | tf_op jit(solution)/shard_map/ppermute | solution.py:414
  15.3 0.0 collective-permute-done.10
  15.3 0.0 collective-permute-done.11
  15.3 0.0 collective-permute-done.12
  15.4 0.1 collective-permute-start.16
  15.5 0.2 collective-permute-start.7
  15.7 3.2 %collective-permute-done.3.refs_1_ = bf16[4,136,128]{2,1,0:T(8,128)(2,1)S(1)} collective-permute-done((bf16[4,136,128]{2,1,0:T(8,128)(2,1)S(1)}, bf16[4,136,128]{2,1,0:T(8,128)(2,1)S(1)}, u32[]{:S(2)}, u32[]{:S(2)}) %collective-permute-start.3) | collective-permute-done | bytes 139296 | tf_op jit(solution)/shard_map/ppermute | solution.py:414
  18.9 3.7 %collective-permute-start.4 = (bf16[4,136,128]{2,1,0:T(8,128)(2,1)S(1)}, bf16[4,136,128]{2,1,0:T(8,128)(2,1)S(1)}, u32[]{:S(2)}, u32[]{:S(2)}) collective-permute-start(bf16[4,136,128]{2,1,0:T(8,128)(2,1)S(1)} %collective-permute-done.3.refs_1_), channel_id=1, source_target_pairs={{0,28},{4,0},{8,4},{12,8},{16,12},{20,16},{24,20},{28,24},{1,29},{... | collective-permute-start | bytes 417800 | tf_op jit(solution)/shard_map/ppermute | solution.py:414
  22.5 0.0 collective-permute-start.13
  22.6 0.4 collective-permute-done.16.refs_7_
  23.0 1.6 %collective-permute-start.17 = (bf16[4,128,128]{2,1,0:T(8,128)(2,1)S(1)}, bf16[4,128,128]{2,1,0:T(8,128)(2,1)S(1)}, u32[]{:S(2)}, u32[]{:S(2)}) collective-permute-start(bf16[4,128,128]{2,1,0:T(8,128)(2,1)S(1)} %collective-permute-done.16.refs_7_), channel_id=1, source_target_pairs={{0,4},{4,8},{8,12},{12,16},{16,20},{20,24},{24,28},{28,0},{1,5},{5... | collective-permute-start | bytes 393224 | tf_op jit(solution)/shard_map/ppermute | solution.py:414
  24.6 0.6 collective-permute-done.7.refs_7_
  25.2 0.0 collective-permute-start.8
  25.2 1.4 %collective-permute-done.4.refs_2_ = bf16[4,136,128]{2,1,0:T(8,128)(2,1)S(1)} collective-permute-done((bf16[4,136,128]{2,1,0:T(8,128)(2,1)S(1)}, bf16[4,136,128]{2,1,0:T(8,128)(2,1)S(1)}, u32[]{:S(2)}, u32[]{:S(2)}) %collective-permute-start.4) | collective-permute-done | bytes 139296 | tf_op jit(solution)/shard_map/ppermute | solution.py:414
  26.6 3.7 %collective-permute-start.5 = (bf16[4,136,128]{2,1,0:T(8,128)(2,1)S(1)}, bf16[4,136,128]{2,1,0:T(8,128)(2,1)S(1)}, u32[]{:S(2)}, u32[]{:S(2)}) collective-permute-start(bf16[4,136,128]{2,1,0:T(8,128)(2,1)S(1)} %collective-permute-done.4.refs_2_), channel_id=1, source_target_pairs={{0,28},{4,0},{8,4},{12,8},{16,12},{20,16},{24,20},{28,24},{1,29},{... | collective-permute-start | bytes 417800 | tf_op jit(solution)/shard_map/ppermute | solution.py:414
  30.3 0.0 collective-permute-done.13.refs_1_
  30.3 1.7 %collective-permute-start.14 = (bf16[4,128,128]{2,1,0:T(8,128)(2,1)S(1)}, bf16[4,128,128]{2,1,0:T(8,128)(2,1)S(1)}, u32[]{:S(2)}, u32[]{:S(2)}) collective-permute-start(bf16[4,128,128]{2,1,0:T(8,128)(2,1)S(1)} %collective-permute-done.13.refs_1_), channel_id=1, source_target_pairs={{0,28},{4,0},{8,4},{12,8},{16,12},{20,16},{24,20},{28,24},{1,29},{... | collective-permute-start | bytes 393224 | tf_op jit(solution)/shard_map/ppermute | solution.py:414
  32.0 0.0 collective-permute-done.17.refs_6_
  32.0 0.3 collective-permute-start.18
  33.0 2.3 %collective-permute-done.14.refs_2_ = bf16[4,128,128]{2,1,0:T(8,128)(2,1)S(1)} collective-permute-done((bf16[4,128,128]{2,1,0:T(8,128)(2,1)S(1)}, bf16[4,128,128]{2,1,0:T(8,128)(2,1)S(1)}, u32[]{:S(2)}, u32[]{:S(2)}) %collective-permute-start.14) | collective-permute-done | bytes 131104 | tf_op jit(solution)/shard_map/ppermute | solution.py:414
  35.3 3.3 %collective-permute-start.15 = (bf16[4,128,128]{2,1,0:T(8,128)(2,1)S(1)}, bf16[4,128,128]{2,1,0:T(8,128)(2,1)S(1)}, u32[]{:S(2)}, u32[]{:S(2)}) collective-permute-start(bf16[4,128,128]{2,1,0:T(8,128)(2,1)S(1)} %collective-permute-done.14.refs_2_), channel_id=1, source_target_pairs={{0,28},{4,0},{8,4},{12,8},{16,12},{20,16},{24,20},{28,24},{1,29},{... | collective-permute-start | bytes 393224 | tf_op jit(solution)/shard_map/ppermute | solution.py:414
  38.6 0.0 collective-permute-done.8.refs_6_
  38.6 0.0 collective-permute-start.9
  38.6 0.0 collective-permute-done.18.refs_5_
  38.6 0.1 collective-permute-start.19
  38.7 0.0 collective-permute-done.5.refs_3_
  38.7 3.2 %collective-permute-start.6 = (bf16[4,136,128]{2,1,0:T(8,128)(2,1)S(1)}, bf16[4,136,128]{2,1,0:T(8,128)(2,1)S(1)}, u32[]{:S(2)}, u32[]{:S(2)}) collective-permute-start(bf16[4,136,128]{2,1,0:T(8,128)(2,1)S(1)} %collective-permute-done.5.refs_3_), channel_id=1, source_target_pairs={{0,28},{4,0},{8,4},{12,8},{16,12},{20,16},{24,20},{28,24},{1,29},{... | collective-permute-start | bytes 417800 | tf_op jit(solution)/shard_map/ppermute | solution.py:414
  41.9 0.1 slice_convert_fusion
  42.0 0.2 collective-permute-done.15.refs_3_
  42.1 4.1 %collective-permute-done.19.refs_4_ = bf16[4,128,128]{2,1,0:T(8,128)(2,1)S(1)} collective-permute-done((bf16[4,128,128]{2,1,0:T(8,128)(2,1)S(1)}, bf16[4,128,128]{2,1,0:T(8,128)(2,1)S(1)}, u32[]{:S(2)}, u32[]{:S(2)}) %collective-permute-start.19) | collective-permute-done | bytes 131104 | tf_op jit(solution)/shard_map/ppermute | solution.py:414
  46.2 3.1 %shard_map.73.refs_9_ = f32[1024,384]{1,0:T(8,128)S(1)} custom-call(f32[1]{0:T(128)S(6)} %copy.9.decay_ref, s32[4,4]{1,0:T(4,128)S(1)} %bitcast.12, bf16[4,128,128]{2,1,0:T(8,128)(2,1)S(1)} %pad_maximum_fusion.1.refs_0_, bf16[4,128,128]{2,1,0:T(8,128)(2,1)S(1)} %collective-permute-done.13.refs_1_, bf16[4,128,128]{2,1,0:T(8,128)(2,1)S(1)} %collective-permute-done.14.refs_2_, ...), custom_call_target="tpu_custom_call" | custom-call | tf_op jit(solution)/shard_map/pallas_call | solution.py:356
  49.4 0.0 collective-permute-done.9.refs_5_
  49.4 0.0 collective-permute-done.6.refs_4_
  49.4 2.2 %shard_map.75 = bf16[16,104,128]{2,1,0:T(8,128)(2,1)S(1)} custom-call(f32[1]{0:T(128)S(6)} %copy.9.decay_ref, s32[4,4]{1,0:T(4,128)S(1)} %bitcast.13, bf16[4,136,128]{2,1,0:T(8,128)(2,1)S(1)} %pad_maximum_fusion.refs_0_, bf16[4,136,128]{2,1,0:T(8,128)(2,1)S(1)} %collective-permute-done.3.refs_1_, bf16[4,136,128]{2,1,0:T(8,128)(2,1)S(1)} %collective-permute-done.4.refs_2_, ...), custom_call_target="tpu_custom_call" | custom-call | tf_op jit(solution)/shard_map/pallas_call | solution.py:356
  51.7 0.1 collective-permute-start.20
  51.8 2.3 %shard_map.74 = bf16[16,104,128]{2,1,0:T(8,128)(2,1)S(1)} custom-call(f32[1]{0:T(128)S(6)} %copy.9.decay_ref, s32[4,4]{1,0:T(4,128)S(1)} %bitcast.14, bf16[4,136,128]{2,1,0:T(8,128)(2,1)S(1)} %pad_maximum_fusion.refs_0_, bf16[4,136,128]{2,1,0:T(8,128)(2,1)S(1)} %collective-permute-done.3.refs_1_, bf16[4,136,128]{2,1,0:T(8,128)(2,1)S(1)} %collective-permute-done.4.refs_2_, ...), custom_call_target="tpu_custom_call" | custom-call | tf_op jit(solution)/shard_map/pallas_call | solution.py:356
  54.0 0.0 collective-permute-done.20
  54.0 0.1 add_convert_fusion
  54.2 15.3 %all_to_all.10.parts = bf16[16,104,128]{2,1,0:T(8,128)(2,1)S(1)} all-to-all(bf16[16,104,128]{2,1,0:T(8,128)(2,1)S(1)} %add_convert_fusion), channel_id=1, replica_groups=mesh['section'=8,'z'=8,'y'=2,'c'=2] {'section','y'}, dimensions={0} | all-to-all | bytes 851968 | tf_op jit(solution)/shard_map/all_to_all | solution.py:439
  69.5 0.1 scan.1
  69.5 11.9 %all_to_all.11 = bf16[8,32,384]{2,1,0:T(8,128)(2,1)S(1)} all-to-all(bf16[8,32,384]{2,1,0:T(8,128)(2,1)S(1)} %scan.1), channel_id=1, replica_groups=mesh['section'=8,'z'=8,'y'=2,'c'=2] {'section'}, dimensions={0} | all-to-all | bytes 393216 | tf_op jit(solution)/shard_map/all_to_all | solution.py:440
  81.4 0.7 copy.10
  (2 shorter events, 0.0 us)
Async XLA Ops:
  4.2 3.9 %collective-permute-start = (bf16[136,128]{1,0:T(8,128)(2,1)S(1)}, bf16[136,128]{1,0:T(8,128)(2,1)S(1)}, u32[]{:S(2)}, u32[]{:S(2)}) collective-permute-start(bf16[136,128]{1,0:T(8,128)(2,1)S(1)} %get-tuple-element.14), channel_id=1, source_target_pairs={{0,1},{1,0},{2,3},{3,2},{4,5},{5,4},{6,7},{7,6},{8,9},{9,8},{10,11... | collective-permute-start | bytes 104456 | tf_op jit(solution)/shard_map/ppermute | solution.py:410
  4.3 4.0 %collective-permute-start.1 = (bf16[136,128]{1,0:T(8,128)(2,1)S(1)}, bf16[136,128]{1,0:T(8,128)(2,1)S(1)}, u32[]{:S(2)}, u32[]{:S(2)}) collective-permute-start(bf16[136,128]{1,0:T(8,128)(2,1)S(1)} %get-tuple-element.15), channel_id=1, source_target_pairs={{0,2},{1,3},{2,0},{3,1},{4,6},{5,7},{6,4},{7,5},{8,10},{9,11},{10,... | collective-permute-start | bytes 104456 | tf_op jit(solution)/shard_map/ppermute | solution.py:410
  5.9 3.4 %collective-permute-start.2 = (bf16[136,128]{1,0:T(8,128)(2,1)S(1)}, bf16[136,128]{1,0:T(8,128)(2,1)S(1)}, u32[]{:S(2)}, u32[]{:S(2)}) collective-permute-start(bf16[136,128]{1,0:T(8,128)(2,1)S(1)} %get-tuple-element.16), channel_id=1, source_target_pairs={{0,3},{1,2},{2,1},{3,0},{4,7},{5,6},{6,5},{7,4},{8,11},{9,10},{10,... | collective-permute-start | bytes 104456 | tf_op jit(solution)/shard_map/ppermute | solution.py:410
  6.1 9.2 %collective-permute-start.10 = (bf16[128,128]{1,0:T(8,128)(2,1)S(1)}, bf16[128,128]{1,0:T(8,128)(2,1)S(1)}, u32[]{:S(2)}, u32[]{:S(2)}) collective-permute-start(bf16[128,128]{1,0:T(8,128)(2,1)S(1)} %get-tuple-element.18), channel_id=1, source_target_pairs={{0,1},{1,0},{2,3},{3,2},{4,5},{5,4},{6,7},{7,6},{8,9},{9,8},{10,11... | collective-permute-start | bytes 98312 | tf_op jit(solution)/shard_map/ppermute | solution.py:410
  6.5 8.8 %collective-permute-start.11 = (bf16[128,128]{1,0:T(8,128)(2,1)S(1)}, bf16[128,128]{1,0:T(8,128)(2,1)S(1)}, u32[]{:S(2)}, u32[]{:S(2)}) collective-permute-start(bf16[128,128]{1,0:T(8,128)(2,1)S(1)} %get-tuple-element.19), channel_id=1, source_target_pairs={{0,2},{1,3},{2,0},{3,1},{4,6},{5,7},{6,4},{7,5},{8,10},{9,11},{10,... | collective-permute-start | bytes 98312 | tf_op jit(solution)/shard_map/ppermute | solution.py:410
  8.1 7.2 %collective-permute-start.12 = (bf16[128,128]{1,0:T(8,128)(2,1)S(1)}, bf16[128,128]{1,0:T(8,128)(2,1)S(1)}, u32[]{:S(2)}, u32[]{:S(2)}) collective-permute-start(bf16[128,128]{1,0:T(8,128)(2,1)S(1)} %get-tuple-element.20), channel_id=1, source_target_pairs={{0,3},{1,2},{2,1},{3,0},{4,7},{5,6},{6,5},{7,4},{8,11},{9,10},{10,... | collective-permute-start | bytes 98312 | tf_op jit(solution)/shard_map/ppermute | solution.py:410
  9.4 9.5 %collective-permute-start.3 = (bf16[4,136,128]{2,1,0:T(8,128)(2,1)S(1)}, bf16[4,136,128]{2,1,0:T(8,128)(2,1)S(1)}, u32[]{:S(2)}, u32[]{:S(2)}) collective-permute-start(bf16[4,136,128]{2,1,0:T(8,128)(2,1)S(1)} %pad_maximum_fusion.refs_0_), channel_id=1, source_target_pairs={{0,28},{4,0},{8,4},{12,8},{16,12},{20,16},{24,20},{28,24},{1,29},{... | collective-permute-start | bytes 417800 | tf_op jit(solution)/shard_map/ppermute | solution.py:414
  15.4 7.7 %collective-permute-start.16 = (bf16[4,128,128]{2,1,0:T(8,128)(2,1)S(1)}, bf16[4,128,128]{2,1,0:T(8,128)(2,1)S(1)}, u32[]{:S(2)}, u32[]{:S(2)}) collective-permute-start(bf16[4,128,128]{2,1,0:T(8,128)(2,1)S(1)} %pad_maximum_fusion.1.refs_0_), channel_id=1, source_target_pairs={{0,4},{4,8},{8,12},{12,16},{16,20},{20,24},{24,28},{28,0},{1,5},{5... | collective-permute-start | bytes 393224 | tf_op jit(solution)/shard_map/ppermute | solution.py:414
  15.5 9.7 %collective-permute-start.7 = (bf16[4,136,128]{2,1,0:T(8,128)(2,1)S(1)}, bf16[4,136,128]{2,1,0:T(8,128)(2,1)S(1)}, u32[]{:S(2)}, u32[]{:S(2)}) collective-permute-start(bf16[4,136,128]{2,1,0:T(8,128)(2,1)S(1)} %pad_maximum_fusion.refs_0_), channel_id=1, source_target_pairs={{0,4},{4,8},{8,12},{12,16},{16,20},{20,24},{24,28},{28,0},{1,5},{5... | collective-permute-start | bytes 417800 | tf_op jit(solution)/shard_map/ppermute | solution.py:414
  18.9 7.8 %collective-permute-start.4 = (bf16[4,136,128]{2,1,0:T(8,128)(2,1)S(1)}, bf16[4,136,128]{2,1,0:T(8,128)(2,1)S(1)}, u32[]{:S(2)}, u32[]{:S(2)}) collective-permute-start(bf16[4,136,128]{2,1,0:T(8,128)(2,1)S(1)} %collective-permute-done.3.refs_1_), channel_id=1, source_target_pairs={{0,28},{4,0},{8,4},{12,8},{16,12},{20,16},{24,20},{28,24},{1,29},{... | collective-permute-start | bytes 417800 | tf_op jit(solution)/shard_map/ppermute | solution.py:414
  22.5 7.8 %collective-permute-start.13 = (bf16[4,128,128]{2,1,0:T(8,128)(2,1)S(1)}, bf16[4,128,128]{2,1,0:T(8,128)(2,1)S(1)}, u32[]{:S(2)}, u32[]{:S(2)}) collective-permute-start(bf16[4,128,128]{2,1,0:T(8,128)(2,1)S(1)} %pad_maximum_fusion.1.refs_0_), channel_id=1, source_target_pairs={{0,28},{4,0},{8,4},{12,8},{16,12},{20,16},{24,20},{28,24},{1,29},{... | collective-permute-start | bytes 393224 | tf_op jit(solution)/shard_map/ppermute | solution.py:414
  23.0 9.0 %collective-permute-start.17 = (bf16[4,128,128]{2,1,0:T(8,128)(2,1)S(1)}, bf16[4,128,128]{2,1,0:T(8,128)(2,1)S(1)}, u32[]{:S(2)}, u32[]{:S(2)}) collective-permute-start(bf16[4,128,128]{2,1,0:T(8,128)(2,1)S(1)} %collective-permute-done.16.refs_7_), channel_id=1, source_target_pairs={{0,4},{4,8},{8,12},{12,16},{16,20},{20,24},{24,28},{28,0},{1,5},{5... | collective-permute-start | bytes 393224 | tf_op jit(solution)/shard_map/ppermute | solution.py:414
  25.2 13.4 %collective-permute-start.8 = (bf16[4,136,128]{2,1,0:T(8,128)(2,1)S(1)}, bf16[4,136,128]{2,1,0:T(8,128)(2,1)S(1)}, u32[]{:S(2)}, u32[]{:S(2)}) collective-permute-start(bf16[4,136,128]{2,1,0:T(8,128)(2,1)S(1)} %collective-permute-done.7.refs_7_), channel_id=1, source_target_pairs={{0,4},{4,8},{8,12},{12,16},{16,20},{20,24},{24,28},{28,0},{1,5},{5... | collective-permute-start | bytes 417800 | tf_op jit(solution)/shard_map/ppermute | solution.py:414
  26.6 12.1 %collective-permute-start.5 = (bf16[4,136,128]{2,1,0:T(8,128)(2,1)S(1)}, bf16[4,136,128]{2,1,0:T(8,128)(2,1)S(1)}, u32[]{:S(2)}, u32[]{:S(2)}) collective-permute-start(bf16[4,136,128]{2,1,0:T(8,128)(2,1)S(1)} %collective-permute-done.4.refs_2_), channel_id=1, source_target_pairs={{0,28},{4,0},{8,4},{12,8},{16,12},{20,16},{24,20},{28,24},{1,29},{... | collective-permute-start | bytes 417800 | tf_op jit(solution)/shard_map/ppermute | solution.py:414
  30.3 5.0 %collective-permute-start.14 = (bf16[4,128,128]{2,1,0:T(8,128)(2,1)S(1)}, bf16[4,128,128]{2,1,0:T(8,128)(2,1)S(1)}, u32[]{:S(2)}, u32[]{:S(2)}) collective-permute-start(bf16[4,128,128]{2,1,0:T(8,128)(2,1)S(1)} %collective-permute-done.13.refs_1_), channel_id=1, source_target_pairs={{0,28},{4,0},{8,4},{12,8},{16,12},{20,16},{24,20},{28,24},{1,29},{... | collective-permute-start | bytes 393224 | tf_op jit(solution)/shard_map/ppermute | solution.py:414
  32.0 6.6 %collective-permute-start.18 = (bf16[4,128,128]{2,1,0:T(8,128)(2,1)S(1)}, bf16[4,128,128]{2,1,0:T(8,128)(2,1)S(1)}, u32[]{:S(2)}, u32[]{:S(2)}) collective-permute-start(bf16[4,128,128]{2,1,0:T(8,128)(2,1)S(1)} %collective-permute-done.17.refs_6_), channel_id=1, source_target_pairs={{0,4},{4,8},{8,12},{12,16},{16,20},{20,24},{24,28},{28,0},{1,5},{5... | collective-permute-start | bytes 393224 | tf_op jit(solution)/shard_map/ppermute | solution.py:414
  35.3 6.9 %collective-permute-start.15 = (bf16[4,128,128]{2,1,0:T(8,128)(2,1)S(1)}, bf16[4,128,128]{2,1,0:T(8,128)(2,1)S(1)}, u32[]{:S(2)}, u32[]{:S(2)}) collective-permute-start(bf16[4,128,128]{2,1,0:T(8,128)(2,1)S(1)} %collective-permute-done.14.refs_2_), channel_id=1, source_target_pairs={{0,28},{4,0},{8,4},{12,8},{16,12},{20,16},{24,20},{28,24},{1,29},{... | collective-permute-start | bytes 393224 | tf_op jit(solution)/shard_map/ppermute | solution.py:414
  38.6 10.8 %collective-permute-start.9 = (bf16[4,136,128]{2,1,0:T(8,128)(2,1)S(1)}, bf16[4,136,128]{2,1,0:T(8,128)(2,1)S(1)}, u32[]{:S(2)}, u32[]{:S(2)}) collective-permute-start(bf16[4,136,128]{2,1,0:T(8,128)(2,1)S(1)} %collective-permute-done.8.refs_6_), channel_id=1, source_target_pairs={{0,4},{4,8},{8,12},{12,16},{16,20},{20,24},{24,28},{28,0},{1,5},{5... | collective-permute-start | bytes 417800 | tf_op jit(solution)/shard_map/ppermute | solution.py:414
  38.6 7.7 %collective-permute-start.19 = (bf16[4,128,128]{2,1,0:T(8,128)(2,1)S(1)}, bf16[4,128,128]{2,1,0:T(8,128)(2,1)S(1)}, u32[]{:S(2)}, u32[]{:S(2)}) collective-permute-start(bf16[4,128,128]{2,1,0:T(8,128)(2,1)S(1)} %collective-permute-done.18.refs_5_), channel_id=1, source_target_pairs={{0,4},{4,8},{8,12},{12,16},{16,20},{20,24},{24,28},{28,0},{1,5},{5... | collective-permute-start | bytes 393224 | tf_op jit(solution)/shard_map/ppermute | solution.py:414
  38.7 10.7 %collective-permute-start.6 = (bf16[4,136,128]{2,1,0:T(8,128)(2,1)S(1)}, bf16[4,136,128]{2,1,0:T(8,128)(2,1)S(1)}, u32[]{:S(2)}, u32[]{:S(2)}) collective-permute-start(bf16[4,136,128]{2,1,0:T(8,128)(2,1)S(1)} %collective-permute-done.5.refs_3_), channel_id=1, source_target_pairs={{0,28},{4,0},{8,4},{12,8},{16,12},{20,16},{24,20},{28,24},{1,29},{... | collective-permute-start | bytes 417800 | tf_op jit(solution)/shard_map/ppermute | solution.py:414
  51.7 2.4 %collective-permute-start.20 = (bf16[16,104,128]{2,1,0:T(8,128)(2,1)S(1)}, bf16[16,104,128]{2,1,0:T(8,128)(2,1)S(1)}, u32[]{:S(2)}, u32[]{:S(2)}) collective-permute-start(bf16[16,104,128]{2,1,0:T(8,128)(2,1)S(1)} %shard_map.75), channel_id=1, source_target_pairs={{0,1},{1,0},{2,3},{3,2},{4,5},{5,4},{6,7},{7,6},{8,9},{9,8},{10,11... | collective-permute-start | bytes 1277960 | tf_op jit(solution)/shard_map/ppermute | solution.py:410

commit v6 on v5

--- a/solution.py
+++ b/solution.py
@@ -325,8 +325,10 @@
     if side:
         both = jnp.zeros_like(both)
 
-    def per_part(n, carry):
-        at = pl.ds(pl.multiple_of(n * 32, 32), 32)
+    def per_part(step, carry):
+        at = pl.ds(pl.multiple_of(step * 32, 32), 32)
+        i, y = step // 2, step % 2
+        n = (i // 2) * 4 + y * 2 + i % 2
         part = inverse[at, :]
         for g in range(3):
             value = total[at, 128 * g : 128 * (g + 1)] * part
@@ -381,29 +383,68 @@
     )
 
 
-def scan_kernel(parts, out):
-    state = [jnp.zeros((32, 128), jnp.float32)] * 3
-    for w in range(8):
-        marks = parts[2 * w, 96:104, :].astype(jnp.float32)
-        decay = marks[:1] + marks[4:5]
+def scan_kernel(rescan, parts, *refs):
+    x = lax.axis_index("x")
+    for e in range(2):
         for g in range(3):
             at = slice(32 * g, 32 * (g + 1))
-            lagged = parts[2 * w, at, :].astype(jnp.float32)
-            lagged = lagged + parts[2 * w + 1, at, :].astype(jnp.float32)
-            state[g] = decay * state[g] + lagged
-            out[w, :, 128 * g : 128 * (g + 1)] = state[g].astype(jnp.bfloat16)
-
-
-def scan_windows(parts):
+            if rescan:
+                state = refs[0][e, at, :].astype(jnp.float32)
+            else:
+                state = jnp.zeros((32, 128), jnp.float32)
+            for w in range(4):
+                marks = parts[2 * w, 0, 96:104, :].astype(jnp.float32)
+                decay = marks[:1] + marks[4:5]
+                lagged = parts[2 * w, e, at, :].astype(jnp.float32)
+                lagged = lagged + parts[2 * w + 1, e, at, :].astype(jnp.float32)
+                state = decay * state + lagged
+                if rescan:
+                    value = state.astype(jnp.bfloat16)
+                    refs[5][w, 32 * e : 32 * (e + 1), 128 * g : 128 * (g + 1)] = value
+            if not rescan:
+                refs[0][e, at, :] = state.astype(jnp.bfloat16)
+    if rescan:
+        for r in range(4):
+            refs[1 + r][...] = refs[5][x ^ r]
+
+
+def scan_windows(parts, entering):
     vmem = pl.BlockSpec(memory_space=pltpu.VMEM)
+    if entering:
+        shapes = [pltpu.VMEM((64, LAGS), jnp.bfloat16)] * 4
+    else:
+        shapes = [pltpu.VMEM((2, 96, 128), jnp.bfloat16)]
     return pl.pallas_call(
-        scan_kernel,
-        out_shape=jax.ShapeDtypeStruct((8, 32, LAGS), jnp.bfloat16),
-        in_specs=[vmem],
-        out_specs=vmem,
+        functools.partial(scan_kernel, bool(entering)),
+        out_shape=shapes,
+        in_specs=[vmem] * (1 + len(entering)),
+        out_specs=[vmem] * len(shapes),
+        scratch_shapes=[pltpu.VMEM((4, 64, LAGS), jnp.bfloat16)] if entering else [],
         compiler_params=pltpu.CompilerParams(vmem_limit_bytes=24 << 20),
-        name="scan",
-    )(parts)
+        name="rescan" if entering else "scan",
+    )(*held_in_vmem([parts, *entering]))
+
+
+def gather_kernel(*refs):
+    ins, out, sem = refs[:4], refs[4], refs[5]
+    x = lax.axis_index("x")
+    copies = [pltpu.make_async_copy(ins[r], out.at[x ^ r], sem.at[r]) for r in range(4)]
+    for copy in copies:
+        copy.start()
+    for copy in copies:
+        copy.wait()
+
+
+def gather_stations(ins):
+    return pl.pallas_call(
+        gather_kernel,
+        out_shape=pltpu.HBM((4, 64, LAGS), jnp.bfloat16),
+        in_specs=[pl.BlockSpec(memory_space=pltpu.VMEM)] * 4,
+        out_specs=pl.BlockSpec(memory_space=pl.ANY),
+        scratch_shapes=[pltpu.SemaphoreType.DMA((4,))],
+        compiler_params=pltpu.CompilerParams(vmem_limit_bytes=24 << 20),
+        name="gather",
+    )(*held_in_vmem(ins))
 
 
 def across(value, r):
@@ -436,20 +477,26 @@
     sent = correlate(1, 1, window_decay, pairs, halves[1], table, [lagged])
     kept = correlate(1, 0, window_decay, pairs, halves[1], table, [lagged])
     kept = kept.astype(jnp.float32) + across(sent, 1).astype(jnp.float32)
-    parts = lax.all_to_all(kept.astype(jnp.bfloat16), ("section", "y"), 0, 0)
-    states = lax.all_to_all(scan_windows(parts), "section", 0, 0)
-    return states[None]
+    kept = kept.astype(jnp.bfloat16).reshape(8, 2, 104, 128)
+    parts = lax.all_to_all(kept, ("x", "y"), 0, 0)
+    (total,) = scan_windows(parts, [])
+    entering = lax.ppermute(total, "yh", [(0, 1)])
+    states = list(scan_windows(parts, [entering]))
+    for r in (1, 2, 3):
+        states[r] = lax.ppermute(states[r], "x", [(d, d ^ r) for d in range(4)])
+    return gather_stations(states).reshape(1, LS, 32, LAGS)
 
 
 def solution(mesh):
-    split = Mesh(mesh.devices.reshape(8, 8, 2, 2), ("section", "z", "y", "c"))
+    split = Mesh(mesh.devices.reshape(2, 4, 8, 2, 2), ("yh", "x", "z", "y", "c"))
     sta = ("z", "y", "c")
-    placed = (P("section", sta, None, None), P("section", sta, None), P(sta, None), P("section"))
+    section = ("yh", "x")
+    placed = (P(section, sta, None, None), P(section, sta, None), P(sta, None), P(section))
 
     return jax.shard_map(
         body,
         mesh=split,
         in_specs=placed,
-        out_specs=P("section", sta, None, None),
+        out_specs=P(section, sta, None, None),
         check_vma=False,
     )

time: 83.2 us -> 84 us (level)
  blocking collectives: 27.2 us -> 11.9 us
  starting transfers between devices: 27.8 us -> 37.1 us
  waiting for transfers between devices: 13.5 us -> 19.5 us
  Pallas kernels: 11.9 us -> 13 us
    all_to_all x2 -> x1, blocking collectives: 27.2 us -> 11.9 us  [body(): parts = lax.all_to_all(kept, ('x', 'y'), 0, 0)]
    ppermute x0 -> x4, starting transfers between devices: none -> 9.23 us  [the longest x3 4.79 us: body(): states[r] = lax.ppermute(states[r], 'x', [(d, d ^ r) for d in range(4)])]
    ppermute x0 -> x4, waiting for transfers between devices: none -> 5.95 us  [the longest x3 4.22 us: body(): states[r] = lax.ppermute(states[r], 'x', [(d, d ^ r) for d in range(4)])]
  transfers between devices with their start and end apart: 21 -> 25, of which waited for: 9 -> 12; matrix products, arithmetic and copies ran while one was open for 0% -> 0% of each run, Pallas kernels for 7% -> 7%
where the time goes in v6:
time: 84 us; the launch traced here: 82.6 us
  starting transfers between devices  37.1 us (44%)
  waiting for transfers between devices  19.5 us (23%)
  Pallas kernels  13 us (15%)
  blocking collectives  11.9 us (14%)
  between operations  0.97 us (1%)
    ppermute x14, starting transfers between devices, along(): return lax.ppermute(value, 'z', [(d, (d + step) % 8) for d in range(8)])  23.8 us
    ppermute x14, waiting for transfers between devices, along(): return lax.ppermute(value, 'z', [(d, (d + step) % 8) for d in range(8)])  12.2 us
    all_to_all x1, blocking collectives, body(): parts = lax.all_to_all(kept, ('x', 'y'), 0, 0)  11.9 us
    pallas_call x3, Pallas kernels, correlate(): pl.pallas_call(functools.partial(correlate_kernel, h, side), out_shape=sh...  7.98 us
    ppermute x3, starting transfers between devices, body(): states[r] = lax.ppermute(states[r], 'x', [(d, d ^ r) for d in range(4)])  4.79 us
    ppermute x1, starting transfers between devices, body(): entering = lax.ppermute(total, 'yh', [(0, 1)])  4.45 us
    ppermute x3, waiting for transfers between devices, body(): states[r] = lax.ppermute(states[r], 'x', [(d, d ^ r) for d in range(4)])  4.22 us
    pallas_call x1, Pallas kernels, spectrum(): pl.pallas_call(spectrum_kernel, out_shape=shapes, in_specs=[pl.BlockSpec(...  4.17 us
  transfers between devices with their start and end apart: 25, of which 12 were waited for; matrix products, arithmetic and copies ran while one was open for 0% of the time, Pallas kernels for 7%

profile of v6, /device:TPU:6, one launch (start us, length us, event | category | flops | bytes accessed | tf_op | source)
XLA Modules:
  0.0 82.6 jit_solution(15688884659031279665)
XLA Ops:
  0.0 4.2 %spectrum.1 = (bf16[128,128]{1,0:T(8,128)(2,1)S(1)}, bf16[136,128]{1,0:T(8,128)(2,1)S(1)}, bf16[128,128]{1,0:T(8,128)(2,1)S(1)}, bf16[136,128]{1,0:T(8,128)(2,1)...) custom-call(s32[1,8,8]{2,1,0:T(8,128)} %mask_hbm.1, ...), custom_call_target="tpu_custom_call" | custom-call | tf_op jit(solution)/shard_map/spectrum/pallas_call | solution.py:227
  4.2 0.1 collective-permute-start
  4.3 1.7 %collective-permute-start.1 = (bf16[136,128]{1,0:T(8,128)(2,1)S(1)}, bf16[136,128]{1,0:T(8,128)(2,1)S(1)}, u32[]{:S(2)}, u32[]{:S(2)}) collective-permute-start(bf16[136,128]{1,0:T(8,128)(2,1)S(1)} %get-tuple-element.19), channel_id=1, source_target_pairs={{0,2},{1,3},{2,0},{3,1},{4,6},{5,7},{6,4},{7,5},{8,10},{9,11},{10,... | collective-permute-start | bytes 104456 | tf_op jit(solution)/shard_map/ppermute | solution.py:451
  5.9 0.2 collective-permute-start.2
  6.1 0.4 collective-permute-start.10
  6.5 1.6 %collective-permute-start.11 = (bf16[128,128]{1,0:T(8,128)(2,1)S(1)}, bf16[128,128]{1,0:T(8,128)(2,1)S(1)}, u32[]{:S(2)}, u32[]{:S(2)}) collective-permute-start(bf16[128,128]{1,0:T(8,128)(2,1)S(1)} %get-tuple-element.23), channel_id=1, source_target_pairs={{0,2},{1,3},{2,0},{3,1},{4,6},{5,7},{6,4},{7,5},{8,10},{9,11},{10,... | collective-permute-start | bytes 98312 | tf_op jit(solution)/shard_map/ppermute | solution.py:451
  8.1 0.0 collective-permute-done
  8.1 0.0 collective-permute-start.12
  8.1 0.2 collective-permute-done.1
  8.3 1.1 %collective-permute-done.2 = bf16[136,128]{1,0:T(8,128)(2,1)S(1)} collective-permute-done((bf16[136,128]{1,0:T(8,128)(2,1)S(1)}, bf16[136,128]{1,0:T(8,128)(2,1)S(1)}, u32[]{:S(2)}, u32[]{:S(2)}) %collective-permute-start.2) | collective-permute-done | bytes 34848 | tf_op jit(solution)/shard_map/ppermute | solution.py:451
  9.4 5.9 %collective-permute-start.3 = (bf16[4,136,128]{2,1,0:T(8,128)(2,1)S(1)}, bf16[4,136,128]{2,1,0:T(8,128)(2,1)S(1)}, u32[]{:S(2)}, u32[]{:S(2)}) collective-permute-start(bf16[4,136,128]{2,1,0:T(8,128)(2,1)S(1)} %pad_maximum_fusion.refs_0_), channel_id=1, source_target_pairs={{0,28},{4,0},{8,4},{12,8},{16,12},{20,16},{24,20},{28,24},{1,29},{... | collective-permute-start | bytes 417800 | tf_op jit(solution)/shard_map/ppermute | solution.py:455
  15.3 0.0 collective-permute-done.10
  15.3 0.0 collective-permute-done.11
  15.3 0.0 collective-permute-done.12
  15.4 0.1 collective-permute-start.16
  15.5 0.2 collective-permute-start.7
  15.7 3.2 %collective-permute-done.3.refs_1_ = bf16[4,136,128]{2,1,0:T(8,128)(2,1)S(1)} collective-permute-done((bf16[4,136,128]{2,1,0:T(8,128)(2,1)S(1)}, bf16[4,136,128]{2,1,0:T(8,128)(2,1)S(1)}, u32[]{:S(2)}, u32[]{:S(2)}) %collective-permute-start.3) | collective-permute-done | bytes 139296 | tf_op jit(solution)/shard_map/ppermute | solution.py:455
  18.9 3.7 %collective-permute-start.4 = (bf16[4,136,128]{2,1,0:T(8,128)(2,1)S(1)}, bf16[4,136,128]{2,1,0:T(8,128)(2,1)S(1)}, u32[]{:S(2)}, u32[]{:S(2)}) collective-permute-start(bf16[4,136,128]{2,1,0:T(8,128)(2,1)S(1)} %collective-permute-done.3.refs_1_), channel_id=1, source_target_pairs={{0,28},{4,0},{8,4},{12,8},{16,12},{20,16},{24,20},{28,24},{1,29},{... | collective-permute-start | bytes 417800 | tf_op jit(solution)/shard_map/ppermute | solution.py:455
  22.5 0.0 collective-permute-start.13
  22.6 0.4 collective-permute-done.16.refs_7_
  23.0 1.6 %collective-permute-start.17 = (bf16[4,128,128]{2,1,0:T(8,128)(2,1)S(1)}, bf16[4,128,128]{2,1,0:T(8,128)(2,1)S(1)}, u32[]{:S(2)}, u32[]{:S(2)}) collective-permute-start(bf16[4,128,128]{2,1,0:T(8,128)(2,1)S(1)} %collective-permute-done.16.refs_7_), channel_id=1, source_target_pairs={{0,4},{4,8},{8,12},{12,16},{16,20},{20,24},{24,28},{28,0},{1,5},{5... | collective-permute-start | bytes 393224 | tf_op jit(solution)/shard_map/ppermute | solution.py:455
  24.6 0.6 collective-permute-done.7.refs_7_
  25.2 0.0 collective-permute-start.8
  25.2 1.4 %collective-permute-done.4.refs_2_ = bf16[4,136,128]{2,1,0:T(8,128)(2,1)S(1)} collective-permute-done((bf16[4,136,128]{2,1,0:T(8,128)(2,1)S(1)}, bf16[4,136,128]{2,1,0:T(8,128)(2,1)S(1)}, u32[]{:S(2)}, u32[]{:S(2)}) %collective-permute-start.4) | collective-permute-done | bytes 139296 | tf_op jit(solution)/shard_map/ppermute | solution.py:455
  26.6 3.7 %collective-permute-start.5 = (bf16[4,136,128]{2,1,0:T(8,128)(2,1)S(1)}, bf16[4,136,128]{2,1,0:T(8,128)(2,1)S(1)}, u32[]{:S(2)}, u32[]{:S(2)}) collective-permute-start(bf16[4,136,128]{2,1,0:T(8,128)(2,1)S(1)} %collective-permute-done.4.refs_2_), channel_id=1, source_target_pairs={{0,28},{4,0},{8,4},{12,8},{16,12},{20,16},{24,20},{28,24},{1,29},{... | collective-permute-start | bytes 417800 | tf_op jit(solution)/shard_map/ppermute | solution.py:455
  30.3 0.0 collective-permute-done.13.refs_1_
  30.3 1.7 %collective-permute-start.14 = (bf16[4,128,128]{2,1,0:T(8,128)(2,1)S(1)}, bf16[4,128,128]{2,1,0:T(8,128)(2,1)S(1)}, u32[]{:S(2)}, u32[]{:S(2)}) collective-permute-start(bf16[4,128,128]{2,1,0:T(8,128)(2,1)S(1)} %collective-permute-done.13.refs_1_), channel_id=1, source_target_pairs={{0,28},{4,0},{8,4},{12,8},{16,12},{20,16},{24,20},{28,24},{1,29},{... | collective-permute-start | bytes 393224 | tf_op jit(solution)/shard_map/ppermute | solution.py:455
  32.0 0.0 collective-permute-done.17.refs_6_
  32.0 0.3 collective-permute-start.18
  33.0 2.3 %collective-permute-done.14.refs_2_ = bf16[4,128,128]{2,1,0:T(8,128)(2,1)S(1)} collective-permute-done((bf16[4,128,128]{2,1,0:T(8,128)(2,1)S(1)}, bf16[4,128,128]{2,1,0:T(8,128)(2,1)S(1)}, u32[]{:S(2)}, u32[]{:S(2)}) %collective-permute-start.14) | collective-permute-done | bytes 131104 | tf_op jit(solution)/shard_map/ppermute | solution.py:455
  35.3 3.3 %collective-permute-start.15 = (bf16[4,128,128]{2,1,0:T(8,128)(2,1)S(1)}, bf16[4,128,128]{2,1,0:T(8,128)(2,1)S(1)}, u32[]{:S(2)}, u32[]{:S(2)}) collective-permute-start(bf16[4,128,128]{2,1,0:T(8,128)(2,1)S(1)} %collective-permute-done.14.refs_2_), channel_id=1, source_target_pairs={{0,28},{4,0},{8,4},{12,8},{16,12},{20,16},{24,20},{28,24},{1,29},{... | collective-permute-start | bytes 393224 | tf_op jit(solution)/shard_map/ppermute | solution.py:455
  38.6 0.0 collective-permute-done.8.refs_6_
  38.6 0.0 collective-permute-start.9
  38.6 0.0 collective-permute-done.18.refs_5_
  38.6 0.1 collective-permute-start.19
  38.7 0.0 collective-permute-done.5.refs_3_
  38.7 3.2 %collective-permute-start.6 = (bf16[4,136,128]{2,1,0:T(8,128)(2,1)S(1)}, bf16[4,136,128]{2,1,0:T(8,128)(2,1)S(1)}, u32[]{:S(2)}, u32[]{:S(2)}) collective-permute-start(bf16[4,136,128]{2,1,0:T(8,128)(2,1)S(1)} %collective-permute-done.5.refs_3_), channel_id=1, source_target_pairs={{0,28},{4,0},{8,4},{12,8},{16,12},{20,16},{24,20},{28,24},{1,29},{... | collective-permute-start | bytes 417800 | tf_op jit(solution)/shard_map/ppermute | solution.py:455
  41.9 0.1 slice_convert_fusion
  42.0 0.2 collective-permute-done.15.refs_3_
  42.1 4.1 %collective-permute-done.19.refs_4_ = bf16[4,128,128]{2,1,0:T(8,128)(2,1)S(1)} collective-permute-done((bf16[4,128,128]{2,1,0:T(8,128)(2,1)S(1)}, bf16[4,128,128]{2,1,0:T(8,128)(2,1)S(1)}, u32[]{:S(2)}, u32[]{:S(2)}) %collective-permute-start.19) | collective-permute-done | bytes 131104 | tf_op jit(solution)/shard_map/ppermute | solution.py:455
  46.2 3.1 %shard_map.73.refs_9_ = f32[1024,384]{1,0:T(8,128)S(1)} custom-call(f32[1]{0:T(128)S(6)} %copy.8.decay_ref, s32[4,4]{1,0:T(4,128)S(1)} %bitcast.13, bf16[4,128,128]{2,1,0:T(8,128)(2,1)S(1)} %pad_maximum_fusion.1.refs_0_, bf16[4,128,128]{2,1,0:T(8,128)(2,1)S(1)} %collective-permute-done.13.refs_1_, bf16[4,128,128]{2,1,0:T(8,128)(2,1)S(1)} %collective-permute-done.14.refs_2_, ...), custom_call_target="tpu_custom_call" | custom-call | tf_op jit(solution)/shard_map/pallas_call | solution.py:358
  49.4 0.0 collective-permute-done.9.refs_5_
  49.4 0.0 collective-permute-done.6.refs_4_
  49.4 2.4 %shard_map.75 = bf16[16,104,128]{2,1,0:T(8,128)(2,1)S(1)} custom-call(f32[1]{0:T(128)S(6)} %copy.8.decay_ref, s32[4,4]{1,0:T(4,128)S(1)} %bitcast.14, bf16[4,136,128]{2,1,0:T(8,128)(2,1)S(1)} %pad_maximum_fusion.refs_0_, bf16[4,136,128]{2,1,0:T(8,128)(2,1)S(1)} %collective-permute-done.3.refs_1_, bf16[4,136,128]{2,1,0:T(8,128)(2,1)S(1)} %collective-permute-done.4.refs_2_, ...), custom_call_target="tpu_custom_call" | custom-call | tf_op jit(solution)/shard_map/pallas_call | solution.py:358
  51.8 0.1 collective-permute-start.20
  51.9 2.4 %shard_map.74 = bf16[16,104,128]{2,1,0:T(8,128)(2,1)S(1)} custom-call(f32[1]{0:T(128)S(6)} %copy.8.decay_ref, s32[4,4]{1,0:T(4,128)S(1)} %bitcast.15, bf16[4,136,128]{2,1,0:T(8,128)(2,1)S(1)} %pad_maximum_fusion.refs_0_, bf16[4,136,128]{2,1,0:T(8,128)(2,1)S(1)} %collective-permute-done.3.refs_1_, bf16[4,136,128]{2,1,0:T(8,128)(2,1)S(1)} %collective-permute-done.4.refs_2_, ...), custom_call_target="tpu_custom_call" | custom-call | tf_op jit(solution)/shard_map/pallas_call | solution.py:358
  54.4 0.0 collective-permute-done.20
  54.4 0.1 add_convert_fusion
  54.5 11.9 %all_to_all.5.parts = bf16[8,2,104,128]{3,2,1,0:T(8,128)(2,1)S(1)} all-to-all(bf16[8,2,104,128]{3,2,1,0:T(8,128)(2,1)S(1)} %bitcast.17), channel_id=1, replica_groups=mesh['yh'=2,'x'=4,'z'=8,'y'=2,'c'=2] {'x','y'}, dimensions={0} | all-to-all | bytes 851968 | tf_op jit(solution)/shard_map/all_to_all | solution.py:481
  66.4 0.1 scan.1
  66.5 4.4 %collective-permute-start.21 = (bf16[2,96,128]{2,1,0:T(8,128)(2,1)S(1)}, bf16[2,96,128]{2,1,0:T(8,128)(2,1)S(1)}, u32[]{:S(2)}, u32[]{:S(2)}) collective-permute-start(bf16[2,96,128]{2,1,0:T(8,128)(2,1)S(1)} %scan.1), channel_id=1, source_target_pairs={{0,128},{1,129},{2,130},{3,131},{4,132},{5,133},{6,134},{7,135},{8... | collective-permute-start | bytes 147464 | tf_op jit(solution)/shard_map/ppermute | solution.py:483
  70.9 1.7 %collective-permute-done.21.refs_0_ = bf16[2,96,128]{2,1,0:T(8,128)(2,1)S(1)} collective-permute-done((bf16[2,96,128]{2,1,0:T(8,128)(2,1)S(1)}, bf16[2,96,128]{2,1,0:T(8,128)(2,1)S(1)}, u32[]{:S(2)}, u32[]{:S(2)}) %collective-permute-start.21) | collective-permute-done | bytes 49184 | tf_op jit(solution)/shard_map/ppermute | solution.py:483
  72.7 0.1 rescan.1
  72.8 1.0 %collective-permute-start.22 = (bf16[64,384]{1,0:T(8,128)(2,1)S(1)}, bf16[64,384]{1,0:T(8,128)(2,1)S(1)}, u32[]{:S(2)}, u32[]{:S(2)}) collective-permute-start(bf16[64,384]{1,0:T(8,128)(2,1)S(1)} %get-tuple-element.26), channel_id=1, source_target_pairs={{0,32},{32,0},{64,96},{96,64},{1,33},{33,1},{65,97},{97,65},{2,34}... | collective-permute-start | bytes 147464 | tf_op jit(solution)/shard_map/ppermute | solution.py:486
  73.8 2.7 %collective-permute-start.23 = (bf16[64,384]{1,0:T(8,128)(2,1)S(1)}, bf16[64,384]{1,0:T(8,128)(2,1)S(1)}, u32[]{:S(2)}, u32[]{:S(2)}) collective-permute-start(bf16[64,384]{1,0:T(8,128)(2,1)S(1)} %get-tuple-element.27), channel_id=1, source_target_pairs={{0,64},{32,96},{64,0},{96,32},{1,65},{33,97},{65,1},{97,33},{2,66}... | collective-permute-start | bytes 147464 | tf_op jit(solution)/shard_map/ppermute | solution.py:486
  76.5 1.1 %collective-permute-start.24 = (bf16[64,384]{1,0:T(8,128)(2,1)S(1)}, bf16[64,384]{1,0:T(8,128)(2,1)S(1)}, u32[]{:S(2)}, u32[]{:S(2)}) collective-permute-start(bf16[64,384]{1,0:T(8,128)(2,1)S(1)} %get-tuple-element.28), channel_id=1, source_target_pairs={{0,96},{32,64},{64,32},{96,0},{1,97},{33,65},{65,33},{97,1},{2,98}... | collective-permute-start | bytes 147464 | tf_op jit(solution)/shard_map/ppermute | solution.py:486
  77.6 0.0 collective-permute-done.22.refs_1_
  77.6 1.8 %collective-permute-done.23.refs_2_ = bf16[64,384]{1,0:T(8,128)(2,1)S(1)} collective-permute-done((bf16[64,384]{1,0:T(8,128)(2,1)S(1)}, bf16[64,384]{1,0:T(8,128)(2,1)S(1)}, u32[]{:S(2)}, u32[]{:S(2)}) %collective-permute-start.23) | collective-permute-done | bytes 49184 | tf_op jit(solution)/shard_map/ppermute | solution.py:486
  79.4 2.4 %collective-permute-done.24.refs_3_ = bf16[64,384]{1,0:T(8,128)(2,1)S(1)} collective-permute-done((bf16[64,384]{1,0:T(8,128)(2,1)S(1)}, bf16[64,384]{1,0:T(8,128)(2,1)S(1)}, u32[]{:S(2)}, u32[]{:S(2)}) %collective-permute-start.24) | collective-permute-done | bytes 49184 | tf_op jit(solution)/shard_map/ppermute | solution.py:486
  81.8 0.7 gather.1
  (2 shorter events, 0.0 us)
Async XLA Ops:
  4.2 3.9 %collective-permute-start = (bf16[136,128]{1,0:T(8,128)(2,1)S(1)}, bf16[136,128]{1,0:T(8,128)(2,1)S(1)}, u32[]{:S(2)}, u32[]{:S(2)}) collective-permute-start(bf16[136,128]{1,0:T(8,128)(2,1)S(1)} %get-tuple-element.18), channel_id=1, source_target_pairs={{0,1},{1,0},{2,3},{3,2},{4,5},{5,4},{6,7},{7,6},{8,9},{9,8},{10,11... | collective-permute-start | bytes 104456 | tf_op jit(solution)/shard_map/ppermute | solution.py:451
  4.3 4.0 %collective-permute-start.1 = (bf16[136,128]{1,0:T(8,128)(2,1)S(1)}, bf16[136,128]{1,0:T(8,128)(2,1)S(1)}, u32[]{:S(2)}, u32[]{:S(2)}) collective-permute-start(bf16[136,128]{1,0:T(8,128)(2,1)S(1)} %get-tuple-element.19), channel_id=1, source_target_pairs={{0,2},{1,3},{2,0},{3,1},{4,6},{5,7},{6,4},{7,5},{8,10},{9,11},{10,... | collective-permute-start | bytes 104456 | tf_op jit(solution)/shard_map/ppermute | solution.py:451
  5.9 3.4 %collective-permute-start.2 = (bf16[136,128]{1,0:T(8,128)(2,1)S(1)}, bf16[136,128]{1,0:T(8,128)(2,1)S(1)}, u32[]{:S(2)}, u32[]{:S(2)}) collective-permute-start(bf16[136,128]{1,0:T(8,128)(2,1)S(1)} %get-tuple-element.20), channel_id=1, source_target_pairs={{0,3},{1,2},{2,1},{3,0},{4,7},{5,6},{6,5},{7,4},{8,11},{9,10},{10,... | collective-permute-start | bytes 104456 | tf_op jit(solution)/shard_map/ppermute | solution.py:451
  6.1 9.2 %collective-permute-start.10 = (bf16[128,128]{1,0:T(8,128)(2,1)S(1)}, bf16[128,128]{1,0:T(8,128)(2,1)S(1)}, u32[]{:S(2)}, u32[]{:S(2)}) collective-permute-start(bf16[128,128]{1,0:T(8,128)(2,1)S(1)} %get-tuple-element.22), channel_id=1, source_target_pairs={{0,1},{1,0},{2,3},{3,2},{4,5},{5,4},{6,7},{7,6},{8,9},{9,8},{10,11... | collective-permute-start | bytes 98312 | tf_op jit(solution)/shard_map/ppermute | solution.py:451
  6.5 8.8 %collective-permute-start.11 = (bf16[128,128]{1,0:T(8,128)(2,1)S(1)}, bf16[128,128]{1,0:T(8,128)(2,1)S(1)}, u32[]{:S(2)}, u32[]{:S(2)}) collective-permute-start(bf16[128,128]{1,0:T(8,128)(2,1)S(1)} %get-tuple-element.23), channel_id=1, source_target_pairs={{0,2},{1,3},{2,0},{3,1},{4,6},{5,7},{6,4},{7,5},{8,10},{9,11},{10,... | collective-permute-start | bytes 98312 | tf_op jit(solution)/shard_map/ppermute | solution.py:451
  8.1 7.2 %collective-permute-start.12 = (bf16[128,128]{1,0:T(8,128)(2,1)S(1)}, bf16[128,128]{1,0:T(8,128)(2,1)S(1)}, u32[]{:S(2)}, u32[]{:S(2)}) collective-permute-start(bf16[128,128]{1,0:T(8,128)(2,1)S(1)} %get-tuple-element.24), channel_id=1, source_target_pairs={{0,3},{1,2},{2,1},{3,0},{4,7},{5,6},{6,5},{7,4},{8,11},{9,10},{10,... | collective-permute-start | bytes 98312 | tf_op jit(solution)/shard_map/ppermute | solution.py:451
  9.4 9.5 %collective-permute-start.3 = (bf16[4,136,128]{2,1,0:T(8,128)(2,1)S(1)}, bf16[4,136,128]{2,1,0:T(8,128)(2,1)S(1)}, u32[]{:S(2)}, u32[]{:S(2)}) collective-permute-start(bf16[4,136,128]{2,1,0:T(8,128)(2,1)S(1)} %pad_maximum_fusion.refs_0_), channel_id=1, source_target_pairs={{0,28},{4,0},{8,4},{12,8},{16,12},{20,16},{24,20},{28,24},{1,29},{... | collective-permute-start | bytes 417800 | tf_op jit(solution)/shard_map/ppermute | solution.py:455
  15.4 7.7 %collective-permute-start.16 = (bf16[4,128,128]{2,1,0:T(8,128)(2,1)S(1)}, bf16[4,128,128]{2,1,0:T(8,128)(2,1)S(1)}, u32[]{:S(2)}, u32[]{:S(2)}) collective-permute-start(bf16[4,128,128]{2,1,0:T(8,128)(2,1)S(1)} %pad_maximum_fusion.1.refs_0_), channel_id=1, source_target_pairs={{0,4},{4,8},{8,12},{12,16},{16,20},{20,24},{24,28},{28,0},{1,5},{5... | collective-permute-start | bytes 393224 | tf_op jit(solution)/shard_map/ppermute | solution.py:455
  15.5 9.7 %collective-permute-start.7 = (bf16[4,136,128]{2,1,0:T(8,128)(2,1)S(1)}, bf16[4,136,128]{2,1,0:T(8,128)(2,1)S(1)}, u32[]{:S(2)}, u32[]{:S(2)}) collective-permute-start(bf16[4,136,128]{2,1,0:T(8,128)(2,1)S(1)} %pad_maximum_fusion.refs_0_), channel_id=1, source_target_pairs={{0,4},{4,8},{8,12},{12,16},{16,20},{20,24},{24,28},{28,0},{1,5},{5... | collective-permute-start | bytes 417800 | tf_op jit(solution)/shard_map/ppermute | solution.py:455
  18.9 7.8 %collective-permute-start.4 = (bf16[4,136,128]{2,1,0:T(8,128)(2,1)S(1)}, bf16[4,136,128]{2,1,0:T(8,128)(2,1)S(1)}, u32[]{:S(2)}, u32[]{:S(2)}) collective-permute-start(bf16[4,136,128]{2,1,0:T(8,128)(2,1)S(1)} %collective-permute-done.3.refs_1_), channel_id=1, source_target_pairs={{0,28},{4,0},{8,4},{12,8},{16,12},{20,16},{24,20},{28,24},{1,29},{... | collective-permute-start | bytes 417800 | tf_op jit(solution)/shard_map/ppermute | solution.py:455
  22.5 7.8 %collective-permute-start.13 = (bf16[4,128,128]{2,1,0:T(8,128)(2,1)S(1)}, bf16[4,128,128]{2,1,0:T(8,128)(2,1)S(1)}, u32[]{:S(2)}, u32[]{:S(2)}) collective-permute-start(bf16[4,128,128]{2,1,0:T(8,128)(2,1)S(1)} %pad_maximum_fusion.1.refs_0_), channel_id=1, source_target_pairs={{0,28},{4,0},{8,4},{12,8},{16,12},{20,16},{24,20},{28,24},{1,29},{... | collective-permute-start | bytes 393224 | tf_op jit(solution)/shard_map/ppermute | solution.py:455
  23.0 9.0 %collective-permute-start.17 = (bf16[4,128,128]{2,1,0:T(8,128)(2,1)S(1)}, bf16[4,128,128]{2,1,0:T(8,128)(2,1)S(1)}, u32[]{:S(2)}, u32[]{:S(2)}) collective-permute-start(bf16[4,128,128]{2,1,0:T(8,128)(2,1)S(1)} %collective-permute-done.16.refs_7_), channel_id=1, source_target_pairs={{0,4},{4,8},{8,12},{12,16},{16,20},{20,24},{24,28},{28,0},{1,5},{5... | collective-permute-start | bytes 393224 | tf_op jit(solution)/shard_map/ppermute | solution.py:455
  25.2 13.4 %collective-permute-start.8 = (bf16[4,136,128]{2,1,0:T(8,128)(2,1)S(1)}, bf16[4,136,128]{2,1,0:T(8,128)(2,1)S(1)}, u32[]{:S(2)}, u32[]{:S(2)}) collective-permute-start(bf16[4,136,128]{2,1,0:T(8,128)(2,1)S(1)} %collective-permute-done.7.refs_7_), channel_id=1, source_target_pairs={{0,4},{4,8},{8,12},{12,16},{16,20},{20,24},{24,28},{28,0},{1,5},{5... | collective-permute-start | bytes 417800 | tf_op jit(solution)/shard_map/ppermute | solution.py:455
  26.6 12.1 %collective-permute-start.5 = (bf16[4,136,128]{2,1,0:T(8,128)(2,1)S(1)}, bf16[4,136,128]{2,1,0:T(8,128)(2,1)S(1)}, u32[]{:S(2)}, u32[]{:S(2)}) collective-permute-start(bf16[4,136,128]{2,1,0:T(8,128)(2,1)S(1)} %collective-permute-done.4.refs_2_), channel_id=1, source_target_pairs={{0,28},{4,0},{8,4},{12,8},{16,12},{20,16},{24,20},{28,24},{1,29},{... | collective-permute-start | bytes 417800 | tf_op jit(solution)/shard_map/ppermute | solution.py:455
  30.3 5.0 %collective-permute-start.14 = (bf16[4,128,128]{2,1,0:T(8,128)(2,1)S(1)}, bf16[4,128,128]{2,1,0:T(8,128)(2,1)S(1)}, u32[]{:S(2)}, u32[]{:S(2)}) collective-permute-start(bf16[4,128,128]{2,1,0:T(8,128)(2,1)S(1)} %collective-permute-done.13.refs_1_), channel_id=1, source_target_pairs={{0,28},{4,0},{8,4},{12,8},{16,12},{20,16},{24,20},{28,24},{1,29},{... | collective-permute-start | bytes 393224 | tf_op jit(solution)/shard_map/ppermute | solution.py:455
  32.0 6.6 %collective-permute-start.18 = (bf16[4,128,128]{2,1,0:T(8,128)(2,1)S(1)}, bf16[4,128,128]{2,1,0:T(8,128)(2,1)S(1)}, u32[]{:S(2)}, u32[]{:S(2)}) collective-permute-start(bf16[4,128,128]{2,1,0:T(8,128)(2,1)S(1)} %collective-permute-done.17.refs_6_), channel_id=1, source_target_pairs={{0,4},{4,8},{8,12},{12,16},{16,20},{20,24},{24,28},{28,0},{1,5},{5... | collective-permute-start | bytes 393224 | tf_op jit(solution)/shard_map/ppermute | solution.py:455
  35.3 6.9 %collective-permute-start.15 = (bf16[4,128,128]{2,1,0:T(8,128)(2,1)S(1)}, bf16[4,128,128]{2,1,0:T(8,128)(2,1)S(1)}, u32[]{:S(2)}, u32[]{:S(2)}) collective-permute-start(bf16[4,128,128]{2,1,0:T(8,128)(2,1)S(1)} %collective-permute-done.14.refs_2_), channel_id=1, source_target_pairs={{0,28},{4,0},{8,4},{12,8},{16,12},{20,16},{24,20},{28,24},{1,29},{... | collective-permute-start | bytes 393224 | tf_op jit(solution)/shard_map/ppermute | solution.py:455
  38.6 10.8 %collective-permute-start.9 = (bf16[4,136,128]{2,1,0:T(8,128)(2,1)S(1)}, bf16[4,136,128]{2,1,0:T(8,128)(2,1)S(1)}, u32[]{:S(2)}, u32[]{:S(2)}) collective-permute-start(bf16[4,136,128]{2,1,0:T(8,128)(2,1)S(1)} %collective-permute-done.8.refs_6_), channel_id=1, source_target_pairs={{0,4},{4,8},{8,12},{12,16},{16,20},{20,24},{24,28},{28,0},{1,5},{5... | collective-permute-start | bytes 417800 | tf_op jit(solution)/shard_map/ppermute | solution.py:455
  38.6 7.7 %collective-permute-start.19 = (bf16[4,128,128]{2,1,0:T(8,128)(2,1)S(1)}, bf16[4,128,128]{2,1,0:T(8,128)(2,1)S(1)}, u32[]{:S(2)}, u32[]{:S(2)}) collective-permute-start(bf16[4,128,128]{2,1,0:T(8,128)(2,1)S(1)} %collective-permute-done.18.refs_5_), channel_id=1, source_target_pairs={{0,4},{4,8},{8,12},{12,16},{16,20},{20,24},{24,28},{28,0},{1,5},{5... | collective-permute-start | bytes 393224 | tf_op jit(solution)/shard_map/ppermute | solution.py:455
  38.7 10.7 %collective-permute-start.6 = (bf16[4,136,128]{2,1,0:T(8,128)(2,1)S(1)}, bf16[4,136,128]{2,1,0:T(8,128)(2,1)S(1)}, u32[]{:S(2)}, u32[]{:S(2)}) collective-permute-start(bf16[4,136,128]{2,1,0:T(8,128)(2,1)S(1)} %collective-permute-done.5.refs_3_), channel_id=1, source_target_pairs={{0,28},{4,0},{8,4},{12,8},{16,12},{20,16},{24,20},{28,24},{1,29},{... | collective-permute-start | bytes 417800 | tf_op jit(solution)/shard_map/ppermute | solution.py:455
  51.8 2.5 %collective-permute-start.20 = (bf16[16,104,128]{2,1,0:T(8,128)(2,1)S(1)}, bf16[16,104,128]{2,1,0:T(8,128)(2,1)S(1)}, u32[]{:S(2)}, u32[]{:S(2)}) collective-permute-start(bf16[16,104,128]{2,1,0:T(8,128)(2,1)S(1)} %shard_map.75), channel_id=1, source_target_pairs={{0,1},{1,0},{2,3},{3,2},{4,5},{5,4},{6,7},{7,6},{8,9},{9,8},{10,11... | collective-permute-start | bytes 1277960 | tf_op jit(solution)/shard_map/ppermute | solution.py:451
  66.5 6.2 %collective-permute-start.21 = (bf16[2,96,128]{2,1,0:T(8,128)(2,1)S(1)}, bf16[2,96,128]{2,1,0:T(8,128)(2,1)S(1)}, u32[]{:S(2)}, u32[]{:S(2)}) collective-permute-start(bf16[2,96,128]{2,1,0:T(8,128)(2,1)S(1)} %scan.1), channel_id=1, source_target_pairs={{0,128},{1,129},{2,130},{3,131},{4,132},{5,133},{6,134},{7,135},{8... | collective-permute-start | bytes 147464 | tf_op jit(solution)/shard_map/ppermute | solution.py:483
  72.8 4.8 %collective-permute-start.22 = (bf16[64,384]{1,0:T(8,128)(2,1)S(1)}, bf16[64,384]{1,0:T(8,128)(2,1)S(1)}, u32[]{:S(2)}, u32[]{:S(2)}) collective-permute-start(bf16[64,384]{1,0:T(8,128)(2,1)S(1)} %get-tuple-element.26), channel_id=1, source_target_pairs={{0,32},{32,0},{64,96},{96,64},{1,33},{33,1},{65,97},{97,65},{2,34}... | collective-permute-start | bytes 147464 | tf_op jit(solution)/shard_map/ppermute | solution.py:486
  73.8 5.6 %collective-permute-start.23 = (bf16[64,384]{1,0:T(8,128)(2,1)S(1)}, bf16[64,384]{1,0:T(8,128)(2,1)S(1)}, u32[]{:S(2)}, u32[]{:S(2)}) collective-permute-start(bf16[64,384]{1,0:T(8,128)(2,1)S(1)} %get-tuple-element.27), channel_id=1, source_target_pairs={{0,64},{32,96},{64,0},{96,32},{1,65},{33,97},{65,1},{97,33},{2,66}... | collective-permute-start | bytes 147464 | tf_op jit(solution)/shard_map/ppermute | solution.py:486
  76.5 5.3 %collective-permute-start.24 = (bf16[64,384]{1,0:T(8,128)(2,1)S(1)}, bf16[64,384]{1,0:T(8,128)(2,1)S(1)}, u32[]{:S(2)}, u32[]{:S(2)}) collective-permute-start(bf16[64,384]{1,0:T(8,128)(2,1)S(1)} %get-tuple-element.28), channel_id=1, source_target_pairs={{0,96},{32,64},{64,32},{96,0},{1,97},{33,65},{65,33},{97,1},{2,98}... | collective-permute-start | bytes 147464 | tf_op jit(solution)/shard_map/ppermute | solution.py:486
